TPU v7x, 32 devices: a whole 2x2x4 slice. The times are simulated.
32 devices in a mesh: dp: 8 (over z, y), seq: 4 (over x, core).
Axes of the slice: x: 2, y: 2, z: 4, core: 2. Of those that a mesh axis runs over, the one named last changes fastest.
Arguments:
- inputs: bfloat16 [48, 1024, 256], P('dp', 'seq')
- cotangent: bfloat16 [48, 1024, 256], P('dp', 'seq')
- owner_list: int32 [7], replicated, may hold values from 0 to 7, as said below
- master_rows: float32 [8, 524288], P('dp'), as said below
- moment1_rows: float32 [8, 524288], P('dp'), as said below
- moment2_rows: float32 [8, 524288], P('dp'), as said below
Outputs:
- final_state: float32 [48, 1024, 256], P('dp', 'seq')
- input_grad: float32 [48, 1024, 256], P('dp', 'seq')
- state_stats: float32 [2, 48], replicated
- new_moment1: float32 [8, 524288], P('dp')
- new_moment2: float32 [8, 524288], P('dp')
- new_master: float32 [8, 524288], P('dp')
Inputs may be any that keep to these rules, and one draw needn't show every extreme that they name: Tensor t goes to dp index owner_list[t]. W_up and W_down share one owner that holds no other tensor, so the busiest owner holds 524288 entries; the other five tensors are dealt among the other indices, several may share one. `master_rows`: entries of a row beyond the tensors its owner holds are not read. `moment1_rows`: entries of a row beyond the tensors its owner holds are not read. `moment2_rows`: Positive. Entries beyond the tensors an owner holds are not read.
All inputs are finite; a program needn't handle non-finite values.
Results may differ from a plain program's by a relative error of at most 0.02.
The roundings to bfloat16 on the way count: a program that leaves them out, or rounds other values in their place, can miss the bound.
Values may be sent and summed in bfloat16 or wider, within the bound.
A program may use at most 192 MiB of HBM per device.

v0:
```python
from functools import partial

import jax
import jax.numpy as jnp
from jax import lax
from jax.sharding import PartitionSpec as P

D = 256
HEADS = 4
HD = 64
FF = 1024
STEP = 3
SMALL = 9


norm_eps = 1e-05
stat_eps = 1e-06
adam_eps = 1e-08
masked_score = -1e30


def tensor_shapes():
    return [(D, D), (D, D), (D, D), (D, D), (D, FF), (FF, D), (SMALL, D)]


def owner_starts(owner_list):
    shapes = tensor_shapes()
    starts = []
    for tensor_id in range(7):
        offset = jnp.zeros((), jnp.int32)
        for earlier in range(tensor_id):
            shared = (owner_list[earlier] == owner_list[tensor_id]).astype(jnp.int32)
            offset = offset + shared * (shapes[earlier][0] * shapes[earlier][1])
        starts.append(offset)
    return starts


def layer_norm(values, norm_gain, norm_shift):
    average = jnp.mean(values, axis=-1, keepdims=True)
    centered = values - average
    spread = jnp.mean(centered * centered, axis=-1, keepdims=True)
    return centered * lax.rsqrt(spread + norm_eps) * norm_gain + norm_shift


def masked_scores(packed):
    length = packed.shape[0]
    queries = packed[:, :, :HD]
    keys_part = packed[:, :, HD : 2 * HD]
    scores = jnp.einsum(
        "qhd,khd->hqk", queries, keys_part, preferred_element_type=jnp.float32
    ) * HD ** (-0.5)
    causal = lax.broadcasted_iota(jnp.int32, (length, length), 0) >= lax.broadcasted_iota(
        jnp.int32, (length, length), 1
    )
    return jnp.where(causal[None], scores, masked_score)


def attend_single(packed):
    scores = masked_scores(packed)
    highest_score = jnp.max(scores, axis=-1, keepdims=True)
    raw_weights = jnp.exp(scores - highest_score)
    totals = jnp.sum(raw_weights, axis=-1, keepdims=True)
    attention_probs = raw_weights / totals
    values_part = packed[:, :, 2 * HD :]
    attention_output = jnp.einsum(
        "hqk,khd->qhd",
        attention_probs.astype(jnp.bfloat16),
        values_part,
        preferred_element_type=jnp.float32,
    )
    return (attention_output.astype(jnp.bfloat16), (highest_score + jnp.log(totals))[..., 0])


def attend_items(packed_items):
    attention_output, log_total = lax.map(attend_single, packed_items)
    return (attention_output, log_total, packed_items)


def attend_single_back(parts):
    packed, log_total, grad_attended = parts
    queries = packed[:, :, :HD]
    keys_part = packed[:, :, HD : 2 * HD]
    values_part = packed[:, :, 2 * HD :]
    scores = masked_scores(packed)
    attention_probs = jnp.exp(scores - log_total[..., None])
    grad_probs = jnp.einsum(
        "qhd,khd->hqk", grad_attended, values_part, preferred_element_type=jnp.float32
    )
    inner_sum = jnp.sum(attention_probs * grad_probs, axis=-1, keepdims=True)
    grad_scores = (attention_probs * (grad_probs - inner_sum)).astype(jnp.bfloat16)
    grad_queries = jnp.einsum(
        "hqk,khd->qhd", grad_scores, keys_part, preferred_element_type=jnp.float32
    ) * HD ** (-0.5)
    grad_keys = jnp.einsum(
        "hqk,qhd->khd", grad_scores, queries, preferred_element_type=jnp.float32
    ) * HD ** (-0.5)
    grad_values = jnp.einsum(
        "hqk,qhd->khd",
        attention_probs.astype(jnp.bfloat16),
        grad_attended,
        preferred_element_type=jnp.float32,
    )
    return jnp.concatenate([grad_queries, grad_keys, grad_values], axis=-1).astype(jnp.bfloat16)


def block_forward(loop_state, combined_weight, output_weight, up_weight, down_weight, small_piece):
    seq_count, quarter, features = loop_state.shape
    normalized_input = layer_norm(loop_state, small_piece[0], small_piece[1]).astype(jnp.bfloat16)
    projected = jnp.einsum(
        "fur,rk->fuk", normalized_input, combined_weight, preferred_element_type=jnp.float32
    ).astype(jnp.bfloat16)
    per_head = projected.reshape(seq_count, quarter, HEADS, 3 * HD)
    head_out, log_total, packed = attend_items(
        lax.all_to_all(per_head, "seq", split_axis=2, concat_axis=1, tiled=True)
    )
    attention_output = lax.all_to_all(
        head_out, "seq", split_axis=1, concat_axis=2, tiled=True
    ).reshape(seq_count, quarter, features)
    middle_state = loop_state + jnp.einsum(
        "fur,rk->fuk", attention_output, output_weight, preferred_element_type=jnp.float32
    )
    normalized_middle = layer_norm(middle_state, small_piece[2], small_piece[3]).astype(
        jnp.bfloat16
    )
    before = jnp.einsum(
        "sgm,mk->sgk", normalized_middle, up_weight, preferred_element_type=jnp.float32
    ) + small_piece[5:].reshape(FF)
    hidden_units = jax.nn.gelu(before, approximate=False).astype(jnp.bfloat16)
    result = middle_state + (
        jnp.einsum("czm,mg->czg", hidden_units, down_weight, preferred_element_type=jnp.float32)
        + small_piece[4]
    )
    saved = (
        loop_state,
        normalized_input,
        packed,
        log_total,
        attention_output,
        middle_state,
        normalized_middle,
        before,
        hidden_units,
    )
    return (result, saved)


def block_backward(
    grad_result, saved, combined_weight, output_weight, up_weight, down_weight, small_piece
):
    (
        loop_state,
        normalized_input,
        packed,
        log_total,
        attention_output,
        middle_state,
        normalized_middle,
        before,
        hidden_units,
    ) = saved
    seq_count, quarter, features = loop_state.shape
    branch_gradient = grad_result.astype(jnp.bfloat16)
    down_gradient = jnp.einsum(
        "yeo,yen->on", hidden_units, branch_gradient, preferred_element_type=jnp.float32
    )
    grad_bias_down = jnp.sum(branch_gradient.astype(jnp.float32), axis=(0, 1))
    hidden_gradient = jnp.einsum(
        "vel,kl->vek", branch_gradient, down_weight, preferred_element_type=jnp.float32
    )
    gelu_pull = jax.vjp(partial(jax.nn.gelu, approximate=False), before)[1]
    gradient_prior = gelu_pull(hidden_gradient)[0].astype(jnp.bfloat16)
    up_gradient = jnp.einsum(
        "erv,erh->vh", normalized_middle, gradient_prior, preferred_element_type=jnp.float32
    )
    grad_bias_up = jnp.sum(gradient_prior.astype(jnp.float32), axis=(0, 1))
    grad_normed_mid = jnp.einsum(
        "tam,em->tae", gradient_prior, up_weight, preferred_element_type=jnp.float32
    )
    second_pull = jax.vjp(layer_norm, middle_state, small_piece[2], small_piece[3])[1]
    grad_mid_part, grad_gain_two, grad_shift_two = second_pull(grad_normed_mid)
    grad_middle = grad_result + grad_mid_part
    attention_gradient = grad_middle.astype(jnp.bfloat16)
    grad_out_weight = jnp.einsum(
        "tck,tcp->kp", attention_output, attention_gradient, preferred_element_type=jnp.float32
    )
    grad_attended = jnp.einsum(
        "tkh,nh->tkn", attention_gradient, output_weight, preferred_element_type=jnp.float32
    ).astype(jnp.bfloat16)
    grad_heads = lax.all_to_all(
        grad_attended.reshape(seq_count, quarter, HEADS, HD),
        "seq",
        split_axis=2,
        concat_axis=1,
        tiled=True,
    )
    grad_packed = lax.map(attend_single_back, (packed, log_total, grad_heads))
    projected_gradient = lax.all_to_all(
        grad_packed, "seq", split_axis=1, concat_axis=2, tiled=True
    ).reshape(seq_count, quarter, 3 * features)
    grad_joined = jnp.einsum(
        "tck,tcp->kp", normalized_input, projected_gradient, preferred_element_type=jnp.float32
    )
    grad_normed = jnp.einsum(
        "tkh,nh->tkn", projected_gradient, combined_weight, preferred_element_type=jnp.float32
    )
    first_pull = jax.vjp(layer_norm, loop_state, small_piece[0], small_piece[1])[1]
    grad_state_part, grad_gain_one, grad_shift_one = first_pull(grad_normed)
    grad_state = grad_middle + grad_state_part
    grad_small = jnp.concatenate(
        [
            jnp.stack(
                [grad_gain_one, grad_shift_one, grad_gain_two, grad_shift_two, grad_bias_down]
            ),
            grad_bias_up.reshape(FF // D, D),
        ],
        axis=0,
    )
    return (grad_state, (grad_joined, grad_out_weight, up_gradient, down_gradient, grad_small))


def gather_stat(square_sums):
    return lax.all_gather(square_sums, ("dp", "seq"), axis=1, tiled=True)


def finish_stats(gathered, entries_total):
    loop_count = gathered.shape[0]
    folded = gathered.reshape(loop_count, lax.axis_size("dp"), lax.axis_size("seq"), -1)
    folded = jnp.sum(folded, axis=2).reshape(loop_count, -1)
    return jnp.sqrt(folded / entries_total + stat_eps)


def split_joined(grad_joined):
    arranged = grad_joined.reshape(D, HEADS, 3, HD)
    return [arranged[:, :, slot_id, :].reshape(D, D) for slot_id in range(3)]


def per_device(inputs, cotangent, owner_list, master_rows, moment1_rows, moment2_rows):
    shapes = tensor_shapes()
    starts = owner_starts(owner_list)
    device_row = lax.axis_index("dp")
    zero_row = jnp.zeros((), jnp.int32)
    owned_parts = []
    for tensor_id in range(7):
        entries = shapes[tensor_id][0] * shapes[tensor_id][1]
        sliced = lax.dynamic_slice(
            master_rows, (zero_row, starts[tensor_id]), (1, entries)
        ).reshape(shapes[tensor_id])
        is_owner = owner_list[tensor_id] == device_row
        owned_parts.append(jnp.where(is_owner, sliced, 0.0))
    masters = lax.psum(
        (
            owned_parts[0],
            owned_parts[1],
            owned_parts[2],
            owned_parts[3],
            owned_parts[4],
            owned_parts[5],
            owned_parts[6],
        ),
        "dp",
    )
    small_piece = masters[6]
    matrices = [matrix.astype(jnp.bfloat16) for matrix in masters[:6]]
    query_low, key_low, value_low, out_low, up_low, down_low = matrices
    combined_weight = jnp.stack(
        [
            query_low.reshape(D, HEADS, HD),
            key_low.reshape(D, HEADS, HD),
            value_low.reshape(D, HEADS, HD),
        ],
        axis=2,
    ).reshape(D, 3 * D)
    start_state = inputs.astype(jnp.float32)
    seq_count, quarter, features = start_state.shape
    entries_total = quarter * lax.axis_size("seq") * features
    first_out, first_saved = block_forward(
        start_state, combined_weight, out_low, up_low, down_low, small_piece
    )
    first_squares = jnp.sum(first_out * first_out, axis=(1, 2))
    first_gathered = gather_stat(first_squares[None])
    second_out, second_saved = block_forward(
        first_out + start_state, combined_weight, out_low, up_low, down_low, small_piece
    )
    second_squares = jnp.sum(second_out * second_out, axis=(1, 2))
    second_gathered = gather_stat(second_squares[None])
    gathered = jnp.concatenate([first_gathered, second_gathered], axis=0)
    state_stats = finish_stats(gathered, entries_total)
    grad_second_in, grads_two = block_backward(
        cotangent.astype(jnp.float32),
        second_saved,
        combined_weight,
        out_low,
        up_low,
        down_low,
        small_piece,
    )
    grad_first_in, grads_one = block_backward(
        grad_second_in, first_saved, combined_weight, out_low, up_low, down_low, small_piece
    )
    local_sums = [part_two + part_one for part_two, part_one in zip(grads_two, grads_one)]
    summed = lax.psum(
        (local_sums[0], local_sums[1], local_sums[2], local_sums[3], local_sums[4]), ("dp", "seq")
    )
    input_grad = grad_second_in + grad_first_in
    gradients = split_joined(summed[0]) + [summed[1], summed[2], summed[3], summed[4]]
    learning_rates = [D ** (-0.5)] * 5 + [FF ** (-0.5), 0.5]
    decays_list = [0.1] * 6 + [0.0]
    correction = 1.0 - 0.5**STEP
    new_moment1 = jnp.zeros_like(moment1_rows)
    new_moment2 = jnp.zeros_like(moment2_rows)
    new_master = jnp.zeros_like(master_rows)
    for tensor_id in range(7):
        entries = shapes[tensor_id][0] * shapes[tensor_id][1]
        corner = (zero_row, starts[tensor_id])
        is_owner = owner_list[tensor_id] == device_row
        gradient = gradients[tensor_id].reshape(1, entries)
        old_first = lax.dynamic_slice(moment1_rows, corner, (1, entries))
        old_second = lax.dynamic_slice(moment2_rows, corner, (1, entries))
        old_weight = lax.dynamic_slice(master_rows, corner, (1, entries))
        first_new = 0.5 * old_first + 0.5 * gradient
        second_new = 0.5 * old_second + 0.5 * gradient * gradient
        update = (
            first_new / correction / (jnp.sqrt(second_new / correction) + adam_eps)
            + decays_list[tensor_id] * old_weight
        )
        weight_new = old_weight - learning_rates[tensor_id] * update
        new_moment1 = lax.dynamic_update_slice(
            new_moment1,
            jnp.where(is_owner, first_new, lax.dynamic_slice(new_moment1, corner, (1, entries))),
            corner,
        )
        new_moment2 = lax.dynamic_update_slice(
            new_moment2,
            jnp.where(is_owner, second_new, lax.dynamic_slice(new_moment2, corner, (1, entries))),
            corner,
        )
        new_master = lax.dynamic_update_slice(
            new_master,
            jnp.where(is_owner, weight_new, lax.dynamic_slice(new_master, corner, (1, entries))),
            corner,
        )
    return (second_out, input_grad, state_stats, new_moment1, new_moment2, new_master)


def solution(mesh):
    placed = (
        P("dp", "seq", None),
        P("dp", "seq", None),
        P(),
        P("dp", None),
        P("dp", None),
        P("dp", None),
    )
    return jax.shard_map(
        per_device,
        mesh=mesh,
        in_specs=placed,
        out_specs=(
            P("dp", "seq", None),
            P("dp", "seq", None),
            P(),
            P("dp", None),
            P("dp", None),
            P("dp", None),
        ),
        check_vma=False,
    )
```

profile of v0, /device:TPU:0, one launch (start us, length us, event | category | flops | bytes accessed | tf_op | source)
XLA Modules:
  0.0 949.5 jit_solution(13561079497772902134)
XLA Ops:
  40.8 13.1 %fusion.104 = (f32[262144]{0:T(1024)S(1)}, f32[262144]{0:T(1024)}) fusion(pred[]{:T(512)S(6)} %eq.113, f32[1,524288]{1,0:T(1,128)} %param.17, s32[]{:T(128)S(6)} %select_n.271, s32[]{:T(128)S(6)} %select_n.267, pred[]{:T(512)S(6)} %eq.108), kind=kLoop, calls=%fused_computation.227 | loop fusion | flops 524288 | bytes 4194314 | tf_op jit(solution)/shard_map/jit(_where)/select_n | solution.py:249
  59.3 3.5 fusion.134
  69.9 132.7 %all-reduce.12 = (bf16[256,256]{1,0:T(8,128)(2,1)S(1)}, bf16[256,256]{1,0:T(8,128)(2,1)S(1)}, bf16[256,256]{1,0:T(8,128)(2,1)S(1)}, f32[9,256]{1,0:T(8,128)S(1)}...) all-reduce(f32[256,256]{1,0:T(8,128)} %select_n.261, ...), channel_id=1, replica_groups=mesh['dp'=8,'seq'=4] {'dp'}, use_global_device_ids=true, to_apply=%region_5.6 | all-reduce | flops 788736 | bytes 4737024 | tf_op jit(solution)/shard_map/psum | solution.py:250
  206.1 4.3 copy.262
  213.7 4.5 all-to-all-start
  218.2 28.5 %all-to-all-done = bf16[6,256,4,192]{1,3,0,2:T(8,128)(2,1)} async-done(((bf16[6,256,4,192]{1,3,0,2:T(8,128)(2,1)}), bf16[6,256,4,192]{1,3,0,2:T(8,128)(2,1)}, u32[]{:S(2)}, u32[]{:S(2)}) %all-to-all-start) | async-done | bytes 2359328 | tf_op jit(solution)/shard_map/all_to_all | solution.py:114
  246.7 3.4 copy.374
  250.2 18.3 %while.44 = (s32[]{:T(128)}, bf16[6,1024,1,64]{1,3,2,0:T(8,128)(2,1)S(1)}, f32[6,1,1024]{2,1,0:T(1,128)S(1)}, bf16[6,1024,1,192]{1,3,2,0:T(8,128)(2,1)}, s32[]{:T(128)}) while((s32[]{:T(128)}, bf16[6,1024,1,64]{1,3,2,0:T(8,128)(2,1)S(1)}, f32[6,1,1024]{2,1,0:T(1,128)S(1)}, bf16[6,1024,1,192]{1,3,2,0:T(8,128)(2,1)}, s32[]{:T(128)}) %tuple.165), condition=%wide.region_9.10_spmd, body=%wide.region_6.9_spmd.sunk | while | flops 284228608 | bytes 13934665 | solution.py:75
  271.0 4.2 reshape.839
  275.2 3.9 all-to-all-start.1
  279.2 11.5 %all-to-all-done.1 = bf16[4,2,49152]{2,1,0:T(2,128)(2,1)S(1)} async-done(((bf16[4,2,49152]{2,1,0:T(2,128)(2,1)}), bf16[4,2,49152]{2,1,0:T(2,128)(2,1)S(1)}, u32[]{:S(2)}, u32[]{:S(2)}) %all-to-all-start.1) | async-done | bytes 786464 | tf_op jit(solution)/shard_map/all_to_all | solution.py:116
  300.9 15.2 %multiply_convert_fusion.3 = (bf16[6,256,1024]{2,1,0:T(8,128)(2,1)S(1)}, f32[6,256,1024]{2,1,0:T(8,128)}) fusion(f32[6,256,1024]{2,1,0:T(8,128)S(1)} %get-tuple-element.342, f32[1024]{0:T(1024)S(1)} %bitcast.501, u8[256,1024]{1,0:T(8,128)(4,1)S(1)} %get-tuple-element.217, u8[256,1024]{1,0:T(8,128)(4,1)S(1)} %get-tuple-element.216), kind=kLoop, calls=%fused_computation.130 | loop fusion | flops 111673344 | bytes 16257024 | tf_op jit(solution)/shard_map/convert_element_type | solution.py:128
  320.7 4.3 copy.275
  325.1 3.3 copy.276
  328.4 4.5 all-to-all-start.2
  332.9 28.5 %all-to-all-done.2 = bf16[6,256,4,192]{1,3,0,2:T(8,128)(2,1)} async-done(((bf16[6,256,4,192]{1,3,0,2:T(8,128)(2,1)}), bf16[6,256,4,192]{1,3,0,2:T(8,128)(2,1)}, u32[]{:S(2)}, u32[]{:S(2)}) %all-to-all-start.2) | async-done | bytes 2359328 | tf_op jit(solution)/shard_map/all_to_all | solution.py:114
  361.4 3.4 copy.375
  364.9 18.3 %while.45 = (s32[]{:T(128)}, bf16[6,1024,1,64]{1,3,2,0:T(8,128)(2,1)S(1)}, f32[6,1,1024]{2,1,0:T(1,128)S(1)}, bf16[6,1024,1,192]{1,3,2,0:T(8,128)(2,1)}, s32[]{:T(128)}) while((s32[]{:T(128)}, bf16[6,1024,1,64]{1,3,2,0:T(8,128)(2,1)S(1)}, f32[6,1,1024]{2,1,0:T(1,128)S(1)}, bf16[6,1024,1,192]{1,3,2,0:T(8,128)(2,1)}, s32[]{:T(128)}) %tuple.167), condition=%wide.region_20.21_spmd, body=%wide.region_17.20_spmd.sunk | while | flops 284228608 | bytes 13934665 | solution.py:75
  385.8 4.3 reshape.841
  390.1 3.7 all-to-all-start.3
  394.9 10.4 %all-to-all-done.3 = bf16[4,2,49152]{2,1,0:T(2,128)(2,1)S(1)} async-done(((bf16[4,2,49152]{2,1,0:T(2,128)(2,1)}), bf16[4,2,49152]{2,1,0:T(2,128)(2,1)S(1)}, u32[]{:S(2)}, u32[]{:S(2)}) %all-to-all-start.3) | async-done | bytes 786464 | tf_op jit(solution)/shard_map/all_to_all | solution.py:116
  415.5 15.1 %multiply_convert_fusion.2 = (bf16[6,256,1024]{2,1,0:T(8,128)(2,1)}, f32[6,256,1024]{2,1,0:T(8,128)S(1)}) fusion(f32[6,256,1024]{2,1,0:T(8,128)S(1)} %get-tuple-element.345, f32[1024]{0:T(1024)S(1)} %bitcast.503, u8[256,1024]{1,0:T(8,128)(4,1)S(1)} %get-tuple-element.215, u8[256,1024]{1,0:T(8,128)(4,1)S(1)} %get-tuple-element.214), kind=kLoop, calls=%fused_computation.117 | loop fusion | flops 111673344 | bytes 16257024 | tf_op jit(solution)/shard_map/convert_element_type | solution.py:128
  430.6 3.4 convert_reduce_fusion.1
  444.4 4.4 all-to-all-start.4
  448.9 11.7 %all-to-all-done.4 = bf16[6,256,4,64]{1,3,0,2:T(8,128)(2,1)} async-done(((bf16[6,256,4,64]{1,3,0,2:T(8,128)(2,1)}), bf16[6,256,4,64]{1,3,0,2:T(8,128)(2,1)}, u32[]{:S(2)}, u32[]{:S(2)}) %all-to-all-start.4) | async-done | bytes 786464 | tf_op jit(solution)/shard_map/all_to_all | solution.py:189
  464.3 52.6 %while.46 = (s32[]{:T(128)}, bf16[6,1024,1,192]{1,3,2,0:T(8,128)(2,1)}, bf16[6,1024,1,192]{1,3,2,0:T(8,128)(2,1)}, f32[6,1,1024]{2,1,0:T(1,128)S(1)}, bf16[6,1024,1,64]{1,3,2,0:T(8,128)(2,1)}, /*index=5*/s32[]{:T(128)}) while((s32[]{:T(128)}, bf16[6,1024,1,192]{1,3,2,0:T(8,128)(2,1)}, bf16[6,1024,1,192]{1,3,2,0:T(8,128)(2,1)}, ...), condition=%wide.region_27.28_spmd, body=%wide.region_25.27_spmd.sunk | while | flops 683080704 | bytes 34362956 | solution.py:196
  516.9 6.6 copy.295
  523.5 53.8 %all_to_all.132 = bf16[6,1024,1,192]{3,0,2,1:T(8,128)(2,1)} all-to-all(bf16[6,1024,1,192]{3,0,2,1:T(8,128)(2,1)} %copy.295), channel_id=1, replica_groups=mesh['dp'=8,'seq'=4] {'seq'}, dimensions={1} | all-to-all | bytes 4718592 | tf_op jit(solution)/shard_map/all_to_all | solution.py:197
  577.3 5.6 copy.368
  594.6 7.0 convert_reduce_fusion
  613.3 4.6 all-to-all-start.6
  618.1 4.2 multiply_reduce_fusion.5
  625.5 4.0 all-to-all-done.6
  633.3 56.6 %while.47 = (s32[]{:T(128)}, bf16[6,1024,1,192]{1,3,2,0:T(8,128)(2,1)}, bf16[6,1024,1,192]{1,3,2,0:T(8,128)(2,1)}, f32[6,1,1024]{2,1,0:T(1,128)}, bf16[6,1024,1,64]{1,3,2,0:T(8,128)(2,1)}, /*index=5*/s32[]{:T(128)}) while((s32[]{:T(128)}, bf16[6,1024,1,192]{1,3,2,0:T(8,128)(2,1)}, bf16[6,1024,1,192]{1,3,2,0:T(8,128)(2,1)}, ...), condition=%wide.region_34.35_spmd, body=%wide.region_32.34_spmd.sunk | while | flops 683080704 | bytes 34362956 | solution.py:196
  689.9 6.5 copy.310
  696.4 4.9 all-to-all-start.7
  701.6 3.5 convolution_bitcast_fusion
  715.5 34.0 %all-to-all-done.7 = bf16[6,1024,1,192]{3,0,2,1:T(8,128)(2,1)} async-done(((bf16[6,1024,1,192]{3,0,2,1:T(8,128)(2,1)}), bf16[6,1024,1,192]{3,0,2,1:T(8,128)(2,1)}, u32[]{:S(2)}, u32[]{:S(2)}) %all-to-all-start.7) | async-done | bytes 2359328 | tf_op jit(solution)/shard_map/all_to_all | solution.py:197
  749.5 5.6 copy.372
  765.9 39.1 %all-reduce.5 = (f32[192]{0:T(256)S(1)}, f32[192]{0:T(256)S(1)}, f32[1,2304]{1,0:T(1,128)S(1)}) all-reduce(f32[192]{0:T(256)S(1)} %dynamic-update-slice.1, f32[192]{0:T(256)S(1)} %dynamic-update-slice, f32[1,2304]{1,0:T(1,128)S(1)} %bitcast.506), channel_id=3, replica_groups=mesh['dp'=8,'seq'=4] {'dp','seq'}, use_global_device_ids=true, to_apply=%add.4 | all-reduce | flops 2688 | bytes 21504
  805.9 3.7 add_add_fusion.4
  812.7 88.7 %all-reduce.11.cloned.1.call-done = (f32[256,4,3,64]{0,3,2,1:T(8,128)}, f32[1,65536]{1,0:T(1,128)}, f32[1,262144]{1,0:T(1,128)}, f32[1,262144]{1,0:T(1,128)}) async-done(((f32[256,4,3,64]{0,3,2,1:T(8,128)}, f32[1,65536]{1,0:T(1,128)}, f32[1,262144]{1,0:T(1,128)}, f32[1,262144]{1,0:T(1,128)}), (f32[256,4,3,64]{0,3,2,1:T(8,128)}, f32[1,65536]{1,0:T(1,128)}, f32[1,262144]{1,0:T(1,128)}, ...) | async-done | bytes 3145744 | tf_op jit(solution)/shard_map/psum | solution.py:301
  903.3 3.5 broadcast_select_fusion.20
  908.5 3.7 dynamic_update_slice.91
  912.2 3.7 dynamic_update_slice.84
  915.8 3.9 dynamic_update_slice.98
  925.2 7.1 fusion.103
  932.3 7.1 fusion.107
  (469 shorter events, 278.0 us)
Async XLA Ops:
  55.2 4.1 copy-start.6
  69.9 133.1 %copy-start.42 = (bf16[6,256,256]{2,1,0:T(8,128)(2,1)S(1)}, bf16[6,256,256]{2,1,0:T(8,128)(2,1)}, u32[]{:S(2)}) copy-start(bf16[6,256,256]{2,1,0:T(8,128)(2,1)} %param.14) | copy-start | bytes 2359300
  203.0 115.3 %copy-start.35 = (bf16[256,4,3,64]{0,3,2,1:T(8,128)(2,1)}, bf16[256,4,3,64]{0,3,2,1:T(8,128)(2,1)S(1)}, u32[]{:S(2)}) copy-start(bf16[256,4,3,64]{0,3,2,1:T(8,128)(2,1)S(1)} %copy.259) | copy-start | bytes 1179652
  203.0 113.1 %copy-start.63 = (f32[1,256]{1,0:T(1,128)}, f32[1,256]{1,0:T(1,128)S(1)}, u32[]{:S(2)}) copy-start(f32[1,256]{1,0:T(1,128)S(1)} %get-tuple-element.328) | copy-start | bytes 3076
  203.0 115.3 %copy-start.65 = (f32[1,256]{1,0:T(1,128)}, f32[1,256]{1,0:T(1,128)S(1)}, u32[]{:S(2)}) copy-start(f32[1,256]{1,0:T(1,128)S(1)} %get-tuple-element.331) | copy-start | bytes 3076
  203.1 209.1 %copy-start.67 = (f32[1,256]{1,0:T(1,128)}, f32[1,256]{1,0:T(1,128)S(1)}, u32[]{:S(2)}) copy-start(f32[1,256]{1,0:T(1,128)S(1)} %get-tuple-element.329) | copy-start | bytes 3076
  203.3 112.8 %copy-start = (bf16[6,256,256]{1,2,0:T(8,128)(2,1)}, bf16[6,256,256]{1,2,0:T(8,128)(2,1)S(1)}, u32[]{:S(2)}) copy-start(bf16[6,256,256]{1,2,0:T(8,128)(2,1)S(1)} %copy.255) | copy-start | bytes 2359300
  203.7 6.7 copy-start.59
  203.7 6.6 copy-start.55
  213.7 33.0 %all-to-all-start = ((bf16[6,256,4,192]{1,3,0,2:T(8,128)(2,1)}), bf16[6,256,4,192]{1,3,0,2:T(8,128)(2,1)}, u32[]{:S(2)}, u32[]{:S(2)}) async-start(bf16[6,256,4,192]{1,3,0,2:T(8,128)(2,1)} %copy.263), calls=%async_computation | async-start | bytes 4718592 | tf_op jit(solution)/shard_map/all_to_all | solution.py:114
  268.5 6.7 copy-start.54
  275.2 15.5 %all-to-all-start.1 = ((bf16[4,2,49152]{2,1,0:T(2,128)(2,1)}), bf16[4,2,49152]{2,1,0:T(2,128)(2,1)S(1)}, u32[]{:S(2)}, u32[]{:S(2)}) async-start(bf16[4,2,49152]{2,1,0:T(2,128)(2,1)} %reshape.839), calls=%async_computation.1 | async-start | bytes 1572864 | tf_op jit(solution)/shard_map/all_to_all | solution.py:116
  297.3 18.9 %copy-start.3 = (f32[6,256,256]{1,2,0:T(8,128)}, f32[6,256,256]{1,2,0:T(8,128)S(1)}, u32[]{:S(2)}) copy-start(f32[6,256,256]{1,2,0:T(8,128)S(1)} %get-tuple-element.341) | copy-start | bytes 4718596
  297.3 3.5 copy-start.52
  297.5 3.4 copy-start.61
  297.5 3.3 copy-start.57
  300.9 15.3 %copy-start.29 = (f32[6,256,1024]{2,1,0:T(8,128)}, f32[6,256,1024]{2,1,0:T(8,128)S(1)}, u32[]{:S(2)}) copy-start(f32[6,256,1024]{2,1,0:T(8,128)S(1)} %get-tuple-element.342) | copy-start | bytes 18874372
  300.9 15.3 %copy-start.46 = (bf16[1024,256]{0,1:T(8,128)(2,1)S(1)}, bf16[1024,256]{0,1:T(8,128)(2,1)}, u32[]{:S(2)}) copy-start(bf16[1024,256]{0,1:T(8,128)(2,1)} %get-tuple-element.281) | copy-start | bytes 1572868
  328.4 33.0 %all-to-all-start.2 = ((bf16[6,256,4,192]{1,3,0,2:T(8,128)(2,1)}), bf16[6,256,4,192]{1,3,0,2:T(8,128)(2,1)}, u32[]{:S(2)}, u32[]{:S(2)}) async-start(bf16[6,256,4,192]{1,3,0,2:T(8,128)(2,1)} %copy.276), calls=%async_computation.2 | async-start | bytes 4718592 | tf_op jit(solution)/shard_map/all_to_all | solution.py:114
  385.8 8.0 copy-start.43
  390.1 15.2 %all-to-all-start.3 = ((bf16[4,2,49152]{2,1,0:T(2,128)(2,1)}), bf16[4,2,49152]{2,1,0:T(2,128)(2,1)S(1)}, u32[]{:S(2)}, u32[]{:S(2)}) async-start(bf16[4,2,49152]{2,1,0:T(2,128)(2,1)} %reshape.841), calls=%async_computation.3 | async-start | bytes 1572864 | tf_op jit(solution)/shard_map/all_to_all | solution.py:116
  415.5 15.1 %copy-start.44 = (bf16[6,256,256]{2,1,0:T(8,128)(2,1)S(1)}, bf16[6,256,256]{2,1,0:T(8,128)(2,1)}, u32[]{:S(2)}) copy-start(bf16[6,256,256]{2,1,0:T(8,128)(2,1)} %param.15) | copy-start | bytes 2359300
  415.5 15.1 %copy-start.47 = (bf16[1024,256]{0,1:T(8,128)(2,1)S(1)}, bf16[1024,256]{0,1:T(8,128)(2,1)}, u32[]{:S(2)}) copy-start(bf16[1024,256]{0,1:T(8,128)(2,1)} %get-tuple-element.281) | copy-start | bytes 1572868
  444.4 16.1 %all-to-all-start.4 = ((bf16[6,256,4,64]{1,3,0,2:T(8,128)(2,1)}), bf16[6,256,4,64]{1,3,0,2:T(8,128)(2,1)}, u32[]{:S(2)}, u32[]{:S(2)}) async-start(bf16[6,256,4,64]{1,3,0,2:T(8,128)(2,1)} %copy.291), calls=%async_computation.4 | async-start | bytes 1572864 | tf_op jit(solution)/shard_map/all_to_all | solution.py:189
  594.5 7.0 copy-start.8
  594.6 7.0 copy-start.71
  603.8 3.1 copy-start.53
  603.8 3.1 copy-start.58
  611.4 6.5 copy-start.72
  611.4 6.7 copy-start.64
  613.3 16.3 %all-to-all-start.6 = ((bf16[6,256,4,64]{1,3,0,2:T(8,128)(2,1)}), bf16[6,256,4,64]{1,3,0,2:T(8,128)(2,1)}, u32[]{:S(2)}, u32[]{:S(2)}) async-start(bf16[6,256,4,64]{1,3,0,2:T(8,128)(2,1)} %copy.306), calls=%async_computation.6 | async-start | bytes 1572864 | tf_op jit(solution)/shard_map/all_to_all | solution.py:189
  696.4 53.1 %all-to-all-start.7 = ((bf16[6,1024,1,192]{3,0,2,1:T(8,128)(2,1)}), bf16[6,1024,1,192]{3,0,2,1:T(8,128)(2,1)}, u32[]{:S(2)}, u32[]{:S(2)}) async-start(bf16[6,1024,1,192]{3,0,2,1:T(8,128)(2,1)} %copy.310), calls=%async_computation.7 | async-start | bytes 8388608 | tf_op jit(solution)/shard_map/all_to_all | solution.py:197
  701.3 200.0 %all-reduce.11.cloned.1.call-start = ((), (), s32[]{:S(2)}) async-start(), calls=%async_computation.8 | async-start | bytes 6291456 | tf_op jit(solution)/shard_map/psum | solution.py:301
  701.5 3.6 copy-start.15
  701.5 3.6 copy-start.45
  705.1 3.1 copy-start.5
  705.1 3.1 copy-start.68
  705.1 3.1 copy-start.76
  710.1 3.2 copy-start.20
  710.1 3.2 copy-start.26
  812.6 90.6 %copy-start.7 = (f32[1,524288]{1,0:T(1,128)S(1)}, f32[1,524288]{1,0:T(1,128)}, u32[]{:S(2)}) copy-start(f32[1,524288]{1,0:T(1,128)} %param.17) | copy-start | bytes 6291460
  908.5 3.7 copy-start.39
  908.5 7.4 copy-start.38
  912.1 7.6 copy-start.30
  912.2 7.6 copy-start.31
  919.8 3.6 copy-start.49
  921.6 3.6 copy-start.41
  925.2 7.1 copy-start.40
  (37 other events, 65.3 us)
Sparse Core Ops, SparseCore 0:
  764.7 136.5 all-reduce.10
where the time goes:
time: 962 us; the launch traced here: 949 us
  blocking collectives  226 us (23%)
  waiting for transfers between devices  217 us (23%)
  local copies, waits for them, and re-layouts  179 us (19%)
  matrix products  133 us (14%)
  other arithmetic  115 us (12%)
  between operations  48 us (5%)
  starting transfers between devices  30.6 us (3%)
    psum x1, blocking collectives, per_device(): lax.psum((owned_parts[0], owned_parts[1], owned_parts[2], owned_parts[3],...  133 us
    psum x1, waiting for transfers between devices, per_device(): lax.psum((local_sums[0], local_sums[1], local_sums[2], local_sums[3], loc...  88.7 us
    all_to_all x2, waiting for transfers between devices, block_forward(): lax.all_to_all(per_head, 'seq', split_axis=2, concat_axis=1, tiled=True)  57.1 us
    all_to_all x1, blocking collectives, block_backward(): lax.all_to_all(grad_packed, 'seq', split_axis=1, concat_axis=2, tiled=True)  53.8 us
    unnamed x1, blocking collectives  39.1 us
    unnamed x172, local copies, waits for them, and re-layouts  36.9 us
    all_to_all x1, waiting for transfers between devices, block_backward(): lax.all_to_all(grad_packed, 'seq', split_axis=1, concat_axis=2, tiled=True)  34 us
    convert_element_type x2, other arithmetic, block_forward(): hidden_units = jax.nn.gelu(before, approximate=False).astype(jnp.bfloat16)  30.4 us
  transfers between devices with their start and end apart: 8, of which 8 were waited for; matrix products, arithmetic and copies ran while one was open for 3% of the time, Pallas kernels for 0%

commit v1 on v0

v1 whole, which is shorter than its diff:
```python
import math
from functools import partial

import jax
import jax.numpy as jnp
from jax import lax
from jax.experimental import pallas as pl
from jax.experimental.pallas import tpu as pltpu
from jax.sharding import PartitionSpec as P

D = 256
HEADS = 4
HD = 64
FF = 1024
STEP = 3
SMALL = 9
BLK = 256
OWN = 4
UNITS = 6
ALL = 8
F32 = jnp.float32
BF16 = jnp.bfloat16
MESH = pl.DeviceIdType.MESH

norm_eps = 1e-05
stat_eps = 1e-06
adam_eps = 1e-08
masked_score = -1e30


def dot(left, right):
    return lax.dot_general(left, right, (((1,), (0,)), ((), ())), preferred_element_type=F32)


def dot_nt(left, right):
    return lax.dot_general(left, right, (((1,), (1,)), ((), ())), preferred_element_type=F32)


def wide(column):
    return jnp.concatenate([column, column], axis=1)


def fold(values):
    return values[:, :128] + values[:, 128:]


def standardize(values):
    average = jnp.mean(values, axis=0, keepdims=True)
    centered = values - average
    spread = jnp.mean(centered * centered, axis=0, keepdims=True)
    inverse = lax.rsqrt(spread + norm_eps)
    return centered * inverse, inverse


def standardize_back(grad, unit_values, inverse):
    average = jnp.mean(grad, axis=0, keepdims=True)
    inner = jnp.mean(grad * unit_values, axis=0, keepdims=True)
    return (grad - average - unit_values * inner) * inverse


def param(small_ref, row):
    return wide(small_ref[row * D : (row + 1) * D, :])


def gelu_parts(e):
    cdf = 0.5 * lax.erf(e * math.sqrt(0.5)) + 0.5
    hid = e * cdf
    slope = cdf + e * (jnp.exp(-0.5 * e * e) * (1.0 / math.sqrt(2.0 * math.pi)))
    return hid, slope


def full(shape):
    return pl.BlockSpec(shape, lambda *args: (0,) * len(shape), pipeline_mode=pl.Buffered(1))


def params_of(ndims=1, mib=56):
    return pltpu.CompilerParams(
        dimension_semantics=("arbitrary",) * ndims, vmem_limit_bytes=mib << 20
    )


def cost(flops, nbytes, trans=0):
    return pl.CostEstimate(flops=int(flops), bytes_accessed=int(nbytes), transcendentals=int(trans))


def project(a, wt_ref, q_ref, kt_ref, vt_ref, k_ref, v_ref):
    q_ref[0] = (dot(wt_ref[0:D], a) * HD ** (-0.5)).astype(BF16)
    kt = dot(wt_ref[D : 2 * D], a).astype(BF16)
    kt_ref[0] = kt
    k_ref[0] = kt.T
    vt = dot(wt_ref[2 * D : 3 * D], a).astype(BF16)
    vt_ref[0] = vt
    v_ref[0] = vt.T


def first_body(x_ref, small_ref, wt_ref, xt_ref, a_ref, q_ref, kt_ref, vt_ref, k_ref, v_ref):
    xt = x_ref[0].T
    xt_ref[0] = xt
    unit_values, _ = standardize(xt.astype(F32))
    a = (unit_values * param(small_ref, 0) + param(small_ref, 1)).astype(BF16)
    a_ref[0] = a
    project(a, wt_ref, q_ref, kt_ref, vt_ref, k_ref, v_ref)


def second_body(a_ref, wt_ref, q_ref, kt_ref, vt_ref, k_ref, v_ref):
    project(a_ref[0], wt_ref, q_ref, kt_ref, vt_ref, k_ref, v_ref)


def tile_spec(blocks=None):
    if blocks is None:
        return pl.BlockSpec((1, BLK, BLK), lambda j, *t: (j, 0, 0))
    return blocks


def first_projection(x, small, wt):
    tile = pl.BlockSpec((1, BLK, BLK), lambda j: (j, 0, 0))
    out = jax.ShapeDtypeStruct((ALL, BLK, BLK), BF16)
    return pl.pallas_call(
        first_body,
        grid=(ALL,),
        in_specs=[tile, full(small.shape), full(wt.shape)],
        out_specs=[tile] * 7,
        out_shape=[out] * 7,
        compiler_params=params_of(),
        cost_estimate=cost(2 * 2048 * 256 * 768, 9 << 20),
        name="first_projection",
    )(x, small, wt)


def second_projection(a, wt):
    tile = pl.BlockSpec((1, BLK, BLK), lambda j: (j, 0, 0))
    out = jax.ShapeDtypeStruct((ALL, BLK, BLK), BF16)
    return pl.pallas_call(
        second_body,
        grid=(ALL,),
        in_specs=[tile, full(wt.shape)],
        out_specs=[tile] * 5,
        out_shape=[out] * 5,
        compiler_params=params_of(),
        cost_estimate=cost(2 * 2048 * 256 * 768, 6 << 20),
        name="second_projection",
    )(a, wt)


def head_rows(values, half):
    rows = lax.broadcasted_iota(jnp.int32, values.shape, 0)
    keep = (rows < HD) if half == 0 else (rows >= HD)
    return jnp.where(keep, values, jnp.zeros_like(values))


def causal_mask():
    keys = lax.broadcasted_iota(jnp.int32, (BLK, BLK), 0)
    queries = lax.broadcasted_iota(jnp.int32, (BLK, BLK), 1)
    return keys <= queries


def attend_body(table, q_ref, k_ref, vt_ref, o_ref, log_ref, score_ref):
    unit = pl.program_id(1)
    base = table[UNITS + unit]
    place = table[2 * UNITS + unit]

    def branch(last):
        for half in range(2):
            lo, hi = half * HD, (half + 1) * HD
            q = head_rows(q_ref[0], half)
            top = None
            for kb in range(last + 1):
                score = dot(k_ref[base + kb], q)
                if kb == last:
                    score = jnp.where(causal_mask(), score, masked_score)
                score_ref[half, kb] = score
                peak = jnp.max(score, axis=0, keepdims=True)
                top = peak if top is None else jnp.maximum(top, peak)
            total = jnp.zeros((1, BLK), F32)
            acc = jnp.zeros((HD, BLK), F32)
            for kb in range(last + 1):
                weight = jnp.exp(score_ref[half, kb] - top)
                total = total + jnp.sum(weight, axis=0, keepdims=True)
                acc = acc + dot(vt_ref[base + kb, lo:hi, :], weight.astype(BF16))
            o_ref[0, lo:hi, :] = (acc / total).astype(BF16)
            log_ref[0, 0, half : half + 1, :] = top + jnp.log(total)

    for last in range(OWN):
        pl.when(place == last)(partial(branch, last))


def attend(table, q, k, vt):
    spec = pltpu.PrefetchScalarGridSpec(
        num_scalar_prefetch=1,
        grid=(2, UNITS),
        in_specs=[
            pl.BlockSpec((1, 128, BLK), lambda h, u, t: (t[u], h, 0)),
            pl.BlockSpec((ALL, BLK, 128), lambda h, u, t: (0, 0, h)),
            pl.BlockSpec((ALL, 128, BLK), lambda h, u, t: (0, h, 0)),
        ],
        out_specs=[
            pl.BlockSpec((1, 128, BLK), lambda h, u, t: (u, h, 0)),
            pl.BlockSpec((1, 1, 8, BLK), lambda h, u, t: (u, h, 0, 0)),
        ],
        scratch_shapes=[pltpu.VMEM((2, OWN, BLK, BLK), F32)],
    )
    return pl.pallas_call(
        attend_body,
        grid_spec=spec,
        out_shape=[
            jax.ShapeDtypeStruct((UNITS, BLK, BLK), BF16),
            jax.ShapeDtypeStruct((UNITS, 2, 8, BLK), F32),
        ],
        compiler_params=params_of(2),
        cost_estimate=cost(4 * 4 * 15 * BLK * BLK * HD, 5 << 20, 4 * 15 * BLK * BLK),
        name="attend",
    )(table, q, k, vt)


def attend_back_body(
    table, q_ref, k_ref, kt_ref, v_ref, go_ref, o_ref, log_ref, dq_ref, dk_ref, dv_ref, dk_acc, dv_acc
):
    unit = pl.program_id(1)
    base = table[UNITS + unit]
    place = table[2 * UNITS + unit]

    @pl.when(unit == 0)
    def _():
        dk_acc[...] = jnp.zeros_like(dk_acc)
        dv_acc[...] = jnp.zeros_like(dv_acc)

    def branch(last):
        for half in range(2):
            lo, hi = half * HD, (half + 1) * HD
            q = head_rows(q_ref[0], half)
            go = head_rows(go_ref[0], half)
            q_head = q_ref[0, lo:hi, :]
            go_head = go_ref[0, lo:hi, :]
            log_total = log_ref[0, 0, half : half + 1, :]
            inner = jnp.sum(
                go_head.astype(F32) * o_ref[0, lo:hi, :].astype(F32), axis=0, keepdims=True
            )
            dq = jnp.zeros((HD, BLK), F32)
            for kb in range(last + 1):
                score = dot(k_ref[base + kb], q)
                if kb == last:
                    score = jnp.where(causal_mask(), score, masked_score)
                weight = jnp.exp(score - log_total)
                slope = dot(v_ref[base + kb], go)
                dscore = (weight * (slope - inner)).astype(BF16)
                dv_acc[base + kb, lo:hi, :] += dot_nt(go_head, weight.astype(BF16))
                dk_acc[base + kb, lo:hi, :] += dot_nt(q_head, dscore)
                dq = dq + dot(kt_ref[base + kb, lo:hi, :], dscore)
            dq_ref[0, lo:hi, :] = (dq * HD ** (-0.5)).astype(BF16)

    for last in range(OWN):
        pl.when(place == last)(partial(branch, last))

    @pl.when(unit == UNITS - 1)
    def _():
        dk_ref[...] = dk_acc[...].astype(BF16)
        dv_ref[...] = dv_acc[...].astype(BF16)


def attend_back(table, q, k, kt, v, go, o, log_total):
    spec = pltpu.PrefetchScalarGridSpec(
        num_scalar_prefetch=1,
        grid=(2, UNITS),
        in_specs=[
            pl.BlockSpec((1, 128, BLK), lambda h, u, t: (t[u], h, 0)),
            pl.BlockSpec((ALL, BLK, 128), lambda h, u, t: (0, 0, h)),
            pl.BlockSpec((ALL, 128, BLK), lambda h, u, t: (0, h, 0)),
            pl.BlockSpec((ALL, BLK, 128), lambda h, u, t: (0, 0, h)),
            pl.BlockSpec((1, 128, BLK), lambda h, u, t: (u, h, 0)),
            pl.BlockSpec((1, 128, BLK), lambda h, u, t: (u, h, 0)),
            pl.BlockSpec((1, 1, 8, BLK), lambda h, u, t: (u, h, 0, 0)),
        ],
        out_specs=[
            pl.BlockSpec((1, 128, BLK), lambda h, u, t: (u, h, 0)),
            pl.BlockSpec((ALL, 128, BLK), lambda h, u, t: (0, h, 0)),
            pl.BlockSpec((ALL, 128, BLK), lambda h, u, t: (0, h, 0)),
        ],
        scratch_shapes=[pltpu.VMEM((ALL, 128, BLK), F32)] * 2,
    )
    return pl.pallas_call(
        attend_back_body,
        grid_spec=spec,
        out_shape=[
            jax.ShapeDtypeStruct((UNITS, BLK, BLK), BF16),
            jax.ShapeDtypeStruct((ALL, BLK, BLK), BF16),
            jax.ShapeDtypeStruct((ALL, BLK, BLK), BF16),
        ],
        compiler_params=params_of(2),
        cost_estimate=cost(10 * 4 * 15 * BLK * BLK * HD, 8 << 20, 4 * 15 * BLK * BLK),
        name="attend_back",
    )(table, q, k, kt, v, go, o, log_total)


def middle(z, o_ref, wot_ref, small_ref):
    r = z + dot(wot_ref[...], o_ref[0])
    unit_values, inverse = standardize(r)
    m = (unit_values * param(small_ref, 2) + param(small_ref, 3)).astype(BF16)
    return r, unit_values, inverse, m


def feed_first_body(
    table, xt_ref, o_ref, small_ref, wot_ref, wut_ref, wdt_ref, r_ref, hid_ref, slope_ref, z_ref, a_ref, sq_ref
):
    x = xt_ref[0].astype(F32)
    r, _, _, m = middle(x, o_ref, wot_ref, small_ref)
    r_ref[0] = r
    out = r + param(small_ref, 4)
    for c in range(FF // BLK):
        rows = slice(c * BLK, (c + 1) * BLK)
        e = dot(wut_ref[rows, :], m) + param(small_ref, 5 + c)
        hid, slope = gelu_parts(e)
        hid = hid.astype(BF16)
        hid_ref[0, rows, :] = hid
        slope_ref[0, rows, :] = slope.astype(BF16)
        out = out + dot(wdt_ref[:, rows], hid)
    sq_ref[0] = jnp.broadcast_to(jnp.sum(out * out, axis=0, keepdims=True), (8, BLK))
    z = out + x
    z_ref[0] = z
    unit_values, _ = standardize(z)
    a_ref[0] = (unit_values * param(small_ref, 0) + param(small_ref, 1)).astype(BF16)


def feed_first(table, xt, o, small, wot, wut, wdt):
    spec = pltpu.PrefetchScalarGridSpec(
        num_scalar_prefetch=1,
        grid=(UNITS,),
        in_specs=[
            pl.BlockSpec((1, BLK, BLK), lambda u, t: (t[u], 0, 0)),
            pl.BlockSpec((1, BLK, BLK), lambda u, t: (u, 0, 0)),
            full(small.shape),
            full(wot.shape),
            full(wut.shape),
            full(wdt.shape),
        ],
        out_specs=[
            pl.BlockSpec((1, BLK, BLK), lambda u, t: (u, 0, 0)),
            pl.BlockSpec((1, FF, BLK), lambda u, t: (u, 0, 0)),
            pl.BlockSpec((1, FF, BLK), lambda u, t: (u, 0, 0)),
            pl.BlockSpec((1, BLK, BLK), lambda u, t: (u, 0, 0)),
            pl.BlockSpec((1, BLK, BLK), lambda u, t: (u, 0, 0)),
            pl.BlockSpec((1, 8, BLK), lambda u, t: (u, 0, 0)),
        ],
    )
    tile = (UNITS, BLK, BLK)
    return pl.pallas_call(
        feed_first_body,
        grid_spec=spec,
        out_shape=[
            jax.ShapeDtypeStruct(tile, F32),
            jax.ShapeDtypeStruct((UNITS, FF, BLK), BF16),
            jax.ShapeDtypeStruct((UNITS, FF, BLK), BF16),
            jax.ShapeDtypeStruct(tile, F32),
            jax.ShapeDtypeStruct(tile, BF16),
            jax.ShapeDtypeStruct((UNITS, 8, BLK), F32),
        ],
        compiler_params=params_of(),
        cost_estimate=cost(2 * 1536 * 256 * 2304, 14 << 20),
        name="feed_first",
    )(table, xt, o, small, wot, wut, wdt)


def feed_back_tail(
    g, gy, r_unit, r_inv, m, o, small_ref, parts, wu_ref, wd_ref, wo_ref, gr_ref, go_ref, gd_acc, gu_acc, go_acc, tail_acc
):
    tail_acc[2 * D : 3 * D, :] += fold(gy.astype(F32))
    gm = jnp.zeros((D, BLK), F32)
    for c in range(FF // BLK):
        rows = slice(c * BLK, (c + 1) * BLK)
        hid, slope = parts(c)
        gd_acc[rows, :] += dot_nt(hid, gy)
        ge = (dot(wd_ref[rows, :], gy) * slope).astype(BF16)
        gu_acc[:, rows] += dot_nt(m, ge)
        tail_acc[3 * D + c * BLK : 3 * D + (c + 1) * BLK, :] += fold(ge.astype(F32))
        gm = gm + dot(wu_ref[:, rows], ge)
    tail_acc[0:D, :] += fold(gm * r_unit)
    tail_acc[D : 2 * D, :] += fold(gm)
    gr = g + standardize_back(gm * param(small_ref, 2), r_unit, r_inv)
    gr_ref[0] = gr
    ga = gr.astype(BF16)
    go_acc[...] += dot_nt(o, ga)
    go_ref[0] = dot(wo_ref[...], ga).astype(BF16)


def feed_second_body(
    z_ref, o_ref, cot_ref, small_ref, wot_ref, wut_ref, wdt_ref, wo_ref, wu_ref, wd_ref,
    final_ref, sq_ref, gr_ref, go_ref, gd_acc, gu_acc, go_acc, tail_acc, hid_buf, slope_buf,
):
    @pl.when(pl.program_id(0) == 0)
    def _():
        for acc in (gd_acc, gu_acc, go_acc, tail_acc):
            acc[...] = jnp.zeros_like(acc)

    r, r_unit, r_inv, m = middle(z_ref[0], o_ref, wot_ref, small_ref)
    out = r + param(small_ref, 4)
    for c in range(FF // BLK):
        rows = slice(c * BLK, (c + 1) * BLK)
        e = dot(wut_ref[rows, :], m) + param(small_ref, 5 + c)
        hid, slope = gelu_parts(e)
        hid = hid.astype(BF16)
        hid_buf[rows, :] = hid
        slope_buf[rows, :] = slope
        out = out + dot(wdt_ref[:, rows], hid)
    sq_ref[0] = jnp.broadcast_to(jnp.sum(out * out, axis=0, keepdims=True), (8, BLK))
    final_ref[0] = out.T.astype(BF16)
    gy = cot_ref[0].T
    feed_back_tail(
        gy.astype(F32), gy, r_unit, r_inv, m, o_ref[0], small_ref,
        lambda c: (hid_buf[c * BLK : (c + 1) * BLK, :], slope_buf[c * BLK : (c + 1) * BLK, :]),
        wu_ref, wd_ref, wo_ref, gr_ref, go_ref, gd_acc, gu_acc, go_acc, tail_acc,
    )


TAIL = 3 * D + FF


def feed_second(z, o, cot, small, wot, wut, wdt, wo, wu, wd):
    tile = pl.BlockSpec((1, BLK, BLK), lambda u: (u, 0, 0))
    whole = lambda shape: pl.BlockSpec(shape, lambda u: (0,) * len(shape))
    return pl.pallas_call(
        feed_second_body,
        grid=(UNITS,),
        in_specs=[tile, tile, tile] + [full(w.shape) for w in (small, wot, wut, wdt, wo, wu, wd)],
        out_specs=[
            tile,
            pl.BlockSpec((1, 8, BLK), lambda u: (u, 0, 0)),
            tile,
            tile,
            whole((FF, D)),
            whole((D, FF)),
            whole((D, D)),
            whole((TAIL, 128)),
        ],
        out_shape=[
            jax.ShapeDtypeStruct((UNITS, BLK, BLK), BF16),
            jax.ShapeDtypeStruct((UNITS, 8, BLK), F32),
            jax.ShapeDtypeStruct((UNITS, BLK, BLK), F32),
            jax.ShapeDtypeStruct((UNITS, BLK, BLK), BF16),
            jax.ShapeDtypeStruct((FF, D), F32),
            jax.ShapeDtypeStruct((D, FF), F32),
            jax.ShapeDtypeStruct((D, D), F32),
            jax.ShapeDtypeStruct((TAIL, 128), F32),
        ],
        scratch_shapes=[pltpu.VMEM((FF, BLK), BF16), pltpu.VMEM((FF, BLK), F32)],
        compiler_params=params_of(),
        cost_estimate=cost(2 * 1536 * 256 * 2304 * 3, 12 << 20),
        name="feed_second",
    )(z, o, cot, small, wot, wut, wdt, wo, wu, wd)


def project_back(z, a, dq, dk, dv, gr, small_ref, wqkv_ref, gqkv_acc, head_acc):
    grad = dot(wqkv_ref[0], dq) + dot(wqkv_ref[1], dk) + dot(wqkv_ref[2], dv)
    gqkv_acc[0] += dot_nt(a, dq)
    gqkv_acc[1] += dot_nt(a, dk)
    gqkv_acc[2] += dot_nt(a, dv)
    unit_values, inverse = standardize(z)
    head_acc[0:D, :] += fold(grad * unit_values)
    head_acc[D : 2 * D, :] += fold(grad)
    return gr + standardize_back(grad * param(small_ref, 0), unit_values, inverse)


def turn_body(
    table, dq_ref, dk_ref, dv_ref, a_ref, z_ref, gr_ref, hid_ref, slope_ref, r_ref, o_ref, small_ref, wqkv_ref,
    wo_ref, wu_ref, wd_ref, gd_in, gu_in, go_in, tail_in,
    gz_ref, gr_out, go_out, gd_acc, gu_acc, go_acc, tail_acc, gqkv_acc, head_acc,
):
    @pl.when(pl.program_id(0) == 0)
    def _():
        gd_acc[...] = gd_in[...]
        gu_acc[...] = gu_in[...]
        go_acc[...] = go_in[...]
        tail_acc[...] = tail_in[...]
        gqkv_acc[...] = jnp.zeros_like(gqkv_acc)
        head_acc[...] = jnp.zeros_like(head_acc)

    g = project_back(
        z_ref[0], a_ref[0], dq_ref[0], dk_ref[0], dv_ref[0], gr_ref[0], small_ref, wqkv_ref, gqkv_acc, head_acc
    )
    gz_ref[0] = g
    r_unit, r_inv = standardize(r_ref[0])
    m = (r_unit * param(small_ref, 2) + param(small_ref, 3)).astype(BF16)
    feed_back_tail(
        g, g.astype(BF16), r_unit, r_inv, m, o_ref[0], small_ref,
        lambda c: (hid_ref[0, c * BLK : (c + 1) * BLK, :], slope_ref[0, c * BLK : (c + 1) * BLK, :].astype(F32)),
        wu_ref, wd_ref, wo_ref, gr_out, go_out, gd_acc, gu_acc, go_acc, tail_acc,
    )


def turn(table, dq, dk, dv, a, z, gr, hid, slope, r, o, small, wqkv, wo, wu, wd, gd, gu, go, tail):
    tile = pl.BlockSpec((1, BLK, BLK), lambda u, t: (u, 0, 0))
    moved = pl.BlockSpec((1, BLK, BLK), lambda u, t: (t[u], 0, 0))
    tall = pl.BlockSpec((1, FF, BLK), lambda u, t: (u, 0, 0))
    whole = lambda shape: pl.BlockSpec(shape, lambda u, t: (0,) * len(shape))
    spec = pltpu.PrefetchScalarGridSpec(
        num_scalar_prefetch=1,
        grid=(UNITS,),
        in_specs=[tile, tile, tile, moved, tile, tile, tall, tall, tile, tile]
        + [full(w.shape) for w in (small, wqkv, wo, wu, wd, gd, gu, go, tail)],
        out_specs=[tile, tile, tile]
        + [whole(s) for s in ((FF, D), (D, FF), (D, D), (TAIL, 128), (3, D, D), (2 * D, 128))],
    )
    shape = (UNITS, BLK, BLK)
    return pl.pallas_call(
        turn_body,
        grid_spec=spec,
        out_shape=[
            jax.ShapeDtypeStruct(shape, F32),
            jax.ShapeDtypeStruct(shape, F32),
            jax.ShapeDtypeStruct(shape, BF16),
        ]
        + [jax.ShapeDtypeStruct(s, F32) for s in ((FF, D), (D, FF), (D, D), (TAIL, 128), (3, D, D), (2 * D, 128))],
        compiler_params=params_of(),
        cost_estimate=cost(2 * 1536 * 256 * 3840 * 2, 20 << 20),
        name="turn",
    )(table, dq, dk, dv, a, z, gr, hid, slope, r, o, small, wqkv, wo, wu, wd, gd, gu, go, tail)


def last_body(
    table, dq_ref, dk_ref, dv_ref, a_ref, xt_ref, gr_ref, gz_ref, small_ref, wqkv_ref, gqkv_in, head_in,
    grad_ref, gqkv_acc, head_acc,
):
    @pl.when(pl.program_id(0) == 0)
    def _():
        gqkv_acc[...] = gqkv_in[...]
        head_acc[...] = head_in[...]

    g = project_back(
        xt_ref[0].astype(F32), a_ref[0], dq_ref[0], dk_ref[0], dv_ref[0], gr_ref[0], small_ref, wqkv_ref,
        gqkv_acc, head_acc,
    )
    grad_ref[0] = (g + gz_ref[0]).T.astype(BF16)


def last(table, dq, dk, dv, a, xt, gr, gz, small, wqkv, gqkv, head):
    tile = pl.BlockSpec((1, BLK, BLK), lambda u, t: (u, 0, 0))
    moved = pl.BlockSpec((1, BLK, BLK), lambda u, t: (t[u], 0, 0))
    whole = lambda shape: pl.BlockSpec(shape, lambda u, t: (0,) * len(shape))
    spec = pltpu.PrefetchScalarGridSpec(
        num_scalar_prefetch=1,
        grid=(UNITS,),
        in_specs=[tile, tile, tile, moved, moved, tile, tile]
        + [full(w.shape) for w in (small, wqkv, gqkv, head)],
        out_specs=[tile, whole((3, D, D)), whole((2 * D, 128))],
    )
    return pl.pallas_call(
        last_body,
        grid_spec=spec,
        out_shape=[
            jax.ShapeDtypeStruct((UNITS, BLK, BLK), BF16),
            jax.ShapeDtypeStruct((3, D, D), F32),
            jax.ShapeDtypeStruct((2 * D, 128), F32),
        ],
        compiler_params=params_of(),
        cost_estimate=cost(2 * 1536 * 256 * 768 * 2, 10 << 20),
        name="last",
    )(table, dq, dk, dv, a, xt, gr, gz, small, wqkv, gqkv, head)


def prepare_body(w_ref, p_ref, wt_ref, wot_ref, wut_ref, wdt_ref, wqkv_ref, wo_ref, wu_ref, wd_ref, small_ref):
    for t in range(3):
        matrix = w_ref[0, t]
        wqkv_ref[t] = matrix
        wt_ref[t * D : (t + 1) * D, :] = matrix.T
    matrix = w_ref[0, 3]
    wo_ref[...] = matrix
    wot_ref[...] = matrix.T
    for c in range(4):
        part = slice(c * D, (c + 1) * D)
        matrix = w_ref[1, c]
        wu_ref[:, part] = matrix
        wut_ref[part, :] = matrix.T
        matrix = w_ref[2, c]
        wd_ref[part, :] = matrix
        wdt_ref[:, part] = matrix.T
    for row in range(SMALL):
        for side in range(2):
            line = jnp.broadcast_to(p_ref[2 * row + side : 2 * row + side + 1, :], (128, 128))
            small_ref[row * D + side * 128 : row * D + (side + 1) * 128, :] = line.T


def prepare(w, p):
    shapes = [(3 * D, D), (D, D), (FF, D), (D, FF), (3, D, D), (D, D), (D, FF), (FF, D)]
    return pl.pallas_call(
        prepare_body,
        in_specs=[pl.BlockSpec(memory_space=pltpu.VMEM)] * 2,
        out_specs=[pl.BlockSpec(memory_space=pltpu.VMEM)] * 9,
        out_shape=[jax.ShapeDtypeStruct(s, BF16) for s in shapes] + [jax.ShapeDtypeStruct((SMALL * D, 128), F32)],
        compiler_params=pltpu.CompilerParams(vmem_limit_bytes=40 << 20),
        cost_estimate=cost(1, 6 << 20),
        name="prepare",
    )(w, p)


def owner_scalars(owner_ref):
    sizes = [D * D] * 4 + [D * FF, FF * D, SMALL * D]
    starts = []
    for t in range(7):
        offset = jnp.int32(0)
        for u in range(t):
            offset = offset + jnp.where(owner_ref[u] == owner_ref[t], sizes[u], 0).astype(jnp.int32)
        starts.append(offset)
    return starts


def pack_body(owner_ref, row_ref, w_ref, p_ref):
    dp = lax.axis_index("dp")
    seq = lax.axis_index("seq")
    starts = owner_scalars(owner_ref)
    square = jnp.where(seq == 0, starts[0], jnp.where(seq == 1, starts[1], jnp.where(seq == 2, starts[2], starts[3])))
    plans = (
        (owner_ref[seq], square // 128, 2),
        (owner_ref[4], starts[4] // 128 + 2 * seq, FF // 128),
        (owner_ref[5], starts[5] // 128 + 2 * D * seq, 2),
    )
    for kind, (owner, base, stride) in enumerate(plans):
        keep = jnp.where(owner == dp, 1.0, 0.0).astype(F32)
        for side in range(2):
            values = row_ref[pl.ds(base + side, D, stride=stride), :]
            w_ref[kind, :, side * 128 : (side + 1) * 128] = (values * keep).astype(BF16)
    keep = jnp.where(owner_ref[6] == dp, 1.0, 0.0).astype(F32)
    values = row_ref[pl.ds(pl.multiple_of(starts[6] // 128, 8), 24), :] * keep
    rows = lax.broadcasted_iota(jnp.int32, (24, 128), 0)
    p_ref[...] = jnp.where(rows < 2 * SMALL, values, 0.0)


def pack(owner_list, row):
    return pl.pallas_call(
        pack_body,
        in_specs=[pl.BlockSpec(memory_space=pltpu.SMEM), pl.BlockSpec(memory_space=pltpu.VMEM)],
        out_specs=[pl.BlockSpec(memory_space=pltpu.VMEM)] * 2,
        out_shape=[jax.ShapeDtypeStruct((3, D, D), BF16), jax.ShapeDtypeStruct((24, 128), F32)],
        compiler_params=pltpu.CompilerParams(vmem_limit_bytes=20 << 20),
        cost_estimate=cost(1, 3 << 20),
        name="pack",
    )(owner_list, row)


def peers_of(seq):
    return {1: seq + 1 - 2 * (seq % 2), 2: (seq + 2) % 4, 3: 3 - seq}


def greet(n, dp, peers, wide_group):
    barrier = pltpu.get_barrier_semaphore()
    count = 0
    for peer in peers:
        pl.semaphore_signal(barrier, inc=1, device_id={"seq": peer}, device_id_type=MESH)
        count += 1
    if wide_group:
        for k in range(1, n):
            pl.semaphore_signal(barrier, inc=1, device_id={"dp": (dp + k) % n}, device_id_type=MESH)
            count += 1
    pl.semaphore_wait(barrier, count)


def send(source, target, sems, index, device):
    return pltpu.make_async_remote_copy(
        src_ref=source,
        dst_ref=target,
        send_sem=sems[0].at[index],
        recv_sem=sems[1].at[index],
        device_id=device,
        device_id_type=MESH,
    )


def spread(n, dp, seq, peers, kind, w_ref, chunk_ref, row_sems):
    copies = []
    for k in range(1, n):
        copies.append(
            send(chunk_ref.at[kind], w_ref.at[kind, seq, dp], row_sems, (kind, k), {"dp": (dp + k) % n})
        )
        copies[-1].start()
    return copies


def share(seq, peers, kind, w_ref, side_sems):
    copies = [
        send(w_ref.at[kind, seq], w_ref.at[kind, seq], side_sems, (kind, 0), {"seq": peers[2]}),
        send(w_ref.at[kind, seq], w_ref.at[kind, seq], side_sems, (kind, 1), {"seq": peers[1]}),
    ]
    for copy in copies:
        copy.start()
    return copies


def forward(seq, peers, kind, w_ref, side_sems):
    copy = send(w_ref.at[kind, peers[2]], w_ref.at[kind, peers[2]], side_sems, (kind, 2), {"seq": peers[1]})
    copy.start()
    return copy


def entry_body(
    n, pk_ref, pp_ref, x_ref, c_ref, w_ref, p_ref, xo_ref, co_ref, slot_ref, pslot_ref, chunk_ref,
    ss0, ss1, rs0, rs1, ps0, ps1, gs0, gs1, xs0, xs1, cs0, cs1,
):
    dp = lax.axis_index("dp")
    seq = lax.axis_index("seq")
    chip, core = seq // 2, seq % 2
    peers = peers_of(seq)
    greet(n, dp, [peers[1], peers[2], peers[3]], True)
    done = []
    small = []
    scatter = [[] for _ in range(3)]
    for kind in range(3):
        for k in range(1, n):
            to = (dp + k) % n
            copy = send(pk_ref.at[kind, to], slot_ref.at[kind, k], (ss0, ss1), (kind, k), {"dp": to})
            copy.start()
            scatter[kind].append(copy)
        if kind == 0:
            for k in range(1, n):
                copy = send(pp_ref, pslot_ref.at[k], (ps0, ps1), k, {"dp": (dp + k) % n})
                copy.start()
                small.append(copy)
    for o in (2, 3, 1):
        to = peers[o]
        for part, (source, target) in enumerate(((3 * (to // 2) + to % 2, seq), (3 * (to // 2) + 2, OWN + seq))):
            copy = send(x_ref.at[source], xo_ref.at[target], (xs0, xs1), (o, part), {"seq": to})
            copy.start()
            done.append(copy)
    for o in (2, 3, 1):
        to = peers[o]
        copy = send(c_ref.at[3 * (to // 2) + to % 2], co_ref.at[seq], (cs0, cs1), o, {"seq": to})
        copy.start()
        done.append(copy)

    @pl.when(chip == 0)
    def _():
        send(c_ref.at[5], co_ref.at[4], (cs0, cs1), 4 + 2, {"seq": peers[2]}).start()

    @pl.when(chip == 1)
    def _():
        send(c_ref.at[2], co_ref.at[5], (cs0, cs1), 4 + 3, {"seq": peers[3]}).start()
        send(c_ref.at[5], co_ref.at[5], (cs0, cs1), 4 + 1, {"seq": peers[1]}).start()

    xo_ref[seq] = x_ref[3 * chip + core]
    xo_ref[OWN + seq] = x_ref[3 * chip + 2]
    co_ref[seq] = c_ref[3 * chip + core]

    @pl.when(chip == 0)
    def _():
        co_ref[4] = c_ref[2]

    gathers = []
    for kind in range(3):
        total = pk_ref[kind, dp].astype(F32)
        for k in range(1, n):
            scatter[kind][k - 1].wait_recv()
            total = total + slot_ref[kind, k].astype(F32)
        chunk_ref[kind] = total.astype(BF16)
        w_ref[kind, seq, dp] = total.astype(BF16)
        gathers.append(spread(n, dp, seq, peers, kind, w_ref, chunk_ref, (rs0, rs1)))
    sides = []
    for kind in range(3):
        for copy in gathers[kind]:
            copy.wait_recv()
        sides.append(share(seq, peers, kind, w_ref, (gs0, gs1)))
    total = pp_ref[...]
    for copy in small:
        copy.wait_recv()
    for k in range(1, n):
        total = total + pslot_ref[k]
    p_ref[...] = total
    for kind in range(3):
        sides[kind][0].wait_recv()
        sides[kind].append(forward(seq, peers, kind, w_ref, (gs0, gs1)))
    for kind in range(3):
        sides[kind][1].wait_recv()
        sides[kind][2].wait_recv()

    @pl.when(chip == 0)
    def _():
        send(c_ref.at[5], co_ref.at[4], (cs0, cs1), 4 + 2, {"seq": peers[2]}).wait_send()
        send(c_ref.at[2], co_ref.at[5], (cs0, cs1), 4 + 3, {"seq": peers[3]}).wait_recv()

    @pl.when(chip == 1)
    def _():
        send(c_ref.at[2], co_ref.at[5], (cs0, cs1), 4 + 3, {"seq": peers[3]}).wait_send()
        send(c_ref.at[5], co_ref.at[5], (cs0, cs1), 4 + 1, {"seq": peers[1]}).wait_send()
        send(c_ref.at[5], co_ref.at[4], (cs0, cs1), 4 + 2, {"seq": peers[2]}).wait_recv()
        send(c_ref.at[5], co_ref.at[5], (cs0, cs1), 4 + 1, {"seq": peers[1]}).wait_recv()

    for copy in done:
        copy.wait()
    for kind in range(3):
        for copy in scatter[kind] + gathers[kind] + sides[kind]:
            copy.wait_send()
    for copy in small:
        copy.wait_send()


def pair_of_sems(shape):
    return [pltpu.SemaphoreType.DMA(shape), pltpu.SemaphoreType.DMA(shape)]


def entry(n, pk, pp, x, c):
    rows = D // n
    vmem = pl.BlockSpec(memory_space=pltpu.VMEM)
    return pl.pallas_call(
        partial(entry_body, n),
        in_specs=[vmem] * 4,
        out_specs=[vmem] * 4,
        out_shape=[
            jax.ShapeDtypeStruct((3, 4, n, rows, D), BF16),
            jax.ShapeDtypeStruct((24, 128), F32),
            jax.ShapeDtypeStruct((ALL, BLK, BLK), BF16),
            jax.ShapeDtypeStruct((UNITS, BLK, BLK), BF16),
        ],
        scratch_shapes=[
            pltpu.VMEM((3, n, rows, D), BF16),
            pltpu.VMEM((n, 24, 128), F32),
            pltpu.VMEM((3, rows, D), BF16),
            *pair_of_sems((3, n)),
            *pair_of_sems((3, n)),
            *pair_of_sems((n,)),
            *pair_of_sems((3, 3)),
            *pair_of_sems((4, 2)),
            *pair_of_sems((8,)),
        ],
        compiler_params=pltpu.CompilerParams(collective_id=0, has_side_effects=True, vmem_limit_bytes=40 << 20),
        cost_estimate=cost(1, 12 << 20),
        name="entry",
    )(pk, pp, x, c)


def swap_inputs_body(a_ref, out_ref, s0, s1):
    seq = lax.axis_index("seq")
    core = seq % 2
    peers = peers_of(seq)
    greet(1, 0, [peers[1]], False)
    copies = [
        send(a_ref.at[4], out_ref.at[4 + core], (s0, s1), 0, {"seq": peers[1]}),
        send(a_ref.at[5], out_ref.at[7 - core], (s0, s1), 1, {"seq": peers[1]}),
    ]
    for copy in copies:
        copy.start()
    for j in range(OWN):
        out_ref[j] = a_ref[j]
    out_ref[4 + core] = a_ref[4]
    out_ref[7 - core] = a_ref[5]
    for copy in copies:
        copy.wait()


def swap_inputs(a):
    vmem = pl.BlockSpec(memory_space=pltpu.VMEM)
    return pl.pallas_call(
        swap_inputs_body,
        in_specs=[vmem],
        out_specs=vmem,
        out_shape=jax.ShapeDtypeStruct((ALL, BLK, BLK), BF16),
        scratch_shapes=pair_of_sems((2,)),
        compiler_params=pltpu.CompilerParams(collective_id=1, has_side_effects=True, vmem_limit_bytes=16 << 20),
        cost_estimate=cost(1, 2 << 20),
        name="swap_inputs",
    )(a)


def swap_grads_body(dk_ref, dv_ref, dk_out, dv_out, slot_ref, s0, s1):
    seq = lax.axis_index("seq")
    core = seq % 2
    peers = peers_of(seq)
    greet(1, 0, [peers[1]], False)
    copies = []
    for which, ref in enumerate((dk_ref, dv_ref)):
        for place, position in enumerate((5 - core, 6 + core)):
            copies.append(
                send(ref.at[position], slot_ref.at[which, place], (s0, s1), (which, place), {"seq": peers[1]})
            )
            copies[-1].start()
    for ref, out in ((dk_ref, dk_out), (dv_ref, dv_out)):
        for j in range(OWN):
            out[j] = ref[j]
    for copy in copies:
        copy.wait()
    for which, (ref, out) in enumerate(((dk_ref, dk_out), (dv_ref, dv_out))):
        for place, position in enumerate((4 + core, 7 - core)):
            out[4 + place] = (ref[position].astype(F32) + slot_ref[which, place].astype(F32)).astype(BF16)


def swap_grads(dk, dv):
    vmem = pl.BlockSpec(memory_space=pltpu.VMEM)
    out = jax.ShapeDtypeStruct((UNITS, BLK, BLK), BF16)
    return pl.pallas_call(
        swap_grads_body,
        in_specs=[vmem] * 2,
        out_specs=[vmem] * 2,
        out_shape=[out, out],
        scratch_shapes=[pltpu.VMEM((2, 2, BLK, BLK), BF16), *pair_of_sems((2, 2))],
        compiler_params=pltpu.CompilerParams(collective_id=2, has_side_effects=True, vmem_limit_bytes=16 << 20),
        cost_estimate=cost(1, 4 << 20),
        name="swap_grads",
    )(dk, dv)


def collect_body(n, gqkv_ref, go_ref, gu_ref, gd_ref, head_ref, tail_ref, sq1_ref, sq2_ref, g_ref, p_ref):
    dp = lax.axis_index("dp")
    seq = lax.axis_index("seq")
    chip, core = seq // 2, seq % 2
    for t in range(3):
        g_ref[0, t] = gqkv_ref[t].astype(BF16)
    g_ref[0, 3] = go_ref[...].astype(BF16)
    for c in range(4):
        g_ref[1, c] = gu_ref[:, c * D : (c + 1) * D].astype(BF16)
        g_ref[2, c] = gd_ref[c * D : (c + 1) * D, :].astype(BF16)
    for row in range(SMALL):
        for side in range(2):
            ref, first = (head_ref, row) if row < 2 else (tail_ref, row - 2)
            first = first * D + side * 128
            p_ref[2 * row + side : 2 * row + side + 1, :] = jnp.sum(ref[first : first + 128, :].T, axis=0, keepdims=True)
    sequences = 6 * n
    place = lax.broadcasted_iota(jnp.int32, (6, 128), 0) * 128 + lax.broadcasted_iota(jnp.int32, (6, 128), 1)
    stats = jnp.zeros((6, 128), F32)
    for i, ref in enumerate((sq1_ref, sq2_ref)):
        lines = [ref[u, 0:1, :] for u in range(UNITS)]
        own = jnp.sum(lines[0] + lines[1] + lines[2] + lines[3], axis=1, keepdims=True)
        half = jnp.sum(lines[4] + lines[5], axis=1, keepdims=True)
        start = i * sequences + 6 * dp + 3 * chip
        stats = jnp.where(place == start + core, jnp.broadcast_to(own, (6, 128)), stats)
        stats = jnp.where(place == start + 2, jnp.broadcast_to(half, (6, 128)), stats)
    p_ref[18:24, :] = stats


def collect(n, gqkv, go, gu, gd, head, tail, sq1, sq2):
    vmem = pl.BlockSpec(memory_space=pltpu.VMEM)
    return pl.pallas_call(
        partial(collect_body, n),
        in_specs=[vmem] * 8,
        out_specs=[vmem] * 2,
        out_shape=[jax.ShapeDtypeStruct((3, 4, D, D), BF16), jax.ShapeDtypeStruct((24, 128), F32)],
        compiler_params=pltpu.CompilerParams(vmem_limit_bytes=24 << 20),
        cost_estimate=cost(1, 6 << 20),
        name="collect",
    )(gqkv, go, gu, gd, head, tail, sq1, sq2)


def leave_body(
    n, g_ref, pp_ref, f_ref, i_ref, w_ref, p_ref, fo_ref, io_ref,
    half_ref, quarter_ref, out_ref, mine_ref, slot_ref, chunk_ref, pslot_ref, psum_ref,
    as0, as1, bs0, bs1, ss0, ss1, rs0, rs1, gs0, gs1, ps0, ps1, xs0, xs1,
):
    dp = lax.axis_index("dp")
    seq = lax.axis_index("seq")
    chip, core = seq // 2, seq % 2
    peers = peers_of(seq)
    greet(n, dp, [peers[1], peers[2], peers[3]], True)
    finish = []

    first = []
    for kind in range(3):
        copies = []
        for j, quarter in enumerate((peers[1], peers[3])):
            copies.append(
                send(g_ref.at[kind, quarter], half_ref.at[kind, j], (as0, as1), (kind, j), {"seq": peers[1]})
            )
            copies[-1].start()
        first.append(copies)
        finish += copies
    small = [send(pp_ref, pslot_ref.at[0], (ps0, ps1), 0, {"seq": peers[1]})]
    small[0].start()

    moves = []
    own = 3 * chip + core

    def move(which, source_ref, target_ref):
        for o in (2, 3, 1):
            copy = send(source_ref.at[peers[o]], target_ref.at[own], (xs0, xs1), (which, o), {"seq": peers[o]})
            copy.start()
            moves.append(copy)

        @pl.when(chip == 0)
        def _():
            send(source_ref.at[5], target_ref.at[2], (xs0, xs1), (which, 4 + 3), {"seq": peers[3]}).start()

        @pl.when(chip == 1)
        def _():
            send(source_ref.at[4], target_ref.at[5], (xs0, xs1), (which, 4 + 2), {"seq": peers[2]}).start()
            send(source_ref.at[5], target_ref.at[5], (xs0, xs1), (which, 4 + 1), {"seq": peers[1]}).start()

        target_ref[own] = source_ref[seq]

        @pl.when(chip == 0)
        def _():
            target_ref[2] = source_ref[4]

    def settle(which, source_ref, target_ref):
        @pl.when(chip == 0)
        def _():
            send(source_ref.at[5], target_ref.at[2], (xs0, xs1), (which, 4 + 3), {"seq": peers[3]}).wait_send()
            send(source_ref.at[4], target_ref.at[5], (xs0, xs1), (which, 4 + 2), {"seq": peers[2]}).wait_recv()

        @pl.when(chip == 1)
        def _():
            send(source_ref.at[4], target_ref.at[5], (xs0, xs1), (which, 4 + 2), {"seq": peers[2]}).wait_send()
            send(source_ref.at[5], target_ref.at[5], (xs0, xs1), (which, 4 + 1), {"seq": peers[1]}).wait_send()
            send(source_ref.at[5], target_ref.at[2], (xs0, xs1), (which, 4 + 3), {"seq": peers[3]}).wait_recv()
            send(source_ref.at[5], target_ref.at[5], (xs0, xs1), (which, 4 + 1), {"seq": peers[1]}).wait_recv()

    second = []
    for kind in range(3):
        for copy in first[kind]:
            copy.wait_recv()
        out_ref[kind] = (g_ref[kind, peers[2]].astype(F32) + half_ref[kind, 1].astype(F32)).astype(BF16)
        second.append(send(out_ref.at[kind], quarter_ref.at[kind], (bs0, bs1), kind, {"seq": peers[2]}))
        second[-1].start()
    finish += second
    small[0].wait_recv()
    psum_ref[0] = pp_ref[...] + pslot_ref[0]
    small.append(send(psum_ref.at[0], pslot_ref.at[1], (ps0, ps1), 1, {"seq": peers[2]}))
    small[1].start()
    move(0, f_ref, fo_ref)
    move(1, i_ref, io_ref)

    scatter = []
    for kind in range(3):
        second[kind].wait_recv()
        mine_ref[kind] = (
            g_ref[kind, seq].astype(F32) + half_ref[kind, 0].astype(F32) + quarter_ref[kind].astype(F32)
        ).astype(BF16)
        copies = []
        for k in range(1, n):
            to = (dp + k) % n
            copies.append(send(mine_ref.at[kind, to], slot_ref.at[kind, k], (ss0, ss1), (kind, k), {"dp": to}))
            copies[-1].start()
        scatter.append(copies)
        finish += copies
    small[1].wait_recv()
    psum_ref[1] = psum_ref[0] + pslot_ref[1]
    for k in range(1, n):
        copy = send(psum_ref.at[1], pslot_ref.at[1 + k], (ps0, ps1), 1 + k, {"dp": (dp + k) % n})
        copy.start()
        small.append(copy)
    gathers = []
    for kind in range(3):
        total = mine_ref[kind, dp].astype(F32)
        for k in range(1, n):
            scatter[kind][k - 1].wait_recv()
            total = total + slot_ref[kind, k].astype(F32)
        chunk_ref[kind] = total.astype(BF16)
        w_ref[kind, seq, dp] = total.astype(BF16)
        gathers.append(spread(n, dp, seq, peers, kind, w_ref, chunk_ref, (rs0, rs1)))
    sides = []
    for kind in range(3):
        for copy in gathers[kind]:
            copy.wait_recv()
        sides.append(share(seq, peers, kind, w_ref, (gs0, gs1)))
        finish += gathers[kind]
    total = psum_ref[1]
    for k in range(1, n):
        small[1 + k].wait_recv()
        total = total + pslot_ref[1 + k]
    p_ref[...] = total
    for kind in range(3):
        sides[kind][0].wait_recv()
        sides[kind].append(forward(seq, peers, kind, w_ref, (gs0, gs1)))
    for kind in range(3):
        sides[kind][1].wait_recv()
        sides[kind][2].wait_recv()
        finish += sides[kind]
    settle(0, f_ref, fo_ref)
    settle(1, i_ref, io_ref)
    for copy in moves:
        copy.wait()
    for copy in finish + small:
        copy.wait_send()


def leave(n, g, pp, f, i):
    rows = D // n
    vmem = pl.BlockSpec(memory_space=pltpu.VMEM)
    return pl.pallas_call(
        partial(leave_body, n),
        in_specs=[vmem] * 4,
        out_specs=[vmem] * 4,
        out_shape=[
            jax.ShapeDtypeStruct((3, 4, n, rows, D), BF16),
            jax.ShapeDtypeStruct((24, 128), F32),
            jax.ShapeDtypeStruct((UNITS, BLK, BLK), BF16),
            jax.ShapeDtypeStruct((UNITS, BLK, BLK), BF16),
        ],
        scratch_shapes=[
            pltpu.VMEM((3, 2, n, rows, D), BF16),
            pltpu.VMEM((3, n, rows, D), BF16),
            pltpu.VMEM((3, n, rows, D), BF16),
            pltpu.VMEM((3, n, rows, D), BF16),
            pltpu.VMEM((3, n, rows, D), BF16),
            pltpu.VMEM((3, rows, D), BF16),
            pltpu.VMEM((1 + n, 24, 128), F32),
            pltpu.VMEM((2, 24, 128), F32),
            *pair_of_sems((3, 2)),
            *pair_of_sems((3,)),
            *pair_of_sems((3, n)),
            *pair_of_sems((3, n)),
            *pair_of_sems((3, 3)),
            *pair_of_sems((1 + n,)),
            *pair_of_sems((2, 8)),
        ],
        compiler_params=pltpu.CompilerParams(collective_id=3, has_side_effects=True, vmem_limit_bytes=48 << 20),
        cost_estimate=cost(1, 20 << 20),
        name="leave",
    )(g, pp, f, i)


ROWS = D * D // 128


def adam_body(owner_ref, g_ref, p_ref, m_ref, v_ref, w_ref, m_out, v_out, w_out, grad_ref):
    dp = lax.axis_index("dp")
    block = pl.program_id(0)
    starts = owner_scalars(owner_ref)
    counts = [1, 1, 1, 1, 4, 4, 1]
    rate = jnp.float32(D ** (-0.5))
    decay = jnp.float32(0.1)
    limit = jnp.int32(0)
    for t in range(7):
        first = starts[t] // (D * D)
        here = (owner_ref[t] == dp) & (block >= first) & (block < first + counts[t])
        part = block - first
        limit = jnp.where(here, 2 * SMALL if t == 6 else ROWS, limit)
        if t == 5:
            rate = jnp.where(here, FF ** (-0.5), rate)
        if t == 6:
            rate = jnp.where(here, 0.5, rate)
            decay = jnp.where(here, 0.0, decay)

        @pl.when(here)
        def _(t=t, part=part):
            if t == 6:
                grad_ref[0:24, :] = p_ref[...]
            elif t == 4:
                for c in range(4):
                    piece = g_ref[4 + c, pl.ds(pl.multiple_of(part * 64, 64), 64), :].astype(F32)
                    for side in range(2):
                        grad_ref[pl.ds(2 * c + side, 64, stride=8), :] = piece[:, side * 128 : (side + 1) * 128]
            else:
                piece = g_ref[8 + part if t == 5 else t].astype(F32)
                for side in range(2):
                    grad_ref[pl.ds(side, D, stride=2), :] = piece[:, side * 128 : (side + 1) * 128]

    @pl.when(limit == 0)
    def _():
        for out in (m_out, v_out, w_out):
            out[...] = jnp.zeros_like(out)

    @pl.when(limit > 0)
    def _():
        correction = 1.0 - 0.5**STEP
        grad = grad_ref[...]
        valid = lax.broadcasted_iota(jnp.int32, (ROWS, 128), 0) < limit
        first_new = 0.5 * m_ref[...] + 0.5 * grad
        second_new = 0.5 * v_ref[...] + 0.5 * grad * grad
        old = w_ref[...]
        update = first_new / correction / (jnp.sqrt(second_new / correction) + adam_eps) + decay * old
        m_out[...] = jnp.where(valid, first_new, 0.0)
        v_out[...] = jnp.where(valid, second_new, 0.0)
        w_out[...] = jnp.where(valid, old - rate * update, 0.0)


def adam(owner_list, g, p, m, v, w):
    tile = pl.BlockSpec((ROWS, 128), lambda b, t: (b, 0))
    out = jax.ShapeDtypeStruct(m.shape, F32)
    spec = pltpu.PrefetchScalarGridSpec(
        num_scalar_prefetch=1,
        grid=(m.shape[0] // ROWS,),
        in_specs=[full(g.shape), full(p.shape), tile, tile, tile],
        out_specs=[tile, tile, tile],
        scratch_shapes=[pltpu.VMEM((ROWS, 128), F32)],
    )
    return pl.pallas_call(
        adam_body,
        grid_spec=spec,
        out_shape=[out, out, out],
        compiler_params=params_of(),
        cost_estimate=cost(20 * 524288, 14 << 20),
        name="adam",
    )(owner_list, g, p, m, v, w)


def per_device(inputs, cotangent, owner_list, master_rows, moment1_rows, moment2_rows):
    n = lax.axis_size("dp")
    seq = lax.axis_index("seq")
    core = seq % 2
    rows = D // n
    flat = [r.reshape(-1, 128) for r in (master_rows, moment1_rows, moment2_rows)]
    pk, pp = pack(owner_list, flat[0])
    w, p, x, cot = entry(n, pk.reshape(3, n, rows, D), pp, inputs, cotangent)
    wt, wot, wut, wdt, wqkv, wo, wu, wd, small = prepare(w.reshape(3, 4, D, D), p)
    lane = jnp.arange(UNITS, dtype=jnp.int32)
    place = jnp.where(lane < OWN, lane, jnp.where(lane == OWN, core, 3 - core))
    base = jnp.where(lane < OWN, 0, OWN)
    table = jnp.concatenate([base + place, base, place]).astype(jnp.int32)

    xt, a1, q1, kt1, vt1, k1, v1 = first_projection(x, small, wt)
    o1, log1 = attend(table, q1, k1, vt1)
    r1, hid, slope, z2, a2, sq1 = feed_first(table, xt, o1, small, wot, wut, wdt)
    a2 = swap_inputs(a2)
    q2, kt2, vt2, k2, v2 = second_projection(a2, wt)
    o2, log2 = attend(table, q2, k2, vt2)
    final, sq2, gr, go, gd, gu, gout, tail = feed_second(z2, o2, cot, small, wot, wut, wdt, wo, wu, wd)
    dq, dk, dv = attend_back(table, q2, k2, kt2, v2, go, o2, log2)
    dk, dv = swap_grads(dk, dv)
    gz, gr, go, gd, gu, gout, tail, gqkv, head = turn(
        table, dq, dk, dv, a2, z2, gr, hid, slope, r1, o1, small, wqkv, wo, wu, wd, gd, gu, gout, tail
    )
    dq, dk, dv = attend_back(table, q1, k1, kt1, v1, go, o1, log1)
    dk, dv = swap_grads(dk, dv)
    grad, gqkv, head = last(table, dq, dk, dv, a1, xt, gr, gz, small, wqkv, gqkv, head)
    g, pp = collect(n, gqkv, gout, gu, gd, head, tail, sq1, sq2)
    g, p, final, grad = leave(n, g.reshape(3, 4, n, rows, D), pp, final, grad)
    m_new, v_new, w_new = adam(owner_list, g.reshape(12, D, D), p, flat[1], flat[2], flat[0])
    sequences = inputs.shape[0] * n
    entries = inputs.shape[1] * lax.axis_size("seq") * D
    squares = p[18:].reshape(-1)[: 2 * sequences].reshape(2, sequences)
    stats = jnp.sqrt(squares / entries + stat_eps)
    back = lambda r: r.reshape(master_rows.shape)
    return (final.astype(F32), grad.astype(F32), stats, back(m_new), back(v_new), back(w_new))


def solution(mesh):
    placed = (P("dp", "seq", None), P("dp", "seq", None), P(), P("dp", None), P("dp", None), P("dp", None))
    return jax.shard_map(
        per_device,
        mesh=mesh,
        in_specs=placed,
        out_specs=(P("dp", "seq", None), P("dp", "seq", None), P(), P("dp", None), P("dp", None), P("dp", None)),
        check_vma=False,
    )
```

time: 962 us -> 276 us (0.29); the launches traced: 949 us -> 274 us
  Pallas kernels: 0 us -> 243 us
  blocking collectives: 226 us -> 0 us
  waiting for transfers between devices: 217 us -> 0 us
  local copies, waits for them, and re-layouts: 179 us -> 26.9 us
  matrix products: 133 us -> 0 us
  other arithmetic: 115 us -> 3.74 us
  between operations: 48 us -> 0.9 us
  starting transfers between devices: 30.6 us -> 0 us
    pallas_call x0 -> x19, Pallas kernels: none -> 243 us  [the longest x2 44.3 us: attend_back(): pl.pallas_call(attend_back_body, grid_spec=spec, out_shape=[jax.ShapeDtyp...]
    dot_general x108 -> x0, matrix products: 133 us -> none  [the longest x24 23.6 us: masked_scores(): jnp.einsum('qhd,khd->hqk', queries, keys_part, preferred_element_type=jnp...]
    psum x1 -> x0, blocking collectives: 133 us -> none  [per_device(): lax.psum((owned_parts[0], owned_parts[1], owned_parts[2], owned_parts[3],...]
    all_to_all x7 -> x0, waiting for transfers between devices: 129 us -> none  [the longest x2 57.1 us: block_forward(): lax.all_to_all(per_head, 'seq', split_axis=2, concat_axis=1, tiled=True)]
    psum x1 -> x0, waiting for transfers between devices: 88.7 us -> none  [per_device(): lax.psum((local_sums[0], local_sums[1], local_sums[2], local_sums[3], loc...]
    all_to_all x1 -> x0, blocking collectives: 53.8 us -> none  [block_backward(): lax.all_to_all(grad_packed, 'seq', split_axis=1, concat_axis=2, tiled=True)]
    convert_element_type x16 -> x2, other arithmetic: 44.5 us -> 2.57 us  [the longest x1 1.28 us: per_device(): final.astype(F32)]
    unnamed x1 -> x0, blocking collectives: 39.1 us -> none
  transfers between devices with their start and end apart: 8 -> 0, of which waited for: 8 -> 0; matrix products, arithmetic and copies ran while one was open for 3% -> 0% of each run, Pallas kernels for 0% -> 0%
where the time goes in v1:
time: 276 us; the launch traced here: 274 us
  Pallas kernels  243 us (88%)
  local copies, waits for them, and re-layouts  26.9 us (10%)
  other arithmetic  3.74 us (1%)
    pallas_call x2, Pallas kernels, attend_back(): pl.pallas_call(attend_back_body, grid_spec=spec, out_shape=[jax.ShapeDtyp...  44.3 us
    pallas_call x1, Pallas kernels, leave(): pl.pallas_call(partial(leave_body, n), in_specs=[vmem] * 4, out_specs=[vm...  43.1 us
    pallas_call x1, Pallas kernels, entry(): pl.pallas_call(partial(entry_body, n), in_specs=[vmem] * 4, out_specs=[vm...  38.5 us
    pallas_call x2, Pallas kernels, attend(): pl.pallas_call(attend_body, grid_spec=spec, out_shape=[jax.ShapeDtypeStru...  27.2 us
    unnamed x76, local copies, waits for them, and re-layouts  26.9 us
    pallas_call x1, Pallas kernels, turn(): pl.pallas_call(turn_body, grid_spec=spec, out_shape=[jax.ShapeDtypeStruct...  19.2 us
    pallas_call x1, Pallas kernels, feed_second(): pl.pallas_call(feed_second_body, grid=(UNITS,), in_specs=[tile, tile, til...  18.1 us
    pallas_call x1, Pallas kernels, feed_first(): pl.pallas_call(feed_first_body, grid_spec=spec, out_shape=[jax.ShapeDtype...  10.9 us

profile of v1, /device:TPU:0, one launch (start us, length us, event | category | flops | bytes accessed | tf_op | source)
XLA Modules:
  0.0 274.3 jit_solution(874426846661704471)
XLA Ops:
  0.7 0.6 pad_add_fusion.table
  1.2 1.6 copy-done
  2.8 0.7 copy-done.26
  3.5 0.7 pack.1
  4.9 38.5 %entry.1 = (bf16[3,4,8,32,256]{4,3,2,1,0:T(8,128)(2,1)S(1)}, f32[24,128]{1,0:T(8,128)S(1)}, bf16[8,256,256]{2,1,0:T(8,128)(2,1)S(1)}, bf16[6,256,256]{2,1,0:T(8,128)(2,1)S(1)}) custom-call(bf16[3,8,32,256]{3,2,1,0:T(8,128)(2,1)S(1)} %bitcast.15, f32[24,128]{1,0:T(8,128)S(1)} %get-tuple-element.83.pp_ref, bf16[6,256,256]{2,1,0:T(8,128)(2,1)S(1)} %copy-done.15, ...), custom_call_target="tpu_custom_call" | custom-call | flops 1 | bytes 12582912 | tf_op jit(solution)/shard_map/entry/pallas_call | solution.py:798
  43.4 1.0 copy-done.27
  44.3 0.9 copy-done.28
  45.3 0.8 prepare.1
  46.1 1.1 copy-done.3
  47.1 0.8 copy-done.20
  47.9 0.8 copy-done.31
  48.7 0.8 copy-done.32
  49.5 0.8 copy-done.33
  50.3 0.8 copy-done.34
  51.1 0.7 copy-done.35
  51.9 0.6 copy-done.36
  52.5 0.6 copy-done.37
  53.2 8.2 %first_projection.1 = (bf16[8,256,256]{2,1,0:T(8,128)(2,1)}, bf16[8,256,256]{2,1,0:T(8,128)(2,1)}, bf16[8,256,256]{2,1,0:T(8,128)(2,1)}, bf16[8,256,256]{2,1,0:T...) custom-call(bf16[8,256,256]{2,1,0:T(8,128)(2,1)} %copy-done.27, ...), custom_call_target="tpu_custom_call" | custom-call | flops 805306368 | bytes 9437184 | tf_op jit(solution)/shard_map/first_projection/pallas_call | solution.py:118
  61.4 13.6 %attend.2 = (bf16[6,256,256]{2,1,0:T(8,128)(2,1)}, f32[6,2,8,256]{3,2,1,0:T(8,128)}) custom-call(s32[18]{0:T(128)} %pad_add_fusion.table, bf16[8,256,256]{2,1,0:T(8,128)(2,1)} %get-tuple-element.89.q_ref, bf16[8,256,256]{2,1,0:T(8,128)(2,1)} %get-tuple-element.90.k_ref, bf16[8,256,256]{2,1,0:T(8,128)(2,1)} %get-tuple-element.94.vt_ref), custom_call_target="tpu_custom_call" | custom-call | flops 1006632960 | bytes 5242880 | tf_op jit(solution)/shard_map/attend/pallas_call | solution.py:202
  75.0 10.9 %feed_first.1 = (f32[6,256,256]{2,1,0:T(8,128)}, bf16[6,1024,256]{2,1,0:T(8,128)(2,1)}, bf16[6,1024,256]{2,1,0:T(8,128)(2,1)}, f32[6,256,256]{2,1,0:T(8,128)}, b...) custom-call(s32[18]{0:T(128)} %pad_add_fusion.table, bf16[8,256,256]{2,1,0:T(8,128)(2,1)} %get-tuple-element.93.xt_ref, ...), custom_call_target="tpu_custom_call" | custom-call | flops 1811939328 | bytes 14680064 | tf_op jit(solution)/shard_map/feed_first/pallas_call | solution.py:345
  85.9 1.1 copy-done.14
  87.0 1.6 swap_inputs.1.a_ref
  88.6 1.0 copy-done.4
  89.6 7.0 %second_projection.1 = (bf16[8,256,256]{2,1,0:T(8,128)(2,1)}, bf16[8,256,256]{2,1,0:T(8,128)(2,1)}, bf16[8,256,256]{2,1,0:T(8,128)(2,1)}, bf16[8,256,256]{2,1,0:T(8,128)(2,1)}, bf16[8,256,256]{2,1,0:T(8,128)(2,1)}) custom-call(bf16[8,256,256]{2,1,0:T(8,128)(2,1)} %copy-done.4, bf16[768,256]{1,0:T(8,128)(2,1)} %copy-done.35), custom_call_target="tpu_custom_call" | custom-call | flops 805306368 | bytes 6291456 | tf_op jit(solution)/shard_map/second_projection/pallas_call | solution.py:133
  96.7 13.6 %attend.3 = (bf16[6,256,256]{2,1,0:T(8,128)(2,1)}, f32[6,2,8,256]{3,2,1,0:T(8,128)}) custom-call(s32[18]{0:T(128)} %pad_add_fusion.table, bf16[8,256,256]{2,1,0:T(8,128)(2,1)} %get-tuple-element.100.q_ref, bf16[8,256,256]{2,1,0:T(8,128)(2,1)} %get-tuple-element.101.k_ref, bf16[8,256,256]{2,1,0:T(8,128)(2,1)} %get-tuple-element.105.vt_ref), custom_call_target="tpu_custom_call" | custom-call | flops 1006632960 | bytes 5242880 | tf_op jit(solution)/shard_map/attend/pallas_call | solution.py:202
  110.3 18.1 %feed_second.1 = (bf16[6,256,256]{2,1,0:T(8,128)(2,1)}, f32[6,8,256]{2,1,0:T(8,128)}, f32[6,256,256]{2,1,0:T(8,128)}, bf16[6,256,256]{2,1,0:T(8,128)(2,1)}, f32[...) custom-call(f32[6,256,256]{2,1,0:T(8,128)} %get-tuple-element.104.z_ref, ...), custom_call_target="tpu_custom_call" | custom-call | flops 5435817984 | bytes 12582912 | tf_op jit(solution)/shard_map/feed_second/pallas_call | solution.py:419
  128.3 22.3 %attend_back.2 = (bf16[6,256,256]{2,1,0:T(8,128)(2,1)}, bf16[8,256,256]{2,1,0:T(8,128)(2,1)}, bf16[8,256,256]{2,1,0:T(8,128)(2,1)}) custom-call(s32[18]{0:T(128)} %pad_add_fusion.table, bf16[8,256,256]{2,1,0:T(8,128)(2,1)} %get-tuple-element.100.q_ref, bf16[8,256,256]{2,1,0:T(8,128)(2,1)} %get-tuple-element.101.k_ref, ...), custom_call_target="tpu_custom_call" | custom-call | flops 2516582400 | bytes 8388608 | tf_op jit(solution)/shard_map/attend_back/pallas_call | solution.py:280
  150.6 1.2 copy-done.5
  151.8 1.2 copy-done.6
  153.0 2.1 swap_grads.2
  155.2 0.9 copy-done.29
  156.0 0.9 copy-done.30
  156.9 19.2 %turn.1 = (f32[6,256,256]{2,1,0:T(8,128)}, f32[6,256,256]{2,1,0:T(8,128)}, bf16[6,256,256]{2,1,0:T(8,128)(2,1)}, f32[1024,256]{1,0:T(8,128)}, f32[256,1024]{1,0:...) custom-call(s32[18]{0:T(128)} %pad_add_fusion.table, ...), custom_call_target="tpu_custom_call" | custom-call | flops 6039797760 | bytes 20971520 | tf_op jit(solution)/shard_map/turn/pallas_call | solution.py:502
  176.1 22.0 %attend_back.3 = (bf16[6,256,256]{2,1,0:T(8,128)(2,1)}, bf16[8,256,256]{2,1,0:T(8,128)(2,1)}, bf16[8,256,256]{2,1,0:T(8,128)(2,1)}) custom-call(s32[18]{0:T(128)} %pad_add_fusion.table, bf16[8,256,256]{2,1,0:T(8,128)(2,1)} %get-tuple-element.89.q_ref, bf16[8,256,256]{2,1,0:T(8,128)(2,1)} %get-tuple-element.90.k_ref, ...), custom_call_target="tpu_custom_call" | custom-call | flops 2516582400 | bytes 8388608 | tf_op jit(solution)/shard_map/attend_back/pallas_call | solution.py:280
  198.2 1.2 copy-done.7
  199.4 1.2 copy-done.8
  200.6 2.1 swap_grads.3
  202.7 0.9 copy-done.12
  203.6 0.9 copy-done.13
  204.5 9.1 %last.1 = (bf16[6,256,256]{2,1,0:T(8,128)(2,1)}, f32[3,256,256]{2,1,0:T(8,128)}, f32[512,128]{1,0:T(8,128)}) custom-call(s32[18]{0:T(128)} %pad_add_fusion.table, bf16[6,256,256]{2,1,0:T(8,128)(2,1)} %get-tuple-element.129.dq_ref, bf16[6,256,256]{2,1,0:T(8,128)(2,1)} %copy-done.12, bf16[6,256,256]{2,1,0:T(8,128)(2,1)} %copy-done.13, ...), custom_call_target="tpu_custom_call" | custom-call | flops 1207959552 | bytes 10485760 | tf_op jit(solution)/shard_map/last/pallas_call | solution.py:544
  213.7 1.1 copy-done.19
  214.8 0.9 copy-done.22
  216.3 1.1 copy-done.1
  217.4 43.1 %leave.1 = (bf16[3,4,8,32,256]{4,3,2,1,0:T(8,128)(2,1)S(1)}, f32[24,128]{1,0:T(8,128)S(1)}, bf16[6,256,256]{2,1,0:T(8,128)(2,1)S(1)}, bf16[6,256,256]{2,1,0:T(8,128)(2,1)S(1)}) custom-call(bf16[3,4,8,32,256]{4,3,2,1,0:T(8,128)(2,1)} %bitcast.12, f32[24,128]{1,0:T(8,128)S(1)} %get-tuple-element.148.pp_ref, bf16[6,256,256]{2,1,0:T(8,128)(2,1)S(1)} %copy-done.17, ...), custom_call_target="tpu_custom_call" | custom-call | flops 1 | bytes 20971520 | tf_op jit(solution)/shard_map/leave/pallas_call | solution.py:1070
  260.5 1.2 copy-done.2
  262.3 1.3 convert_element_type.6
  263.6 1.3 convert_element_type.7
  264.9 9.4 %adam.1 = (f32[4096,128]{1,0:T(8,128)}, f32[4096,128]{1,0:T(8,128)}, f32[4096,128]{1,0:T(8,128)}) custom-call(s32[7]{0:T(128)} %owner_ref.3, bf16[12,256,256]{2,1,0:T(8,128)(2,1)} %bitcast.14, f32[24,128]{1,0:T(8,128)} %copy-done.25, f32[4096,128]{1,0:T(8,128)} %bitcast.16, f32[4096,128]{1,0:T(8,128)} %bitcast.17, f32[4096,128]{1,0:T(8,128)} %bitcast.10), custom_call_target="tpu_custom_call" | custom-call | flops 10485760 | bytes 14680064 | tf_op jit(solution)/shard_map/adam/pallas_call | solution.py:1168
  (54 shorter events, 1.9 us)
Async XLA Ops:
  1.2 1.6 copy-start
  2.8 0.7 copy-start.26
  3.5 1.1 copy-start.15
  3.5 1.4 copy-start.16
  43.4 1.0 copy-start.27
  44.3 0.9 copy-start.28
  46.1 1.1 copy-start.3
  47.1 0.8 copy-start.20
  47.9 0.8 copy-start.31
  48.7 0.8 copy-start.32
  49.5 0.8 copy-start.33
  50.3 0.8 copy-start.34
  51.1 0.7 copy-start.35
  51.9 0.7 copy-start.36
  52.5 0.6 copy-start.37
  85.9 1.1 copy-start.14
  88.6 1.0 copy-start.4
  150.6 1.2 copy-start.5
  151.8 1.2 copy-start.6
  155.2 0.9 copy-start.29
  156.0 0.9 copy-start.30
  198.2 1.2 copy-start.7
  199.4 1.2 copy-start.8
  202.7 0.9 copy-start.12
  203.6 0.9 copy-start.13
  204.5 9.1 %copy-start.9 = (f32[1024,256]{1,0:T(8,128)S(1)}, f32[1024,256]{1,0:T(8,128)}, u32[]{:S(2)}) copy-start(f32[1024,256]{1,0:T(8,128)} %get-tuple-element.142.gd_ref) | copy-start | bytes 3145732
  204.5 9.1 %copy-start.10 = (f32[256,1024]{1,0:T(8,128)S(1)}, f32[256,1024]{1,0:T(8,128)}, u32[]{:S(2)}) copy-start(f32[256,1024]{1,0:T(8,128)} %get-tuple-element.141.gu_ref) | copy-start | bytes 3145732
  204.5 9.1 %copy-start.11 = (f32[1792,128]{1,0:T(8,128)S(1)}, f32[1792,128]{1,0:T(8,128)}, u32[]{:S(2)}) copy-start(f32[1792,128]{1,0:T(8,128)} %get-tuple-element.144.tail_ref) | copy-start | bytes 2752516
  204.5 9.2 %copy-start.21 = (f32[256,256]{1,0:T(8,128)S(1)}, f32[256,256]{1,0:T(8,128)}, u32[]{:S(2)}) copy-start(f32[256,256]{1,0:T(8,128)} %get-tuple-element.140.go_ref) | copy-start | bytes 786436
  204.5 9.2 %copy-start.23 = (f32[6,8,256]{2,1,0:T(8,128)S(1)}, f32[6,8,256]{2,1,0:T(8,128)}, u32[]{:S(2)}) copy-start(f32[6,8,256]{2,1,0:T(8,128)} %get-tuple-element.145.sq1_ref) | copy-start | bytes 147460
  204.5 9.2 %copy-start.24 = (f32[6,8,256]{2,1,0:T(8,128)S(1)}, f32[6,8,256]{2,1,0:T(8,128)}, u32[]{:S(2)}) copy-start(f32[6,8,256]{2,1,0:T(8,128)} %get-tuple-element.146.sq2_ref) | copy-start | bytes 147460
  213.7 1.1 copy-start.19
  214.8 0.9 copy-start.22
  215.7 1.6 copy-start.17
  215.7 1.6 copy-start.18
  216.2 1.1 copy-start.1
  260.5 1.2 copy-start.2
  261.6 3.2 %copy-start.25 = (f32[24,128]{1,0:T(8,128)}, f32[24,128]{1,0:T(8,128)S(1)}, u32[]{:S(2)}) copy-start(f32[24,128]{1,0:T(8,128)S(1)} %get-tuple-element.153.p_ref) | copy-start | bytes 36868

commit v2 on v1

--- a/solution.py
+++ b/solution.py
@@ -83,63 +83,40 @@
     return pl.CostEstimate(flops=int(flops), bytes_accessed=int(nbytes), transcendentals=int(trans))
 
 
-def project(a, wt_ref, q_ref, kt_ref, vt_ref, k_ref, v_ref):
-    q_ref[0] = (dot(wt_ref[0:D], a) * HD ** (-0.5)).astype(BF16)
+LOG2E = math.log2(math.e)
+VROWS = HD + 16
+
+
+def unit_place(unit, core):
+    place = jnp.where(unit < OWN, unit, jnp.where(unit == OWN, core, 3 - core))
+    base = jnp.where(unit < OWN, 0, OWN)
+    return place, base
+
+
+def lanes(start, size):
+    return pl.ds(pl.multiple_of(start, BLK), size)
+
+
+def matrix(w_ref, kind, part):
+    n, rows = w_ref.shape[2:4]
+    if rows % 16 == 0:
+        return w_ref[kind, part].reshape(D, D)
+    return jnp.concatenate([w_ref[kind, part, i] for i in range(n)], axis=0)
+
+
+def project(j, a, wt_ref, q_ref, kt_ref, vt_ref, k_ref, v_ref):
+    where = lanes(j * BLK, BLK)
+    q_ref[j] = (dot(wt_ref[0:D], a) * HD ** (-0.5)).astype(BF16)
     kt = dot(wt_ref[D : 2 * D], a).astype(BF16)
-    kt_ref[0] = kt
-    k_ref[0] = kt.T
     vt = dot(wt_ref[2 * D : 3 * D], a).astype(BF16)
-    vt_ref[0] = vt
-    v_ref[0] = vt.T
-
-
-def first_body(x_ref, small_ref, wt_ref, xt_ref, a_ref, q_ref, kt_ref, vt_ref, k_ref, v_ref):
-    xt = x_ref[0].T
-    xt_ref[0] = xt
-    unit_values, _ = standardize(xt.astype(F32))
-    a = (unit_values * param(small_ref, 0) + param(small_ref, 1)).astype(BF16)
-    a_ref[0] = a
-    project(a, wt_ref, q_ref, kt_ref, vt_ref, k_ref, v_ref)
-
-
-def second_body(a_ref, wt_ref, q_ref, kt_ref, vt_ref, k_ref, v_ref):
-    project(a_ref[0], wt_ref, q_ref, kt_ref, vt_ref, k_ref, v_ref)
-
-
-def tile_spec(blocks=None):
-    if blocks is None:
-        return pl.BlockSpec((1, BLK, BLK), lambda j, *t: (j, 0, 0))
-    return blocks
-
-
-def first_projection(x, small, wt):
-    tile = pl.BlockSpec((1, BLK, BLK), lambda j: (j, 0, 0))
-    out = jax.ShapeDtypeStruct((ALL, BLK, BLK), BF16)
-    return pl.pallas_call(
-        first_body,
-        grid=(ALL,),
-        in_specs=[tile, full(small.shape), full(wt.shape)],
-        out_specs=[tile] * 7,
-        out_shape=[out] * 7,
-        compiler_params=params_of(),
-        cost_estimate=cost(2 * 2048 * 256 * 768, 9 << 20),
-        name="first_projection",
-    )(x, small, wt)
-
-
-def second_projection(a, wt):
-    tile = pl.BlockSpec((1, BLK, BLK), lambda j: (j, 0, 0))
-    out = jax.ShapeDtypeStruct((ALL, BLK, BLK), BF16)
-    return pl.pallas_call(
-        second_body,
-        grid=(ALL,),
-        in_specs=[tile, full(wt.shape)],
-        out_specs=[tile] * 5,
-        out_shape=[out] * 5,
-        compiler_params=params_of(),
-        cost_estimate=cost(2 * 2048 * 256 * 768, 6 << 20),
-        name="second_projection",
-    )(a, wt)
+    for h in range(HEADS):
+        kt_ref[h, :, where] = kt[h * HD : (h + 1) * HD]
+        vt_ref[h, 0:HD, where] = vt[h * HD : (h + 1) * HD]
+    k = kt.T
+    v = vt.T
+    for h in range(2):
+        k_ref[h, j] = k[:, h * 128 : (h + 1) * 128]
+        v_ref[h, j] = v[:, h * 128 : (h + 1) * 128]
 
 
 def head_rows(values, half):
@@ -148,219 +125,230 @@
     return jnp.where(keep, values, jnp.zeros_like(values))
 
 
-def causal_mask():
+def set_mask(mask_ref):
     keys = lax.broadcasted_iota(jnp.int32, (BLK, BLK), 0)
     queries = lax.broadcasted_iota(jnp.int32, (BLK, BLK), 1)
-    return keys <= queries
-
-
-def attend_body(table, q_ref, k_ref, vt_ref, o_ref, log_ref, score_ref):
-    unit = pl.program_id(1)
-    base = table[UNITS + unit]
-    place = table[2 * UNITS + unit]
-
-    def branch(last):
-        for half in range(2):
-            lo, hi = half * HD, (half + 1) * HD
-            q = head_rows(q_ref[0], half)
-            top = None
-            for kb in range(last + 1):
-                score = dot(k_ref[base + kb], q)
-                if kb == last:
-                    score = jnp.where(causal_mask(), score, masked_score)
-                score_ref[half, kb] = score
-                peak = jnp.max(score, axis=0, keepdims=True)
-                top = peak if top is None else jnp.maximum(top, peak)
-            total = jnp.zeros((1, BLK), F32)
-            acc = jnp.zeros((HD, BLK), F32)
-            for kb in range(last + 1):
-                weight = jnp.exp(score_ref[half, kb] - top)
-                total = total + jnp.sum(weight, axis=0, keepdims=True)
-                acc = acc + dot(vt_ref[base + kb, lo:hi, :], weight.astype(BF16))
-            o_ref[0, lo:hi, :] = (acc / total).astype(BF16)
-            log_ref[0, 0, half : half + 1, :] = top + jnp.log(total)
-
-    for last in range(OWN):
-        pl.when(place == last)(partial(branch, last))
-
-
-def attend(table, q, k, vt):
-    spec = pltpu.PrefetchScalarGridSpec(
-        num_scalar_prefetch=1,
-        grid=(2, UNITS),
-        in_specs=[
-            pl.BlockSpec((1, 128, BLK), lambda h, u, t: (t[u], h, 0)),
-            pl.BlockSpec((ALL, BLK, 128), lambda h, u, t: (0, 0, h)),
-            pl.BlockSpec((ALL, 128, BLK), lambda h, u, t: (0, h, 0)),
-        ],
-        out_specs=[
-            pl.BlockSpec((1, 128, BLK), lambda h, u, t: (u, h, 0)),
-            pl.BlockSpec((1, 1, 8, BLK), lambda h, u, t: (u, h, 0, 0)),
-        ],
-        scratch_shapes=[pltpu.VMEM((2, OWN, BLK, BLK), F32)],
-    )
-    return pl.pallas_call(
-        attend_body,
-        grid_spec=spec,
-        out_shape=[
-            jax.ShapeDtypeStruct((UNITS, BLK, BLK), BF16),
-            jax.ShapeDtypeStruct((UNITS, 2, 8, BLK), F32),
-        ],
-        compiler_params=params_of(2),
-        cost_estimate=cost(4 * 4 * 15 * BLK * BLK * HD, 5 << 20, 4 * 15 * BLK * BLK),
-        name="attend",
-    )(table, q, k, vt)
-
-
-def attend_back_body(
-    table, q_ref, k_ref, kt_ref, v_ref, go_ref, o_ref, log_ref, dq_ref, dk_ref, dv_ref, dk_acc, dv_acc
+    mask_ref[...] = jnp.where(keys <= queries, 0.0, masked_score)
+
+
+def groups(values, op):
+    out = values[0:8]
+    for i in range(1, values.shape[0] // 8):
+        out = op(out, values[i * 8 : (i + 1) * 8])
+    return out
+
+
+SUB = 128
+
+
+def attend(core, q_ref, k_ref, vt_ref, o_ref, log_ref, mask_ref, score_ref, prob_ref):
+    def step(i, carry):
+        pair, unit = i // UNITS, i % UNITS
+        place, base = unit_place(unit, core)
+
+        def branch(last):
+            block = q_ref[base + place, lanes(pair * 128, 128), :]
+            for half in range(2):
+                q = head_rows(block, half)
+                top = None
+                for kb in range(last + 1):
+                    for sub in range(BLK // SUB):
+                        rows = slice(sub * SUB, (sub + 1) * SUB)
+                        score = dot(k_ref[pair, base + kb, rows, :], q)
+                        if kb == last:
+                            score = score + mask_ref[rows, :]
+                        score_ref[half, kb, rows, :] = score
+                        peak = groups(score, jnp.maximum)
+                        top = peak if top is None else jnp.maximum(top, peak)
+                top = jnp.max(top, axis=0, keepdims=True)
+                for kb in range(last + 1):
+                    for sub in range(BLK // SUB):
+                        rows = slice(sub * SUB, (sub + 1) * SUB)
+                        weight = jnp.exp(score_ref[half, kb, rows, :] - top)
+                        prob_ref[half, kb * BLK + sub * SUB : kb * BLK + (sub + 1) * SUB, :] = weight.astype(BF16)
+                keys = (last + 1) * BLK
+                out = dot(vt_ref[2 * pair + half, :, lanes(base * BLK, keys)], prob_ref[half, 0:keys, :])
+                total = out[HD : HD + 1]
+                o_ref[unit, pl.ds(pl.multiple_of(pair * 128 + half * HD, HD), HD), :] = (out[0:HD] / total).astype(BF16)
+                log_ref[unit, pair, half : half + 1, :] = top + jnp.log(total)
+
+        for last in range(OWN):
+            pl.when(place == last)(partial(branch, last))
+        return carry
+
+    lax.fori_loop(0, 2 * UNITS, step, 0)
+
+
+def attend_back(
+    core, q_ref, k_ref, kt_ref, v_ref, go_ref, o_ref, log_ref, dq_ref, dk_ref, dv_ref, mask_ref, prob_ref, slope_ref, dk_acc, dv_acc
 ):
-    unit = pl.program_id(1)
-    base = table[UNITS + unit]
-    place = table[2 * UNITS + unit]
-
-    @pl.when(unit == 0)
-    def _():
-        dk_acc[...] = jnp.zeros_like(dk_acc)
-        dv_acc[...] = jnp.zeros_like(dv_acc)
-
-    def branch(last):
-        for half in range(2):
-            lo, hi = half * HD, (half + 1) * HD
-            q = head_rows(q_ref[0], half)
-            go = head_rows(go_ref[0], half)
-            q_head = q_ref[0, lo:hi, :]
-            go_head = go_ref[0, lo:hi, :]
-            log_total = log_ref[0, 0, half : half + 1, :]
-            inner = jnp.sum(
-                go_head.astype(F32) * o_ref[0, lo:hi, :].astype(F32), axis=0, keepdims=True
-            )
-            dq = jnp.zeros((HD, BLK), F32)
-            for kb in range(last + 1):
-                score = dot(k_ref[base + kb], q)
-                if kb == last:
-                    score = jnp.where(causal_mask(), score, masked_score)
-                weight = jnp.exp(score - log_total)
-                slope = dot(v_ref[base + kb], go)
-                dscore = (weight * (slope - inner)).astype(BF16)
-                dv_acc[base + kb, lo:hi, :] += dot_nt(go_head, weight.astype(BF16))
-                dk_acc[base + kb, lo:hi, :] += dot_nt(q_head, dscore)
-                dq = dq + dot(kt_ref[base + kb, lo:hi, :], dscore)
-            dq_ref[0, lo:hi, :] = (dq * HD ** (-0.5)).astype(BF16)
-
-    for last in range(OWN):
-        pl.when(place == last)(partial(branch, last))
-
-    @pl.when(unit == UNITS - 1)
-    def _():
-        dk_ref[...] = dk_acc[...].astype(BF16)
-        dv_ref[...] = dv_acc[...].astype(BF16)
-
-
-def attend_back(table, q, k, kt, v, go, o, log_total):
-    spec = pltpu.PrefetchScalarGridSpec(
-        num_scalar_prefetch=1,
-        grid=(2, UNITS),
-        in_specs=[
-            pl.BlockSpec((1, 128, BLK), lambda h, u, t: (t[u], h, 0)),
-            pl.BlockSpec((ALL, BLK, 128), lambda h, u, t: (0, 0, h)),
-            pl.BlockSpec((ALL, 128, BLK), lambda h, u, t: (0, h, 0)),
-            pl.BlockSpec((ALL, BLK, 128), lambda h, u, t: (0, 0, h)),
-            pl.BlockSpec((1, 128, BLK), lambda h, u, t: (u, h, 0)),
-            pl.BlockSpec((1, 128, BLK), lambda h, u, t: (u, h, 0)),
-            pl.BlockSpec((1, 1, 8, BLK), lambda h, u, t: (u, h, 0, 0)),
-        ],
-        out_specs=[
-            pl.BlockSpec((1, 128, BLK), lambda h, u, t: (u, h, 0)),
-            pl.BlockSpec((ALL, 128, BLK), lambda h, u, t: (0, h, 0)),
-            pl.BlockSpec((ALL, 128, BLK), lambda h, u, t: (0, h, 0)),
-        ],
-        scratch_shapes=[pltpu.VMEM((ALL, 128, BLK), F32)] * 2,
-    )
-    return pl.pallas_call(
-        attend_back_body,
-        grid_spec=spec,
-        out_shape=[
-            jax.ShapeDtypeStruct((UNITS, BLK, BLK), BF16),
-            jax.ShapeDtypeStruct((ALL, BLK, BLK), BF16),
-            jax.ShapeDtypeStruct((ALL, BLK, BLK), BF16),
-        ],
-        compiler_params=params_of(2),
-        cost_estimate=cost(10 * 4 * 15 * BLK * BLK * HD, 8 << 20, 4 * 15 * BLK * BLK),
-        name="attend_back",
-    )(table, q, k, kt, v, go, o, log_total)
-
-
-def middle(z, o_ref, wot_ref, small_ref):
-    r = z + dot(wot_ref[...], o_ref[0])
+    dk_acc[...] = jnp.zeros_like(dk_acc)
+    dv_acc[...] = jnp.zeros_like(dv_acc)
+
+    def step(i, carry):
+        pair, unit = i // UNITS, i % UNITS
+        place, base = unit_place(unit, core)
+
+        def branch(last):
+            block = q_ref[base + place, lanes(pair * 128, 128), :]
+            go_block = go_ref[unit, lanes(pair * 128, 128), :]
+            o_block = o_ref[unit, lanes(pair * 128, 128), :]
+            keys = (last + 1) * BLK
+            for half in range(2):
+                lo, hi = half * HD, (half + 1) * HD
+                q = head_rows(block, half)
+                go = head_rows(go_block, half)
+                q_head = block[lo:hi]
+                go_head = go_block[lo:hi]
+                log_total = log_ref[unit, pair, half : half + 1, :]
+                inner = jnp.sum(go_head.astype(F32) * o_block[lo:hi].astype(F32), axis=0, keepdims=True)
+                for kb in range(last + 1):
+                    for sub in range(BLK // SUB):
+                        rows = slice(sub * SUB, (sub + 1) * SUB)
+                        to = slice(kb * BLK + sub * SUB, kb * BLK + (sub + 1) * SUB)
+                        score = dot(k_ref[pair, base + kb, rows, :], q)
+                        if kb == last:
+                            score = score + mask_ref[rows, :]
+                        weight = jnp.exp(score - log_total)
+                        slope = dot(v_ref[pair, base + kb, rows, :], go)
+                        prob_ref[half, to, :] = weight.astype(BF16)
+                        slope_ref[half, to, :] = (weight * (slope - inner)).astype(BF16)
+                head = 2 * pair + half
+                where = lanes(base * BLK, keys)
+                dv_acc[head, :, where] += dot_nt(go_head, prob_ref[half, 0:keys, :])
+                dk_acc[head, :, where] += dot_nt(q_head, slope_ref[half, 0:keys, :])
+                dq = dot(kt_ref[head, :, where], slope_ref[half, 0:keys, :])
+                dq_ref[unit, pl.ds(pl.multiple_of(pair * 128 + lo, HD), HD), :] = (dq * HD ** (-0.5)).astype(BF16)
+
+        for last in range(OWN):
+            pl.when(place == last)(partial(branch, last))
+        return carry
+
+    lax.fori_loop(0, 2 * UNITS, step, 0)
+    for j in range(ALL):
+        for ref, acc in ((dk_ref, dk_acc), (dv_ref, dv_acc)):
+            ref[j] = acc[:, :, j * BLK : (j + 1) * BLK].reshape(D, BLK).astype(BF16)
+
+
+def forward_parts(z, o, wot_ref, small_ref):
+    r = z + dot(wot_ref[...], o)
     unit_values, inverse = standardize(r)
     m = (unit_values * param(small_ref, 2) + param(small_ref, 3)).astype(BF16)
     return r, unit_values, inverse, m
 
 
-def feed_first_body(
-    table, xt_ref, o_ref, small_ref, wot_ref, wut_ref, wdt_ref, r_ref, hid_ref, slope_ref, z_ref, a_ref, sq_ref
+def squares_of(out):
+    return groups(out * out, jnp.add)
+
+
+def first_stage_body(
+    x_ref, w_ref, p_ref,
+    xt_ref, a_ref, q_ref, kt_ref, k_ref, v_ref, o_ref, log_ref, r_ref, hid_ref, slope_ref, z_ref, a2_ref, sq_ref,
+    wt_ref, wot_ref, wut_ref, wdt_ref, small_ref, vt_ref, mask_ref, score_ref, prob_ref,
 ):
-    x = xt_ref[0].astype(F32)
-    r, _, _, m = middle(x, o_ref, wot_ref, small_ref)
-    r_ref[0] = r
-    out = r + param(small_ref, 4)
-    for c in range(FF // BLK):
-        rows = slice(c * BLK, (c + 1) * BLK)
-        e = dot(wut_ref[rows, :], m) + param(small_ref, 5 + c)
-        hid, slope = gelu_parts(e)
-        hid = hid.astype(BF16)
-        hid_ref[0, rows, :] = hid
-        slope_ref[0, rows, :] = slope.astype(BF16)
-        out = out + dot(wdt_ref[:, rows], hid)
-    sq_ref[0] = jnp.broadcast_to(jnp.sum(out * out, axis=0, keepdims=True), (8, BLK))
-    z = out + x
-    z_ref[0] = z
-    unit_values, _ = standardize(z)
-    a_ref[0] = (unit_values * param(small_ref, 0) + param(small_ref, 1)).astype(BF16)
-
-
-def feed_first(table, xt, o, small, wot, wut, wdt):
-    spec = pltpu.PrefetchScalarGridSpec(
-        num_scalar_prefetch=1,
-        grid=(UNITS,),
-        in_specs=[
-            pl.BlockSpec((1, BLK, BLK), lambda u, t: (t[u], 0, 0)),
-            pl.BlockSpec((1, BLK, BLK), lambda u, t: (u, 0, 0)),
-            full(small.shape),
-            full(wot.shape),
-            full(wut.shape),
-            full(wdt.shape),
-        ],
-        out_specs=[
-            pl.BlockSpec((1, BLK, BLK), lambda u, t: (u, 0, 0)),
-            pl.BlockSpec((1, FF, BLK), lambda u, t: (u, 0, 0)),
-            pl.BlockSpec((1, FF, BLK), lambda u, t: (u, 0, 0)),
-            pl.BlockSpec((1, BLK, BLK), lambda u, t: (u, 0, 0)),
-            pl.BlockSpec((1, BLK, BLK), lambda u, t: (u, 0, 0)),
-            pl.BlockSpec((1, 8, BLK), lambda u, t: (u, 0, 0)),
-        ],
-    )
-    tile = (UNITS, BLK, BLK)
+    core = lax.axis_index("seq") % 2
+    for t in range(3):
+        wt_ref[t * D : (t + 1) * D, :] = matrix(w_ref, 0, t).T
+    for row in range(SMALL):
+        for side in range(2):
+            line = jnp.broadcast_to(p_ref[2 * row + side : 2 * row + side + 1, :], (128, 128))
+            small_ref[row * D + side * 128 : row * D + (side + 1) * 128, :] = line.T
+    set_mask(mask_ref)
+    vt_ref[:, HD:, :] = jnp.ones((HEADS, VROWS - HD, ALL * BLK), BF16)
+
+    def begin(j, carry):
+        xt = x_ref[j].T
+        xt_ref[j] = xt
+        unit_values, _ = standardize(xt.astype(F32))
+        a = (unit_values * param(small_ref, 0) + param(small_ref, 1)).astype(BF16)
+        a_ref[j] = a
+        project(j, a, wt_ref, q_ref, kt_ref, vt_ref, k_ref, v_ref)
+        return carry
+
+    lax.fori_loop(0, ALL, begin, 0)
+    attend(core, q_ref, k_ref, vt_ref, o_ref, log_ref, mask_ref, score_ref, prob_ref)
+    wot_ref[...] = matrix(w_ref, 0, 3).T
+    for c in range(4):
+        part = slice(c * D, (c + 1) * D)
+        wut_ref[part, :] = matrix(w_ref, 1, c).T
+        wdt_ref[:, part] = matrix(w_ref, 2, c).T
+
+    def feed(u, carry):
+        place, base = unit_place(u, core)
+        x = xt_ref[base + place].astype(F32)
+        r, _, _, m = forward_parts(x, o_ref[u], wot_ref, small_ref)
+        r_ref[u] = r
+        out = r + param(small_ref, 4)
+        for c in range(FF // BLK):
+            rows = slice(c * BLK, (c + 1) * BLK)
+            e = dot(wut_ref[rows, :], m) + param(small_ref, 5 + c)
+            hid, slope = gelu_parts(e)
+            hid = hid.astype(BF16)
+            hid_ref[u, rows, :] = hid
+            slope_ref[u, rows, :] = slope.astype(BF16)
+            out = out + dot(wdt_ref[:, rows], hid)
+        sq_ref[u] = squares_of(out)
+        z = out + x
+        z_ref[u] = z
+        unit_values, _ = standardize(z)
+        a2_ref[u] = (unit_values * param(small_ref, 0) + param(small_ref, 1)).astype(BF16)
+        return carry
+
+    lax.fori_loop(0, UNITS, feed, 0)
+
+
+VM = pl.BlockSpec(memory_space=pltpu.VMEM)
+
+
+def shape_of(shape, dtype=BF16):
+    return jax.ShapeDtypeStruct(shape, dtype)
+
+
+KEYS = [
+    shape_of((HEADS, HD, ALL * BLK)),
+    shape_of((2, ALL, BLK, 128)),
+    shape_of((2, ALL, BLK, 128)),
+]
+ATTEND_SCRATCH = [
+    pltpu.VMEM((BLK, BLK), F32),
+    pltpu.VMEM((2, OWN, BLK, BLK), F32),
+    pltpu.VMEM((2, OWN * BLK, BLK), BF16),
+]
+BACK_SCRATCH = [
+    pltpu.VMEM((BLK, BLK), F32),
+    pltpu.VMEM((2, OWN * BLK, BLK), BF16),
+    pltpu.VMEM((2, OWN * BLK, BLK), BF16),
+    pltpu.VMEM((HEADS, HD, ALL * BLK), F32),
+    pltpu.VMEM((HEADS, HD, ALL * BLK), F32),
+]
+
+
+def stage_call(body, name, args, outs, scratch, mib, flops):
     return pl.pallas_call(
-        feed_first_body,
-        grid_spec=spec,
-        out_shape=[
-            jax.ShapeDtypeStruct(tile, F32),
-            jax.ShapeDtypeStruct((UNITS, FF, BLK), BF16),
-            jax.ShapeDtypeStruct((UNITS, FF, BLK), BF16),
-            jax.ShapeDtypeStruct(tile, F32),
-            jax.ShapeDtypeStruct(tile, BF16),
-            jax.ShapeDtypeStruct((UNITS, 8, BLK), F32),
-        ],
-        compiler_params=params_of(),
-        cost_estimate=cost(2 * 1536 * 256 * 2304, 14 << 20),
-        name="feed_first",
-    )(table, xt, o, small, wot, wut, wdt)
+        body,
+        in_specs=[VM] * len(args),
+        out_specs=[VM] * len(outs),
+        out_shape=outs,
+        scratch_shapes=scratch,
+        compiler_params=pltpu.CompilerParams(vmem_limit_bytes=mib << 20),
+        cost_estimate=cost(flops, 1 << 20),
+        name=name,
+    )(*args)
+
+
+def first_stage(x, w, p):
+    tile, eight = (UNITS, BLK, BLK), (ALL, BLK, BLK)
+    outs = [shape_of(eight), shape_of(eight), shape_of(eight)] + KEYS
+    outs += [shape_of(tile), shape_of((UNITS, 2, 8, BLK), F32), shape_of(tile, F32)]
+    outs += [shape_of((UNITS, FF, BLK)), shape_of((UNITS, FF, BLK)), shape_of(tile, F32), shape_of(tile)]
+    outs += [shape_of((UNITS, 8, BLK), F32), shape_of((3 * D, D)), shape_of((D, D)), shape_of((FF, D))]
+    outs += [shape_of((D, FF)), shape_of((SMALL * D, 128), F32)]
+    scratch = [pltpu.VMEM((HEADS, VROWS, ALL * BLK), BF16)] + ATTEND_SCRATCH
+    return stage_call(first_stage_body, "first_stage", [x, w, p], outs, scratch, FIRST_MIB, 8e9)
 
 
 def feed_back_tail(
-    g, gy, r_unit, r_inv, m, o, small_ref, parts, wu_ref, wd_ref, wo_ref, gr_ref, go_ref, gd_acc, gu_acc, go_acc, tail_acc
+    u, g, gy, r_unit, r_inv, m, o, small_ref, parts, w_ref, gr_ref, go_ref, gd_acc, gu_acc, go_acc, tail_acc
 ):
     tail_acc[2 * D : 3 * D, :] += fold(gy.astype(F32))
     gm = jnp.zeros((D, BLK), F32)
@@ -368,87 +356,84 @@
         rows = slice(c * BLK, (c + 1) * BLK)
         hid, slope = parts(c)
         gd_acc[rows, :] += dot_nt(hid, gy)
-        ge = (dot(wd_ref[rows, :], gy) * slope).astype(BF16)
+        ge = (dot(matrix(w_ref, 2, c), gy) * slope).astype(BF16)
         gu_acc[:, rows] += dot_nt(m, ge)
         tail_acc[3 * D + c * BLK : 3 * D + (c + 1) * BLK, :] += fold(ge.astype(F32))
-        gm = gm + dot(wu_ref[:, rows], ge)
+        gm = gm + dot(matrix(w_ref, 1, c), ge)
     tail_acc[0:D, :] += fold(gm * r_unit)
     tail_acc[D : 2 * D, :] += fold(gm)
     gr = g + standardize_back(gm * param(small_ref, 2), r_unit, r_inv)
-    gr_ref[0] = gr
+    gr_ref[u] = gr
     ga = gr.astype(BF16)
     go_acc[...] += dot_nt(o, ga)
-    go_ref[0] = dot(wo_ref[...], ga).astype(BF16)
-
-
-def feed_second_body(
-    z_ref, o_ref, cot_ref, small_ref, wot_ref, wut_ref, wdt_ref, wo_ref, wu_ref, wd_ref,
-    final_ref, sq_ref, gr_ref, go_ref, gd_acc, gu_acc, go_acc, tail_acc, hid_buf, slope_buf,
+    go_ref[u] = dot(matrix(w_ref, 0, 3), ga).astype(BF16)
+
+
+TAIL = 3 * D + FF
+
+
+def second_stage_body(
+    a_ref, z_ref, cot_ref, w_ref, wt_ref, wot_ref, wut_ref, wdt_ref, small_ref,
+    final_ref, sq_ref, gr_ref, gd_acc, gu_acc, go_acc, tail_acc, dq_ref, dk_ref, dv_ref,
+    q_ref, kt_ref, k_ref, v_ref, vt_ref, o_ref, log_ref, go_ref, score_ref, hid_buf, slope_buf,
+    mask_ref, prob_ref, ds_ref, dk_acc, dv_acc,
 ):
-    @pl.when(pl.program_id(0) == 0)
-    def _():
-        for acc in (gd_acc, gu_acc, go_acc, tail_acc):
-            acc[...] = jnp.zeros_like(acc)
-
-    r, r_unit, r_inv, m = middle(z_ref[0], o_ref, wot_ref, small_ref)
-    out = r + param(small_ref, 4)
-    for c in range(FF // BLK):
-        rows = slice(c * BLK, (c + 1) * BLK)
-        e = dot(wut_ref[rows, :], m) + param(small_ref, 5 + c)
-        hid, slope = gelu_parts(e)
-        hid = hid.astype(BF16)
-        hid_buf[rows, :] = hid
-        slope_buf[rows, :] = slope
-        out = out + dot(wdt_ref[:, rows], hid)
-    sq_ref[0] = jnp.broadcast_to(jnp.sum(out * out, axis=0, keepdims=True), (8, BLK))
-    final_ref[0] = out.T.astype(BF16)
-    gy = cot_ref[0].T
-    feed_back_tail(
-        gy.astype(F32), gy, r_unit, r_inv, m, o_ref[0], small_ref,
-        lambda c: (hid_buf[c * BLK : (c + 1) * BLK, :], slope_buf[c * BLK : (c + 1) * BLK, :]),
-        wu_ref, wd_ref, wo_ref, gr_ref, go_ref, gd_acc, gu_acc, go_acc, tail_acc,
+    core = lax.axis_index("seq") % 2
+    set_mask(mask_ref)
+    vt_ref[:, HD:, :] = jnp.ones((HEADS, VROWS - HD, ALL * BLK), BF16)
+    for acc in (gd_acc, gu_acc, go_acc, tail_acc):
+        acc[...] = jnp.zeros_like(acc)
+
+    def begin(j, carry):
+        project(j, a_ref[j], wt_ref, q_ref, kt_ref, vt_ref, k_ref, v_ref)
+        return carry
+
+    lax.fori_loop(0, ALL, begin, 0)
+    attend(core, q_ref, k_ref, vt_ref, o_ref, log_ref, mask_ref, score_ref, prob_ref)
+
+    def feed(u, carry):
+        r, r_unit, r_inv, m = forward_parts(z_ref[u], o_ref[u], wot_ref, small_ref)
+        out = r + param(small_ref, 4)
+        for c in range(FF // BLK):
+            rows = slice(c * BLK, (c + 1) * BLK)
+            e = dot(wut_ref[rows, :], m) + param(small_ref, 5 + c)
+            hid, slope = gelu_parts(e)
+            hid = hid.astype(BF16)
+            hid_buf[rows, :] = hid
+            slope_buf[rows, :] = slope
+            out = out + dot(wdt_ref[:, rows], hid)
+        sq_ref[u] = squares_of(out)
+        final_ref[u] = out.T.astype(BF16)
+        gy = cot_ref[u].T
+        feed_back_tail(
+            u, gy.astype(F32), gy, r_unit, r_inv, m, o_ref[u], small_ref,
+            lambda c: (hid_buf[c * BLK : (c + 1) * BLK, :], slope_buf[c * BLK : (c + 1) * BLK, :]),
+            w_ref, gr_ref, go_ref, gd_acc, gu_acc, go_acc, tail_acc,
+        )
+        return carry
+
+    lax.fori_loop(0, UNITS, feed, 0)
+    attend_back(
+        core, q_ref, k_ref, kt_ref, v_ref, go_ref, o_ref, log_ref, dq_ref, dk_ref, dv_ref, mask_ref, prob_ref, ds_ref, dk_acc, dv_acc
     )
 
 
-TAIL = 3 * D + FF
-
-
-def feed_second(z, o, cot, small, wot, wut, wdt, wo, wu, wd):
-    tile = pl.BlockSpec((1, BLK, BLK), lambda u: (u, 0, 0))
-    whole = lambda shape: pl.BlockSpec(shape, lambda u: (0,) * len(shape))
-    return pl.pallas_call(
-        feed_second_body,
-        grid=(UNITS,),
-        in_specs=[tile, tile, tile] + [full(w.shape) for w in (small, wot, wut, wdt, wo, wu, wd)],
-        out_specs=[
-            tile,
-            pl.BlockSpec((1, 8, BLK), lambda u: (u, 0, 0)),
-            tile,
-            tile,
-            whole((FF, D)),
-            whole((D, FF)),
-            whole((D, D)),
-            whole((TAIL, 128)),
-        ],
-        out_shape=[
-            jax.ShapeDtypeStruct((UNITS, BLK, BLK), BF16),
-            jax.ShapeDtypeStruct((UNITS, 8, BLK), F32),
-            jax.ShapeDtypeStruct((UNITS, BLK, BLK), F32),
-            jax.ShapeDtypeStruct((UNITS, BLK, BLK), BF16),
-            jax.ShapeDtypeStruct((FF, D), F32),
-            jax.ShapeDtypeStruct((D, FF), F32),
-            jax.ShapeDtypeStruct((D, D), F32),
-            jax.ShapeDtypeStruct((TAIL, 128), F32),
-        ],
-        scratch_shapes=[pltpu.VMEM((FF, BLK), BF16), pltpu.VMEM((FF, BLK), F32)],
-        compiler_params=params_of(),
-        cost_estimate=cost(2 * 1536 * 256 * 2304 * 3, 12 << 20),
-        name="feed_second",
-    )(z, o, cot, small, wot, wut, wdt, wo, wu, wd)
-
-
-def project_back(z, a, dq, dk, dv, gr, small_ref, wqkv_ref, gqkv_acc, head_acc):
-    grad = dot(wqkv_ref[0], dq) + dot(wqkv_ref[1], dk) + dot(wqkv_ref[2], dv)
+def second_stage(a, z, cot, w, wt, wot, wut, wdt, small):
+    tile, eight = (UNITS, BLK, BLK), (ALL, BLK, BLK)
+    outs = [shape_of(tile), shape_of((UNITS, 8, BLK), F32), shape_of(tile, F32), shape_of((FF, D), F32)]
+    outs += [shape_of((D, FF), F32), shape_of((D, D), F32), shape_of((TAIL, 128), F32), shape_of(tile)]
+    outs += [shape_of(eight), shape_of(eight)]
+    scratch = [pltpu.VMEM(eight, BF16)] + [pltpu.VMEM(s.shape, s.dtype) for s in KEYS]
+    scratch += [pltpu.VMEM((HEADS, VROWS, ALL * BLK), BF16), pltpu.VMEM(tile, BF16)]
+    scratch += [pltpu.VMEM((UNITS, 2, 8, BLK), F32), pltpu.VMEM(tile, BF16), ATTEND_SCRATCH[1]]
+    scratch += [pltpu.VMEM((FF, BLK), BF16), pltpu.VMEM((FF, BLK), F32)] + BACK_SCRATCH
+    return stage_call(
+        second_stage_body, "second_stage", [a, z, cot, w, wt, wot, wut, wdt, small], outs, scratch, SECOND_MIB, 20e9
+    )
+
+
+def project_back(z, a, dq, dk, dv, gr, small_ref, w_ref, gqkv_acc, head_acc):
+    grad = dot(matrix(w_ref, 0, 0), dq) + dot(matrix(w_ref, 0, 1), dk) + dot(matrix(w_ref, 0, 2), dv)
     gqkv_acc[0] += dot_nt(a, dq)
     gqkv_acc[1] += dot_nt(a, dk)
     gqkv_acc[2] += dot_nt(a, dv)
@@ -458,136 +443,103 @@
     return gr + standardize_back(grad * param(small_ref, 0), unit_values, inverse)
 
 
-def turn_body(
-    table, dq_ref, dk_ref, dv_ref, a_ref, z_ref, gr_ref, hid_ref, slope_ref, r_ref, o_ref, small_ref, wqkv_ref,
-    wo_ref, wu_ref, wd_ref, gd_in, gu_in, go_in, tail_in,
-    gz_ref, gr_out, go_out, gd_acc, gu_acc, go_acc, tail_acc, gqkv_acc, head_acc,
+def third_stage_body(
+    dq_in, dk_in, dv_in, a2_ref, z_ref, gr_in, hid_ref, slope_ref, r_ref, o_ref, log_ref, q_ref, kt_ref, k_ref, v_ref,
+    small_ref, w_ref, gd_in, gu_in, go_in, tail_in,
+    gz_ref, gr_ref, gd_acc, gu_acc, go_acc, tail_acc, gqkv_acc, head_acc, dq_ref, dk_ref, dv_ref,
+    go_ref, mask_ref, prob_ref, ds_ref, dk_acc, dv_acc,
 ):
-    @pl.when(pl.program_id(0) == 0)
-    def _():
-        gd_acc[...] = gd_in[...]
-        gu_acc[...] = gu_in[...]
-        go_acc[...] = go_in[...]
-        tail_acc[...] = tail_in[...]
-        gqkv_acc[...] = jnp.zeros_like(gqkv_acc)
-        head_acc[...] = jnp.zeros_like(head_acc)
-
-    g = project_back(
-        z_ref[0], a_ref[0], dq_ref[0], dk_ref[0], dv_ref[0], gr_ref[0], small_ref, wqkv_ref, gqkv_acc, head_acc
+    core = lax.axis_index("seq") % 2
+    set_mask(mask_ref)
+    gqkv_acc[...] = jnp.zeros_like(gqkv_acc)
+    head_acc[...] = jnp.zeros_like(head_acc)
+    for acc, given in ((gd_acc, gd_in), (gu_acc, gu_in), (go_acc, go_in), (tail_acc, tail_in)):
+        acc[...] = given[...]
+
+    def feed(u, carry):
+        place, base = unit_place(u, core)
+        g = project_back(
+            z_ref[u], a2_ref[base + place], dq_in[u], dk_in[u], dv_in[u], gr_in[u], small_ref, w_ref, gqkv_acc, head_acc
+        )
+        gz_ref[u] = g
+        r_unit, r_inv = standardize(r_ref[u])
+        m = (r_unit * param(small_ref, 2) + param(small_ref, 3)).astype(BF16)
+        feed_back_tail(
+            u, g, g.astype(BF16), r_unit, r_inv, m, o_ref[u], small_ref,
+            lambda c: (hid_ref[u, c * BLK : (c + 1) * BLK, :], slope_ref[u, c * BLK : (c + 1) * BLK, :].astype(F32)),
+            w_ref, gr_ref, go_ref, gd_acc, gu_acc, go_acc, tail_acc,
+        )
+        return carry
+
+    lax.fori_loop(0, UNITS, feed, 0)
+    attend_back(
+        core, q_ref, k_ref, kt_ref, v_ref, go_ref, o_ref, log_ref, dq_ref, dk_ref, dv_ref, mask_ref, prob_ref, ds_ref, dk_acc, dv_acc
     )
-    gz_ref[0] = g
-    r_unit, r_inv = standardize(r_ref[0])
-    m = (r_unit * param(small_ref, 2) + param(small_ref, 3)).astype(BF16)
-    feed_back_tail(
-        g, g.astype(BF16), r_unit, r_inv, m, o_ref[0], small_ref,
-        lambda c: (hid_ref[0, c * BLK : (c + 1) * BLK, :], slope_ref[0, c * BLK : (c + 1) * BLK, :].astype(F32)),
-        wu_ref, wd_ref, wo_ref, gr_out, go_out, gd_acc, gu_acc, go_acc, tail_acc,
-    )
-
-
-def turn(table, dq, dk, dv, a, z, gr, hid, slope, r, o, small, wqkv, wo, wu, wd, gd, gu, go, tail):
-    tile = pl.BlockSpec((1, BLK, BLK), lambda u, t: (u, 0, 0))
-    moved = pl.BlockSpec((1, BLK, BLK), lambda u, t: (t[u], 0, 0))
-    tall = pl.BlockSpec((1, FF, BLK), lambda u, t: (u, 0, 0))
-    whole = lambda shape: pl.BlockSpec(shape, lambda u, t: (0,) * len(shape))
-    spec = pltpu.PrefetchScalarGridSpec(
-        num_scalar_prefetch=1,
-        grid=(UNITS,),
-        in_specs=[tile, tile, tile, moved, tile, tile, tall, tall, tile, tile]
-        + [full(w.shape) for w in (small, wqkv, wo, wu, wd, gd, gu, go, tail)],
-        out_specs=[tile, tile, tile]
-        + [whole(s) for s in ((FF, D), (D, FF), (D, D), (TAIL, 128), (3, D, D), (2 * D, 128))],
-    )
-    shape = (UNITS, BLK, BLK)
-    return pl.pallas_call(
-        turn_body,
-        grid_spec=spec,
-        out_shape=[
-            jax.ShapeDtypeStruct(shape, F32),
-            jax.ShapeDtypeStruct(shape, F32),
-            jax.ShapeDtypeStruct(shape, BF16),
-        ]
-        + [jax.ShapeDtypeStruct(s, F32) for s in ((FF, D), (D, FF), (D, D), (TAIL, 128), (3, D, D), (2 * D, 128))],
-        compiler_params=params_of(),
-        cost_estimate=cost(2 * 1536 * 256 * 3840 * 2, 20 << 20),
-        name="turn",
-    )(table, dq, dk, dv, a, z, gr, hid, slope, r, o, small, wqkv, wo, wu, wd, gd, gu, go, tail)
-
-
-def last_body(
-    table, dq_ref, dk_ref, dv_ref, a_ref, xt_ref, gr_ref, gz_ref, small_ref, wqkv_ref, gqkv_in, head_in,
-    grad_ref, gqkv_acc, head_acc,
+
+
+def third_stage(*args):
+    tile, eight = (UNITS, BLK, BLK), (ALL, BLK, BLK)
+    outs = [shape_of(tile, F32), shape_of(tile, F32), shape_of((FF, D), F32), shape_of((D, FF), F32)]
+    outs += [shape_of((D, D), F32), shape_of((TAIL, 128), F32), shape_of((3, D, D), F32), shape_of((2 * D, 128), F32)]
+    outs += [shape_of(tile), shape_of(eight), shape_of(eight)]
+    scratch = [pltpu.VMEM(tile, BF16)] + BACK_SCRATCH
+    return stage_call(third_stage_body, "third_stage", args, outs, scratch, THIRD_MIB, 16e9)
+
+
+def last_stage_body(
+    n, dq_ref, dk_ref, dv_ref, a_ref, xt_ref, gr_ref, gz_ref, small_ref, w_ref, gqkv_in, head_in,
+    gout_ref, gu_ref, gd_ref, tail_ref, sq1_ref, sq2_ref,
+    grad_ref, g_ref, p_ref, gqkv_acc, head_acc,
 ):
-    @pl.when(pl.program_id(0) == 0)
-    def _():
-        gqkv_acc[...] = gqkv_in[...]
-        head_acc[...] = head_in[...]
-
-    g = project_back(
-        xt_ref[0].astype(F32), a_ref[0], dq_ref[0], dk_ref[0], dv_ref[0], gr_ref[0], small_ref, wqkv_ref,
-        gqkv_acc, head_acc,
-    )
-    grad_ref[0] = (g + gz_ref[0]).T.astype(BF16)
-
-
-def last(table, dq, dk, dv, a, xt, gr, gz, small, wqkv, gqkv, head):
-    tile = pl.BlockSpec((1, BLK, BLK), lambda u, t: (u, 0, 0))
-    moved = pl.BlockSpec((1, BLK, BLK), lambda u, t: (t[u], 0, 0))
-    whole = lambda shape: pl.BlockSpec(shape, lambda u, t: (0,) * len(shape))
-    spec = pltpu.PrefetchScalarGridSpec(
-        num_scalar_prefetch=1,
-        grid=(UNITS,),
-        in_specs=[tile, tile, tile, moved, moved, tile, tile]
-        + [full(w.shape) for w in (small, wqkv, gqkv, head)],
-        out_specs=[tile, whole((3, D, D)), whole((2 * D, 128))],
-    )
-    return pl.pallas_call(
-        last_body,
-        grid_spec=spec,
-        out_shape=[
-            jax.ShapeDtypeStruct((UNITS, BLK, BLK), BF16),
-            jax.ShapeDtypeStruct((3, D, D), F32),
-            jax.ShapeDtypeStruct((2 * D, 128), F32),
-        ],
-        compiler_params=params_of(),
-        cost_estimate=cost(2 * 1536 * 256 * 768 * 2, 10 << 20),
-        name="last",
-    )(table, dq, dk, dv, a, xt, gr, gz, small, wqkv, gqkv, head)
-
-
-def prepare_body(w_ref, p_ref, wt_ref, wot_ref, wut_ref, wdt_ref, wqkv_ref, wo_ref, wu_ref, wd_ref, small_ref):
+    dp = lax.axis_index("dp")
+    seq = lax.axis_index("seq")
+    chip, core = seq // 2, seq % 2
+    gqkv_acc[...] = gqkv_in[...]
+    head_acc[...] = head_in[...]
+
+    def end(u, carry):
+        place, base = unit_place(u, core)
+        g = project_back(
+            xt_ref[base + place].astype(F32), a_ref[base + place], dq_ref[u], dk_ref[u], dv_ref[u], gr_ref[u],
+            small_ref, w_ref, gqkv_acc, head_acc,
+        )
+        grad_ref[u] = (g + gz_ref[u]).T.astype(BF16)
+        return carry
+
+    lax.fori_loop(0, UNITS, end, 0)
+    split = lambda values: values.astype(BF16).reshape(g_ref.shape[2:])
     for t in range(3):
-        matrix = w_ref[0, t]
-        wqkv_ref[t] = matrix
-        wt_ref[t * D : (t + 1) * D, :] = matrix.T
-    matrix = w_ref[0, 3]
-    wo_ref[...] = matrix
-    wot_ref[...] = matrix.T
+        g_ref[0, t] = split(gqkv_acc[t])
+    g_ref[0, 3] = split(gout_ref[...])
     for c in range(4):
-        part = slice(c * D, (c + 1) * D)
-        matrix = w_ref[1, c]
-        wu_ref[:, part] = matrix
-        wut_ref[part, :] = matrix.T
-        matrix = w_ref[2, c]
-        wd_ref[part, :] = matrix
-        wdt_ref[:, part] = matrix.T
+        g_ref[1, c] = split(gu_ref[:, c * D : (c + 1) * D])
+        g_ref[2, c] = split(gd_ref[c * D : (c + 1) * D, :])
     for row in range(SMALL):
         for side in range(2):
-            line = jnp.broadcast_to(p_ref[2 * row + side : 2 * row + side + 1, :], (128, 128))
-            small_ref[row * D + side * 128 : row * D + (side + 1) * 128, :] = line.T
-
-
-def prepare(w, p):
-    shapes = [(3 * D, D), (D, D), (FF, D), (D, FF), (3, D, D), (D, D), (D, FF), (FF, D)]
-    return pl.pallas_call(
-        prepare_body,
-        in_specs=[pl.BlockSpec(memory_space=pltpu.VMEM)] * 2,
-        out_specs=[pl.BlockSpec(memory_space=pltpu.VMEM)] * 9,
-        out_shape=[jax.ShapeDtypeStruct(s, BF16) for s in shapes] + [jax.ShapeDtypeStruct((SMALL * D, 128), F32)],
-        compiler_params=pltpu.CompilerParams(vmem_limit_bytes=40 << 20),
-        cost_estimate=cost(1, 6 << 20),
-        name="prepare",
-    )(w, p)
+            ref, first = (head_acc, row) if row < 2 else (tail_ref, row - 2)
+            first = first * D + side * 128
+            p_ref[2 * row + side : 2 * row + side + 1, :] = jnp.sum(ref[first : first + 128, :].T, axis=0, keepdims=True)
+    sequences = 6 * n
+    place = lax.broadcasted_iota(jnp.int32, (6, 128), 0) * 128 + lax.broadcasted_iota(jnp.int32, (6, 128), 1)
+    stats = jnp.zeros((6, 128), F32)
+    for i, ref in enumerate((sq1_ref, sq2_ref)):
+        lines = [jnp.sum(ref[u], axis=0, keepdims=True) for u in range(UNITS)]
+        own = jnp.sum(lines[0] + lines[1] + lines[2] + lines[3], axis=1, keepdims=True)
+        half = jnp.sum(lines[4] + lines[5], axis=1, keepdims=True)
+        start = i * sequences + 6 * dp + 3 * chip
+        stats = jnp.where(place == start + core, jnp.broadcast_to(own, (6, 128)), stats)
+        stats = jnp.where(place == start + 2, jnp.broadcast_to(half, (6, 128)), stats)
+    p_ref[18:24, :] = stats
+
+
+def last_stage(n, *args):
+    rows = D // n
+    outs = [shape_of((UNITS, BLK, BLK)), shape_of((3, 4, n, rows, D)), shape_of((24, 128), F32)]
+    scratch = [pltpu.VMEM((3, D, D), F32), pltpu.VMEM((2 * D, 128), F32)]
+    return stage_call(partial(last_stage_body, n), "last_stage", args, outs, scratch, LAST_MIB, 3e9)
+
+
+FIRST_MIB, SECOND_MIB, THIRD_MIB, LAST_MIB = 14, 24, 14, 8
 
 
 def owner_scalars(owner_ref):
@@ -890,47 +842,6 @@
         cost_estimate=cost(1, 4 << 20),
         name="swap_grads",
     )(dk, dv)
-
-
-def collect_body(n, gqkv_ref, go_ref, gu_ref, gd_ref, head_ref, tail_ref, sq1_ref, sq2_ref, g_ref, p_ref):
-    dp = lax.axis_index("dp")
-    seq = lax.axis_index("seq")
-    chip, core = seq // 2, seq % 2
-    for t in range(3):
-        g_ref[0, t] = gqkv_ref[t].astype(BF16)
-    g_ref[0, 3] = go_ref[...].astype(BF16)
-    for c in range(4):
-        g_ref[1, c] = gu_ref[:, c * D : (c + 1) * D].astype(BF16)
-        g_ref[2, c] = gd_ref[c * D : (c + 1) * D, :].astype(BF16)
-    for row in range(SMALL):
-        for side in range(2):
-            ref, first = (head_ref, row) if row < 2 else (tail_ref, row - 2)
-            first = first * D + side * 128
-            p_ref[2 * row + side : 2 * row + side + 1, :] = jnp.sum(ref[first : first + 128, :].T, axis=0, keepdims=True)
-    sequences = 6 * n
-    place = lax.broadcasted_iota(jnp.int32, (6, 128), 0) * 128 + lax.broadcasted_iota(jnp.int32, (6, 128), 1)
-    stats = jnp.zeros((6, 128), F32)
-    for i, ref in enumerate((sq1_ref, sq2_ref)):
-        lines = [ref[u, 0:1, :] for u in range(UNITS)]
-        own = jnp.sum(lines[0] + lines[1] + lines[2] + lines[3], axis=1, keepdims=True)
-        half = jnp.sum(lines[4] + lines[5], axis=1, keepdims=True)
-        start = i * sequences + 6 * dp + 3 * chip
-        stats = jnp.where(place == start + core, jnp.broadcast_to(own, (6, 128)), stats)
-        stats = jnp.where(place == start + 2, jnp.broadcast_to(half, (6, 128)), stats)
-    p_ref[18:24, :] = stats
-
-
-def collect(n, gqkv, go, gu, gd, head, tail, sq1, sq2):
-    vmem = pl.BlockSpec(memory_space=pltpu.VMEM)
-    return pl.pallas_call(
-        partial(collect_body, n),
-        in_specs=[vmem] * 8,
-        out_specs=[vmem] * 2,
-        out_shape=[jax.ShapeDtypeStruct((3, 4, D, D), BF16), jax.ShapeDtypeStruct((24, 128), F32)],
-        compiler_params=pltpu.CompilerParams(vmem_limit_bytes=24 << 20),
-        cost_estimate=cost(1, 6 << 20),
-        name="collect",
-    )(gqkv, go, gu, gd, head, tail, sq1, sq2)
 
 
 def leave_body(
@@ -1177,35 +1088,20 @@
 
 def per_device(inputs, cotangent, owner_list, master_rows, moment1_rows, moment2_rows):
     n = lax.axis_size("dp")
-    seq = lax.axis_index("seq")
-    core = seq % 2
     rows = D // n
     flat = [r.reshape(-1, 128) for r in (master_rows, moment1_rows, moment2_rows)]
     pk, pp = pack(owner_list, flat[0])
     w, p, x, cot = entry(n, pk.reshape(3, n, rows, D), pp, inputs, cotangent)
-    wt, wot, wut, wdt, wqkv, wo, wu, wd, small = prepare(w.reshape(3, 4, D, D), p)
-    lane = jnp.arange(UNITS, dtype=jnp.int32)
-    place = jnp.where(lane < OWN, lane, jnp.where(lane == OWN, core, 3 - core))
-    base = jnp.where(lane < OWN, 0, OWN)
-    table = jnp.concatenate([base + place, base, place]).astype(jnp.int32)
-
-    xt, a1, q1, kt1, vt1, k1, v1 = first_projection(x, small, wt)
-    o1, log1 = attend(table, q1, k1, vt1)
-    r1, hid, slope, z2, a2, sq1 = feed_first(table, xt, o1, small, wot, wut, wdt)
+    (xt, a1, q1, kt1, k1, v1, o1, log1, r1, hid, slope, z2, a2, sq1, wt, wot, wut, wdt, small) = first_stage(x, w, p)
     a2 = swap_inputs(a2)
-    q2, kt2, vt2, k2, v2 = second_projection(a2, wt)
-    o2, log2 = attend(table, q2, k2, vt2)
-    final, sq2, gr, go, gd, gu, gout, tail = feed_second(z2, o2, cot, small, wot, wut, wdt, wo, wu, wd)
-    dq, dk, dv = attend_back(table, q2, k2, kt2, v2, go, o2, log2)
+    final, sq2, gr, gd, gu, gout, tail, dq, dk, dv = second_stage(a2, z2, cot, w, wt, wot, wut, wdt, small)
     dk, dv = swap_grads(dk, dv)
-    gz, gr, go, gd, gu, gout, tail, gqkv, head = turn(
-        table, dq, dk, dv, a2, z2, gr, hid, slope, r1, o1, small, wqkv, wo, wu, wd, gd, gu, gout, tail
+    gz, gr, gd, gu, gout, tail, gqkv, head, dq, dk, dv = third_stage(
+        dq, dk, dv, a2, z2, gr, hid, slope, r1, o1, log1, q1, kt1, k1, v1, small, w, gd, gu, gout, tail
     )
-    dq, dk, dv = attend_back(table, q1, k1, kt1, v1, go, o1, log1)
     dk, dv = swap_grads(dk, dv)
-    grad, gqkv, head = last(table, dq, dk, dv, a1, xt, gr, gz, small, wqkv, gqkv, head)
-    g, pp = collect(n, gqkv, gout, gu, gd, head, tail, sq1, sq2)
-    g, p, final, grad = leave(n, g.reshape(3, 4, n, rows, D), pp, final, grad)
+    grad, g, pp = last_stage(n, dq, dk, dv, a1, xt, gr, gz, small, w, gqkv, head, gout, gu, gd, tail, sq1, sq2)
+    g, p, final, grad = leave(n, g, pp, final, grad)
     m_new, v_new, w_new = adam(owner_list, g.reshape(12, D, D), p, flat[1], flat[2], flat[0])
     sequences = inputs.shape[0] * n
     entries = inputs.shape[1] * lax.axis_size("seq") * D

time: 276 us -> 202 us (0.73)
  Pallas kernels: 243 us -> 192 us
  local copies, waits for them, and re-layouts: 26.9 us -> 6.5 us
    pallas_call x12 -> x4, Pallas kernels: 145 us -> 94.3 us  [stage_call(): pl.pallas_call(body, in_specs=[VM] * len(args), out_specs=[VM] * len(outs...]
    unnamed x76 -> x26, local copies, waits for them, and re-layouts: 26.9 us -> 6.42 us
where the time goes in v2:
time: 202 us
  Pallas kernels  192 us (95%)
  local copies, waits for them, and re-layouts  6.5 us (3%)
  other arithmetic  3.15 us (2%)
    pallas_call x4, Pallas kernels, stage_call(): pl.pallas_call(body, in_specs=[VM] * len(args), out_specs=[VM] * len(outs...  94.3 us
    pallas_call x1, Pallas kernels, leave(): pl.pallas_call(partial(leave_body, n), in_specs=[vmem] * 4, out_specs=[vm...  43 us
    pallas_call x1, Pallas kernels, entry(): pl.pallas_call(partial(entry_body, n), in_specs=[vmem] * 4, out_specs=[vm...  38.5 us
    pallas_call x1, Pallas kernels, adam(): pl.pallas_call(adam_body, grid_spec=spec, out_shape=[out, out, out], comp...  9.42 us
    unnamed x26, local copies, waits for them, and re-layouts  6.42 us
    pallas_call x2, Pallas kernels, swap_grads(): pl.pallas_call(swap_grads_body, in_specs=[vmem] * 2, out_specs=[vmem] * 2...  4.24 us

profile of v2, /device:TPU:0, one launch (start us, length us, event | category | flops | bytes accessed | tf_op | source)
XLA Modules:
  0.0 202.2 jit_solution(13765623155195600573)
XLA Ops:
  0.6 0.0 copy-start
  0.6 1.6 copy-done
  2.2 0.0 copy-start.6
  2.2 0.7 copy-done.6
  2.9 0.0 copy-start.3
  2.9 0.0 copy-start.4
  2.9 0.7 pack.1
  3.6 0.4 copy-done.3
  4.0 0.2 copy-done.4
  4.3 38.5 %entry.1 = (bf16[3,4,8,32,256]{4,3,2,1,0:T(8,128)(2,1)S(1)}, f32[24,128]{1,0:T(8,128)S(1)}, bf16[8,256,256]{2,1,0:T(8,128)(2,1)S(1)}, bf16[6,256,256]{2,1,0:T(8,128)(2,1)S(1)}) custom-call(bf16[3,8,32,256]{3,2,1,0:T(8,128)(2,1)S(1)} %bitcast.11, f32[24,128]{1,0:T(8,128)S(1)} %get-tuple-element.67.pp_ref, bf16[6,256,256]{2,1,0:T(8,128)(2,1)S(1)} %copy-done.3, ...), custom_call_target="tpu_custom_call" | custom-call | flops 1 | bytes 12582912 | tf_op jit(solution)/shard_map/entry/pallas_call | solution.py:750
  42.8 23.4 %first_stage.1 = (bf16[8,256,256]{2,1,0:T(8,128)(2,1)S(1)}, bf16[8,256,256]{2,1,0:T(8,128)(2,1)S(1)}, bf16[8,256,256]{2,1,0:T(8,128)(2,1)S(1)}, bf16[4,64,2048]{...) custom-call(bf16[8,256,256]{2,1,0:T(8,128)(2,1)S(1)} %get-tuple-elem, ...), custom_call_target="tpu_custom_call" | custom-call | flops 8000000000 | bytes 1048576 | tf_op jit(solution)/shard_map/first_stage/pallas_call | solution.py:327
  66.2 0.0 copy-start.7
  66.2 0.0 copy-start.9
  66.2 1.6 swap_inputs.1.a_ref.a2_ref
  67.8 41.6 %second_stage.1 = (bf16[6,256,256]{2,1,0:T(8,128)(2,1)S(1)}, f32[6,8,256]{2,1,0:T(8,128)S(1)}, f32[6,256,256]{2,1,0:T(8,128)S(1)}, f32[1024,256]{1,0:T(8,128)S(1...) custom-call(bf16[8,256,256]{2,1,0:T(8,128)(2,1)S(1)} %swap_inputs.1., ...), custom_call_target="tpu_custom_call" | custom-call | flops 20000000000 | bytes 1048576 | tf_op jit(solution)/shard_map/second_stage/pallas_call | solution.py:327
  109.4 0.0 copy-done.7
  109.4 0.0 copy-done.9
  109.4 0.0 copy-start.11
  109.4 0.0 copy-start.8
  109.4 0.0 copy-start.10
  109.5 2.1 %swap_grads.2 = (bf16[6,256,256]{2,1,0:T(8,128)(2,1)S(1)}, bf16[6,256,256]{2,1,0:T(8,128)(2,1)S(1)}) custom-call(bf16[8,256,256]{2,1,0:T(8,128)(2,1)S(1)} %get-tuple-element.80.dk_ref, bf16[8,256,256]{2,1,0:T(8,128)(2,1)S(1)} %get-tuple-element.81.dv_ref), custom_call_target="tpu_custom_call" | custom-call | flops 1 | bytes 4194304 | tf_op jit(solution)/shard_map/swap_grads/pallas_call | solution.py:835
  111.6 0.0 copy-done.11
  111.6 0.0 copy-done.8
  111.6 0.0 copy-done.10
  111.6 0.0 copy-start.12
  111.6 1.2 copy-done.12
  112.8 25.6 %third_stage.1 = (f32[6,256,256]{2,1,0:T(8,128)S(1)}, f32[6,256,256]{2,1,0:T(8,128)S(1)}, f32[1024,256]{1,0:T(8,128)S(1)}, f32[256,1024]{1,0:T(8,128)S(1)}, f32[...) custom-call(bf16[6,256,256]{2,1,0:T(8,128)(2,1)S(1)} %get-tuple-elem, ...), custom_call_target="tpu_custom_call" | custom-call | flops 16000000000 | bytes 1048576 | tf_op jit(solution)/shard_map/third_stage/pallas_call | solution.py:327
  138.4 2.1 %swap_grads.3 = (bf16[6,256,256]{2,1,0:T(8,128)(2,1)S(1)}, bf16[6,256,256]{2,1,0:T(8,128)(2,1)S(1)}) custom-call(bf16[8,256,256]{2,1,0:T(8,128)(2,1)S(1)} %get-tuple-element.99.dk_ref, bf16[8,256,256]{2,1,0:T(8,128)(2,1)S(1)} %get-tuple-element.100.dv_ref), custom_call_target="tpu_custom_call" | custom-call | flops 1 | bytes 4194304 | tf_op jit(solution)/shard_map/swap_grads/pallas_call | solution.py:835
  140.5 3.7 %last_stage.1 = (bf16[6,256,256]{2,1,0:T(8,128)(2,1)S(1)}, bf16[3,4,8,32,256]{4,3,2,1,0:T(8,128)(2,1)S(1)}, f32[24,128]{1,0:T(8,128)S(1)}) custom-call(bf16[6,256,256]{2,1,0:T(8,128)(2,1)S(1)} %get-tuple-element.98.dq_ref, bf16[6,256,256]{2,1,0:T(8,128)(2,1)S(1)} %get-tuple-element.101.dk_ref, bf16[6,256,256]{2,1,0:T(8,128)(2,1)S(1)} %get-tuple-element.102.dv_ref, ...), custom_call_target="tpu_custom_call" | custom-call | flops 3000000000 | bytes 1048576 | tf_op jit(solution)/shard_map/last_stage/pallas_call | solution.py:327
  144.2 0.0 copy-start.1
  144.2 1.1 copy-done.1
  145.3 43.0 %leave.1 = (bf16[3,4,8,32,256]{4,3,2,1,0:T(8,128)(2,1)S(1)}, f32[24,128]{1,0:T(8,128)S(1)}, bf16[6,256,256]{2,1,0:T(8,128)(2,1)S(1)}, bf16[6,256,256]{2,1,0:T(8,128)(2,1)S(1)}) custom-call(bf16[3,4,8,32,256]{4,3,2,1,0:T(8,128)(2,1)} %copy-done.1, f32[24,128]{1,0:T(8,128)S(1)} %get-tuple-element.116.pp_ref, ...), custom_call_target="tpu_custom_call" | custom-call | flops 1 | bytes 20971520 | tf_op jit(solution)/shard_map/leave/pallas_call | solution.py:981
  188.4 0.0 copy-start.2
  188.4 1.2 copy-done.2
  189.5 0.0 copy-start.5
  189.5 0.1 slice.10
  189.6 0.6 fusion.1
  190.2 1.3 convert_element_type.6
  191.5 1.3 convert_element_type.7
  192.8 0.0 copy-done.5
  192.8 9.4 %adam.1 = (f32[4096,128]{1,0:T(8,128)}, f32[4096,128]{1,0:T(8,128)}, f32[4096,128]{1,0:T(8,128)}) custom-call(s32[7]{0:T(128)} %owner_ref.3, bf16[12,256,256]{2,1,0:T(8,128)(2,1)} %bitcast.10, f32[24,128]{1,0:T(8,128)} %copy-done.5, f32[4096,128]{1,0:T(8,128)} %bitcast.12, f32[4096,128]{1,0:T(8,128)} %bitcast.13, f32[4096,128]{1,0:T(8,128)} %bitcast.8), custom_call_target="tpu_custom_call" | custom-call | flops 10485760 | bytes 14680064 | tf_op jit(solution)/shard_map/adam/pallas_call | solution.py:1079
  (1 shorter events, 0.0 us)
Async XLA Ops:
  0.6 1.6 copy-start
  2.2 0.7 copy-start.6
  2.9 1.1 copy-start.3
  2.9 1.4 copy-start.4
  66.2 43.2 %copy-start.7 = (bf16[2,8,256,128]{3,2,1,0:T(8,128)(2,1)}, bf16[2,8,256,128]{3,2,1,0:T(8,128)(2,1)S(1)}, u32[]{:S(2)}) copy-start(bf16[2,8,256,128]{3,2,1,0:T(8,128)(2,1)S(1)} %get-tuple-element.92.k_ref) | copy-start | bytes 3145732
  66.2 43.2 %copy-start.9 = (bf16[2,8,256,128]{3,2,1,0:T(8,128)(2,1)}, bf16[2,8,256,128]{3,2,1,0:T(8,128)(2,1)S(1)}, u32[]{:S(2)}) copy-start(bf16[2,8,256,128]{3,2,1,0:T(8,128)(2,1)S(1)} %get-tuple-element.93.v_ref) | copy-start | bytes 3145732
  109.4 2.2 %copy-start.11 = (f32[1792,128]{1,0:T(8,128)}, f32[1792,128]{1,0:T(8,128)S(1)}, u32[]{:S(2)}) copy-start(f32[1792,128]{1,0:T(8,128)S(1)} %get-tuple-element.97.tail_in) | copy-start | bytes 2752516
  109.4 2.2 %copy-start.8 = (bf16[2,8,256,128]{3,2,1,0:T(8,128)(2,1)S(1)}, bf16[2,8,256,128]{3,2,1,0:T(8,128)(2,1)}, u32[]{:S(2)}) copy-start(bf16[2,8,256,128]{3,2,1,0:T(8,128)(2,1)} %copy-done.7) | copy-start | bytes 3145732
  109.4 2.2 %copy-start.10 = (bf16[2,8,256,128]{3,2,1,0:T(8,128)(2,1)S(1)}, bf16[2,8,256,128]{3,2,1,0:T(8,128)(2,1)}, u32[]{:S(2)}) copy-start(bf16[2,8,256,128]{3,2,1,0:T(8,128)(2,1)} %copy-done.9) | copy-start | bytes 3145732
  111.6 1.2 copy-start.12
  144.2 1.1 copy-start.1
  188.4 1.2 copy-start.2
  189.5 3.2 %copy-start.5 = (f32[24,128]{1,0:T(8,128)}, f32[24,128]{1,0:T(8,128)S(1)}, u32[]{:S(2)}) copy-start(f32[24,128]{1,0:T(8,128)S(1)} %get-tuple-element.121.p_ref) | copy-start | bytes 36868

commit v3 on v2

--- a/solution.py
+++ b/solution.py
@@ -88,13 +88,17 @@
 
 
 def unit_place(unit, core):
-    place = jnp.where(unit < OWN, unit, jnp.where(unit == OWN, core, 3 - core))
-    base = jnp.where(unit < OWN, 0, OWN)
-    return place, base
+    later = unit // OWN
+    place = (1 - later) * unit + later * (core + (unit - OWN) * (3 - 2 * core))
+    return place, later * OWN
 
 
 def lanes(start, size):
     return pl.ds(pl.multiple_of(start, BLK), size)
+
+
+def pair_rows(pair):
+    return pl.ds(pl.multiple_of(pair * 128, 128), 128)
 
 
 def matrix(w_ref, kind, part):
@@ -141,13 +145,15 @@
 SUB = 128
 
 
-def attend(core, q_ref, k_ref, vt_ref, o_ref, log_ref, mask_ref, score_ref, prob_ref):
+def attend(core, q_ref, k_ref, vt_ref, o_ref, log_ref, mask_ref, score_ref, prob_ref, progress=None):
     def step(i, carry):
+        if progress is not None:
+            progress(i)
         pair, unit = i // UNITS, i % UNITS
         place, base = unit_place(unit, core)
 
         def branch(last):
-            block = q_ref[base + place, lanes(pair * 128, 128), :]
+            block = q_ref[base + place, pair_rows(pair), :]
             for half in range(2):
                 q = head_rows(block, half)
                 top = None
@@ -190,9 +196,9 @@
         place, base = unit_place(unit, core)
 
         def branch(last):
-            block = q_ref[base + place, lanes(pair * 128, 128), :]
-            go_block = go_ref[unit, lanes(pair * 128, 128), :]
-            o_block = o_ref[unit, lanes(pair * 128, 128), :]
+            block = q_ref[base + place, pair_rows(pair), :]
+            go_block = go_ref[unit, pair_rows(pair), :]
+            o_block = o_ref[unit, pair_rows(pair), :]
             keys = (last + 1) * BLK
             for half in range(2):
                 lo, hi = half * HD, (half + 1) * HD
@@ -242,32 +248,150 @@
 
 
 def first_stage_body(
-    x_ref, w_ref, p_ref,
+    n, pk_ref, pp_ref, x_ref, c_ref,
     xt_ref, a_ref, q_ref, kt_ref, k_ref, v_ref, o_ref, log_ref, r_ref, hid_ref, slope_ref, z_ref, a2_ref, sq_ref,
-    wt_ref, wot_ref, wut_ref, wdt_ref, small_ref, vt_ref, mask_ref, score_ref, prob_ref,
+    wt_ref, wot_ref, wut_ref, wdt_ref, small_ref, w_ref, co_ref,
+    vt_ref, mask_ref, score_ref, prob_ref, xo_ref, slot_ref, pslot_ref, chunk_ref,
+    ss0, ss1, rs0, rs1, ps0, ps1, gs0, gs1, xs0, xs1, cs0, cs1,
 ):
-    core = lax.axis_index("seq") % 2
+    dp = lax.axis_index("dp")
+    seq = lax.axis_index("seq")
+    chip, core = seq // 2, seq % 2
+    peers = peers_of(seq)
+
+    def scatter(kind, k):
+        to = (dp + k) % n
+        return send(pk_ref.at[kind, to], slot_ref.at[kind, k], (ss0, ss1), (kind, k), {"dp": to})
+
+    def small(k):
+        return send(pp_ref, pslot_ref.at[k], (ps0, ps1), k, {"dp": (dp + k) % n})
+
+    def gather(kind, k):
+        return send(chunk_ref.at[kind], w_ref.at[kind, seq, dp], (rs0, rs1), (kind, k), {"dp": (dp + k) % n})
+
+    def side(kind, which):
+        part = peers[2] if which == 2 else seq
+        to = peers[2] if which == 0 else peers[1]
+        return send(w_ref.at[kind, part], w_ref.at[kind, part], (gs0, gs1), (kind, which), {"seq": to})
+
+    def own(o):
+        to = peers[o]
+        return send(x_ref.at[3 * (to // 2) + to % 2], xo_ref.at[seq], (xs0, xs1), (o, 0), {"seq": to})
+
+    def shared(o):
+        if o == 3:
+            there = xo_ref.at[OWN + peers[2]]
+            return send(there, there, (xs0, xs1), (3, 1), {"seq": peers[1]})
+        to = peers[o]
+        return send(x_ref.at[3 * (to // 2) + 2], xo_ref.at[OWN + seq], (xs0, xs1), (o, 1), {"seq": to})
+
+    def target(o):
+        to = peers[o]
+        return send(c_ref.at[3 * (to // 2) + to % 2], co_ref.at[seq], (cs0, cs1), o, {"seq": to})
+
+    def target_shared(o):
+        slot = 4 if o == 2 else 5
+        return send(c_ref.at[2 if o == 3 else 5], co_ref.at[slot], (cs0, cs1), 4 + o, {"seq": peers[o]})
+
+    def sum_up(kind):
+        total = pk_ref[kind, dp].astype(F32)
+        for k in range(1, n):
+            scatter(kind, k).wait_recv()
+            total = total + slot_ref[kind, k].astype(F32)
+        chunk_ref[kind] = total.astype(BF16)
+        w_ref[kind, seq, dp] = total.astype(BF16)
+
+    offsets = range(1, n)
+    greet(n, dp, [peers[1], peers[2], peers[3]], True)
+    for k in offsets:
+        scatter(0, k).start()
+    for o in (2, 1):
+        shared(o).start()
+    for o in (2, 3, 1):
+        own(o).start()
+    for k in offsets:
+        small(k).start()
+    xo_ref[seq] = x_ref[3 * chip + core]
+    xo_ref[OWN + seq] = x_ref[3 * chip + 2]
+    co_ref[seq] = c_ref[3 * chip + core]
+    pl.when(chip == 0)(lambda: co_ref.__setitem__(4, c_ref[2]))
+    set_mask(mask_ref)
+    vt_ref[:, HD:, :] = jnp.ones((HEADS, VROWS - HD, ALL * BLK), BF16)
+    sum_up(0)
+    for k in offsets:
+        gather(0, k).start()
+    for kind in (1, 2):
+        for k in offsets:
+            scatter(kind, k).start()
+    total = pp_ref[...]
+    for k in offsets:
+        small(k).wait_recv()
+        total = total + pslot_ref[k]
+    for row in range(SMALL):
+        for part in range(2):
+            line = jnp.broadcast_to(total[2 * row + part : 2 * row + part + 1, :], (128, 128))
+            small_ref[row * D + part * 128 : row * D + (part + 1) * 128, :] = line.T
+    shared(2).wait_recv()
+    shared(3).start()
+    for o in (2, 3, 1):
+        own(o).wait_recv()
+    shared(1).wait_recv()
+    for k in offsets:
+        gather(0, k).wait_recv()
+    side(0, 0).start()
+    side(0, 1).start()
+    for o in (2, 3, 1):
+        target(o).start()
+    pl.when(chip == 0)(lambda: target_shared(2).start())
+    pl.when(chip == 1)(lambda: target_shared(3).start())
+    pl.when(chip == 1)(lambda: target_shared(1).start())
+    shared(3).wait_recv()
+
+    def begin(j, carry):
+        xt = xo_ref[j].T
+        xt_ref[j] = xt
+        unit_values, _ = standardize(xt.astype(F32))
+        a_ref[j] = (unit_values * param(small_ref, 0) + param(small_ref, 1)).astype(BF16)
+        return carry
+
+    lax.fori_loop(0, ALL, begin, 0)
+    side(0, 0).wait_recv()
+    side(0, 2).start()
+    side(0, 1).wait_recv()
+    side(0, 2).wait_recv()
     for t in range(3):
         wt_ref[t * D : (t + 1) * D, :] = matrix(w_ref, 0, t).T
-    for row in range(SMALL):
-        for side in range(2):
-            line = jnp.broadcast_to(p_ref[2 * row + side : 2 * row + side + 1, :], (128, 128))
-            small_ref[row * D + side * 128 : row * D + (side + 1) * 128, :] = line.T
-    set_mask(mask_ref)
-    vt_ref[:, HD:, :] = jnp.ones((HEADS, VROWS - HD, ALL * BLK), BF16)
-
-    def begin(j, carry):
-        xt = x_ref[j].T
-        xt_ref[j] = xt
-        unit_values, _ = standardize(xt.astype(F32))
-        a = (unit_values * param(small_ref, 0) + param(small_ref, 1)).astype(BF16)
-        a_ref[j] = a
-        project(j, a, wt_ref, q_ref, kt_ref, vt_ref, k_ref, v_ref)
+
+    def middle(j, carry):
+        project(j, a_ref[j], wt_ref, q_ref, kt_ref, vt_ref, k_ref, v_ref)
         return carry
 
-    lax.fori_loop(0, ALL, begin, 0)
-    attend(core, q_ref, k_ref, vt_ref, o_ref, log_ref, mask_ref, score_ref, prob_ref)
+    lax.fori_loop(0, ALL, middle, 0)
+    for kind in (1, 2):
+        sum_up(kind)
+        for k in offsets:
+            gather(kind, k).start()
+
+    def progress(i):
+        @pl.when(i == 5)
+        def _():
+            for kind in (1, 2):
+                for k in offsets:
+                    gather(kind, k).wait_recv()
+                side(kind, 0).start()
+                side(kind, 1).start()
+
+        @pl.when(i == 10)
+        def _():
+            for kind in (1, 2):
+                side(kind, 0).wait_recv()
+                side(kind, 2).start()
+
+    attend(core, q_ref, k_ref, vt_ref, o_ref, log_ref, mask_ref, score_ref, prob_ref, progress)
     wot_ref[...] = matrix(w_ref, 0, 3).T
+    for kind in (1, 2):
+        side(kind, 1).wait_recv()
+        side(kind, 2).wait_recv()
     for c in range(4):
         part = slice(c * D, (c + 1) * D)
         wut_ref[part, :] = matrix(w_ref, 1, c).T
@@ -295,6 +419,35 @@
         return carry
 
     lax.fori_loop(0, UNITS, feed, 0)
+    for o in (2, 3, 1):
+        target(o).wait()
+        own(o).wait_send()
+        shared(o).wait_send()
+
+    @pl.when(chip == 0)
+    def _():
+        target_shared(2).wait_send()
+        target_shared(3).wait_recv()
+
+    @pl.when(chip == 1)
+    def _():
+        target_shared(3).wait_send()
+        target_shared(1).wait_send()
+        target_shared(2).wait_recv()
+        target_shared(1).wait_recv()
+
+    for kind in range(3):
+        for k in offsets:
+            scatter(kind, k).wait_send()
+            gather(kind, k).wait_send()
+        for which in range(3):
+            side(kind, which).wait_send()
+    for k in offsets:
+        small(k).wait_send()
+
+
+def pair_of_sems(shape):
+    return [pltpu.SemaphoreType.DMA(shape), pltpu.SemaphoreType.DMA(shape)]
 
 
 VM = pl.BlockSpec(memory_space=pltpu.VMEM)
@@ -323,28 +476,43 @@
 ]
 
 
-def stage_call(body, name, args, outs, scratch, mib, flops):
+def stage_call(body, name, args, outs, scratch, mib, flops, **comm):
     return pl.pallas_call(
         body,
         in_specs=[VM] * len(args),
         out_specs=[VM] * len(outs),
         out_shape=outs,
         scratch_shapes=scratch,
-        compiler_params=pltpu.CompilerParams(vmem_limit_bytes=mib << 20),
+        compiler_params=pltpu.CompilerParams(vmem_limit_bytes=mib << 20, has_side_effects=bool(comm), **comm),
         cost_estimate=cost(flops, 1 << 20),
         name=name,
     )(*args)
 
 
-def first_stage(x, w, p):
+def first_stage(n, pk, pp, x, c):
+    rows = D // n
     tile, eight = (UNITS, BLK, BLK), (ALL, BLK, BLK)
     outs = [shape_of(eight), shape_of(eight), shape_of(eight)] + KEYS
     outs += [shape_of(tile), shape_of((UNITS, 2, 8, BLK), F32), shape_of(tile, F32)]
     outs += [shape_of((UNITS, FF, BLK)), shape_of((UNITS, FF, BLK)), shape_of(tile, F32), shape_of(tile)]
     outs += [shape_of((UNITS, 8, BLK), F32), shape_of((3 * D, D)), shape_of((D, D)), shape_of((FF, D))]
-    outs += [shape_of((D, FF)), shape_of((SMALL * D, 128), F32)]
+    outs += [shape_of((D, FF)), shape_of((SMALL * D, 128), F32), shape_of((3, 4, n, rows, D)), shape_of(tile)]
     scratch = [pltpu.VMEM((HEADS, VROWS, ALL * BLK), BF16)] + ATTEND_SCRATCH
-    return stage_call(first_stage_body, "first_stage", [x, w, p], outs, scratch, FIRST_MIB, 8e9)
+    scratch += [
+        pltpu.VMEM(eight, BF16),
+        pltpu.VMEM((3, n, rows, D), BF16),
+        pltpu.VMEM((n, 24, 128), F32),
+        pltpu.VMEM((3, rows, D), BF16),
+        *pair_of_sems((3, n)),
+        *pair_of_sems((3, n)),
+        *pair_of_sems((n,)),
+        *pair_of_sems((3, 3)),
+        *pair_of_sems((4, 2)),
+        *pair_of_sems((8,)),
+    ]
+    return stage_call(
+        partial(first_stage_body, n), "first_stage", [pk, pp, x, c], outs, scratch, FIRST_MIB, 8e9, collective_id=0
+    )
 
 
 def feed_back_tail(
@@ -539,7 +707,7 @@
     return stage_call(partial(last_stage_body, n), "last_stage", args, outs, scratch, LAST_MIB, 3e9)
 
 
-FIRST_MIB, SECOND_MIB, THIRD_MIB, LAST_MIB = 14, 24, 14, 8
+FIRST_MIB, SECOND_MIB, THIRD_MIB, LAST_MIB = 18, 24, 14, 8
 
 
 def owner_scalars(owner_ref):
@@ -638,140 +806,6 @@
     copy = send(w_ref.at[kind, peers[2]], w_ref.at[kind, peers[2]], side_sems, (kind, 2), {"seq": peers[1]})
     copy.start()
     return copy
-
-
-def entry_body(
-    n, pk_ref, pp_ref, x_ref, c_ref, w_ref, p_ref, xo_ref, co_ref, slot_ref, pslot_ref, chunk_ref,
-    ss0, ss1, rs0, rs1, ps0, ps1, gs0, gs1, xs0, xs1, cs0, cs1,
-):
-    dp = lax.axis_index("dp")
-    seq = lax.axis_index("seq")
-    chip, core = seq // 2, seq % 2
-    peers = peers_of(seq)
-    greet(n, dp, [peers[1], peers[2], peers[3]], True)
-    done = []
-    small = []
-    scatter = [[] for _ in range(3)]
-    for kind in range(3):
-        for k in range(1, n):
-            to = (dp + k) % n
-            copy = send(pk_ref.at[kind, to], slot_ref.at[kind, k], (ss0, ss1), (kind, k), {"dp": to})
-            copy.start()
-            scatter[kind].append(copy)
-        if kind == 0:
-            for k in range(1, n):
-                copy = send(pp_ref, pslot_ref.at[k], (ps0, ps1), k, {"dp": (dp + k) % n})
-                copy.start()
-                small.append(copy)
-    for o in (2, 3, 1):
-        to = peers[o]
-        for part, (source, target) in enumerate(((3 * (to // 2) + to % 2, seq), (3 * (to // 2) + 2, OWN + seq))):
-            copy = send(x_ref.at[source], xo_ref.at[target], (xs0, xs1), (o, part), {"seq": to})
-            copy.start()
-            done.append(copy)
-    for o in (2, 3, 1):
-        to = peers[o]
-        copy = send(c_ref.at[3 * (to // 2) + to % 2], co_ref.at[seq], (cs0, cs1), o, {"seq": to})
-        copy.start()
-        done.append(copy)
-
-    @pl.when(chip == 0)
-    def _():
-        send(c_ref.at[5], co_ref.at[4], (cs0, cs1), 4 + 2, {"seq": peers[2]}).start()
-
-    @pl.when(chip == 1)
-    def _():
-        send(c_ref.at[2], co_ref.at[5], (cs0, cs1), 4 + 3, {"seq": peers[3]}).start()
-        send(c_ref.at[5], co_ref.at[5], (cs0, cs1), 4 + 1, {"seq": peers[1]}).start()
-
-    xo_ref[seq] = x_ref[3 * chip + core]
-    xo_ref[OWN + seq] = x_ref[3 * chip + 2]
-    co_ref[seq] = c_ref[3 * chip + core]
-
-    @pl.when(chip == 0)
-    def _():
-        co_ref[4] = c_ref[2]
-
-    gathers = []
-    for kind in range(3):
-        total = pk_ref[kind, dp].astype(F32)
-        for k in range(1, n):
-            scatter[kind][k - 1].wait_recv()
-            total = total + slot_ref[kind, k].astype(F32)
-        chunk_ref[kind] = total.astype(BF16)
-        w_ref[kind, seq, dp] = total.astype(BF16)
-        gathers.append(spread(n, dp, seq, peers, kind, w_ref, chunk_ref, (rs0, rs1)))
-    sides = []
-    for kind in range(3):
-        for copy in gathers[kind]:
-            copy.wait_recv()
-        sides.append(share(seq, peers, kind, w_ref, (gs0, gs1)))
-    total = pp_ref[...]
-    for copy in small:
-        copy.wait_recv()
-    for k in range(1, n):
-        total = total + pslot_ref[k]
-    p_ref[...] = total
-    for kind in range(3):
-        sides[kind][0].wait_recv()
-        sides[kind].append(forward(seq, peers, kind, w_ref, (gs0, gs1)))
-    for kind in range(3):
-        sides[kind][1].wait_recv()
-        sides[kind][2].wait_recv()
-
-    @pl.when(chip == 0)
-    def _():
-        send(c_ref.at[5], co_ref.at[4], (cs0, cs1), 4 + 2, {"seq": peers[2]}).wait_send()
-        send(c_ref.at[2], co_ref.at[5], (cs0, cs1), 4 + 3, {"seq": peers[3]}).wait_recv()
-
-    @pl.when(chip == 1)
-    def _():
-        send(c_ref.at[2], co_ref.at[5], (cs0, cs1), 4 + 3, {"seq": peers[3]}).wait_send()
-        send(c_ref.at[5], co_ref.at[5], (cs0, cs1), 4 + 1, {"seq": peers[1]}).wait_send()
-        send(c_ref.at[5], co_ref.at[4], (cs0, cs1), 4 + 2, {"seq": peers[2]}).wait_recv()
-        send(c_ref.at[5], co_ref.at[5], (cs0, cs1), 4 + 1, {"seq": peers[1]}).wait_recv()
-
-    for copy in done:
-        copy.wait()
-    for kind in range(3):
-        for copy in scatter[kind] + gathers[kind] + sides[kind]:
-            copy.wait_send()
-    for copy in small:
-        copy.wait_send()
-
-
-def pair_of_sems(shape):
-    return [pltpu.SemaphoreType.DMA(shape), pltpu.SemaphoreType.DMA(shape)]
-
-
-def entry(n, pk, pp, x, c):
-    rows = D // n
-    vmem = pl.BlockSpec(memory_space=pltpu.VMEM)
-    return pl.pallas_call(
-        partial(entry_body, n),
-        in_specs=[vmem] * 4,
-        out_specs=[vmem] * 4,
-        out_shape=[
-            jax.ShapeDtypeStruct((3, 4, n, rows, D), BF16),
-            jax.ShapeDtypeStruct((24, 128), F32),
-            jax.ShapeDtypeStruct((ALL, BLK, BLK), BF16),
-            jax.ShapeDtypeStruct((UNITS, BLK, BLK), BF16),
-        ],
-        scratch_shapes=[
-            pltpu.VMEM((3, n, rows, D), BF16),
-            pltpu.VMEM((n, 24, 128), F32),
-            pltpu.VMEM((3, rows, D), BF16),
-            *pair_of_sems((3, n)),
-            *pair_of_sems((3, n)),
-            *pair_of_sems((n,)),
-            *pair_of_sems((3, 3)),
-            *pair_of_sems((4, 2)),
-            *pair_of_sems((8,)),
-        ],
-        compiler_params=pltpu.CompilerParams(collective_id=0, has_side_effects=True, vmem_limit_bytes=40 << 20),
-        cost_estimate=cost(1, 12 << 20),
-        name="entry",
-    )(pk, pp, x, c)
 
 
 def swap_inputs_body(a_ref, out_ref, s0, s1):
@@ -1091,8 +1125,9 @@
     rows = D // n
     flat = [r.reshape(-1, 128) for r in (master_rows, moment1_rows, moment2_rows)]
     pk, pp = pack(owner_list, flat[0])
-    w, p, x, cot = entry(n, pk.reshape(3, n, rows, D), pp, inputs, cotangent)
-    (xt, a1, q1, kt1, k1, v1, o1, log1, r1, hid, slope, z2, a2, sq1, wt, wot, wut, wdt, small) = first_stage(x, w, p)
+    (xt, a1, q1, kt1, k1, v1, o1, log1, r1, hid, slope, z2, a2, sq1, wt, wot, wut, wdt, small, w, cot) = first_stage(
+        n, pk.reshape(3, n, rows, D), pp, inputs, cotangent
+    )
     a2 = swap_inputs(a2)
     final, sq2, gr, gd, gu, gout, tail, dq, dk, dv = second_stage(a2, z2, cot, w, wt, wot, wut, wdt, small)
     dk, dv = swap_grads(dk, dv)

time: 202 us -> 192 us (0.950)
  Pallas kernels: 192 us -> 182 us
    pallas_call x1 -> x0, Pallas kernels: 38.5 us -> none  [entry(): pl.pallas_call(partial(entry_body, n), in_specs=[vmem] * 4, out_specs=[vm...]
    pallas_call x4, Pallas kernels: 94.3 us -> 122 us  [stage_call(): pl.pallas_call(body, in_specs=[VM] * len(args), out_specs=[VM] * len(outs...]
    unnamed x26 -> x22, local copies, waits for them, and re-layouts: 6.42 us -> 5.26 us
where the time goes in v3:
time: 192 us; the launch traced here: 191 us
  Pallas kernels  182 us (95%)
  local copies, waits for them, and re-layouts  5.34 us (3%)
  other arithmetic  3.15 us (2%)
    pallas_call x4, Pallas kernels, stage_call(): pl.pallas_call(body, in_specs=[VM] * len(args), out_specs=[VM] * len(outs...  122 us
    pallas_call x1, Pallas kernels, leave(): pl.pallas_call(partial(leave_body, n), in_specs=[vmem] * 4, out_specs=[vm...  44.7 us
    pallas_call x1, Pallas kernels, adam(): pl.pallas_call(adam_body, grid_spec=spec, out_shape=[out, out, out], comp...  9.07 us
    unnamed x22, local copies, waits for them, and re-layouts  5.26 us
    pallas_call x2, Pallas kernels, swap_grads(): pl.pallas_call(swap_grads_body, in_specs=[vmem] * 2, out_specs=[vmem] * 2...  4.23 us

profile of v3, /device:TPU:0, one launch (start us, length us, event | category | flops | bytes accessed | tf_op | source)
XLA Modules:
  0.0 191.1 jit_solution(9795313066042268720)
XLA Ops:
  0.6 0.0 copy-start
  0.6 1.6 copy-done
  2.2 0.0 copy-start.4
  2.2 0.7 copy-done.4
  2.9 0.0 copy-start.5
  2.9 0.0 copy-start.6
  2.9 0.7 pack.1
  3.6 0.4 copy-done.5
  4.0 0.2 copy-done.6
  4.3 50.5 %first_stage.1 = (bf16[8,256,256]{2,1,0:T(8,128)(2,1)S(1)}, bf16[8,256,256]{2,1,0:T(8,128)(2,1)S(1)}, bf16[8,256,256]{2,1,0:T(8,128)(2,1)S(1)}, bf16[4,64,2048]{...) custom-call(bf16[3,8,32,256]{3,2,1,0:T(8,128)(2,1)S(1)} %bitcast.11,, ...), custom_call_target="tpu_custom_call" | custom-call | flops 8000000000 | bytes 1048576 | tf_op jit(solution)/shard_map/first_stage/pallas_call | solution.py:480
  54.8 0.0 copy-start.7
  54.8 0.0 copy-start.9
  54.8 1.6 swap_inputs.1.a_ref.a2_ref
  56.4 41.7 %second_stage.1 = (bf16[6,256,256]{2,1,0:T(8,128)(2,1)S(1)}, f32[6,8,256]{2,1,0:T(8,128)S(1)}, f32[6,256,256]{2,1,0:T(8,128)S(1)}, f32[1024,256]{1,0:T(8,128)S(1...) custom-call(bf16[8,256,256]{2,1,0:T(8,128)(2,1)S(1)} %swap_inputs.1., ...), custom_call_target="tpu_custom_call" | custom-call | flops 20000000000 | bytes 1048576 | tf_op jit(solution)/shard_map/second_stage/pallas_call | solution.py:480
  98.1 0.0 copy-done.7
  98.1 0.0 copy-done.9
  98.2 0.0 copy-start.8
  98.2 0.0 copy-start.10
  98.2 2.1 %swap_grads.2 = (bf16[6,256,256]{2,1,0:T(8,128)(2,1)S(1)}, bf16[6,256,256]{2,1,0:T(8,128)(2,1)S(1)}) custom-call(bf16[8,256,256]{2,1,0:T(8,128)(2,1)S(1)} %get-tuple-element.76.dk_ref, bf16[8,256,256]{2,1,0:T(8,128)(2,1)S(1)} %get-tuple-element.77.dv_ref), custom_call_target="tpu_custom_call" | custom-call | flops 1 | bytes 4194304 | tf_op jit(solution)/shard_map/swap_grads/pallas_call | solution.py:869
  100.3 0.0 copy-done.8
  100.3 0.0 copy-done.10
  100.3 25.7 %third_stage.1 = (f32[6,256,256]{2,1,0:T(8,128)S(1)}, f32[6,256,256]{2,1,0:T(8,128)S(1)}, f32[1024,256]{1,0:T(8,128)S(1)}, f32[256,1024]{1,0:T(8,128)S(1)}, f32[...) custom-call(bf16[6,256,256]{2,1,0:T(8,128)(2,1)S(1)} %get-tuple-elem, ...), custom_call_target="tpu_custom_call" | custom-call | flops 16000000000 | bytes 1048576 | tf_op jit(solution)/shard_map/third_stage/pallas_call | solution.py:480
  126.0 2.1 %swap_grads.3 = (bf16[6,256,256]{2,1,0:T(8,128)(2,1)S(1)}, bf16[6,256,256]{2,1,0:T(8,128)(2,1)S(1)}) custom-call(bf16[8,256,256]{2,1,0:T(8,128)(2,1)S(1)} %get-tuple-element.95.dk_ref, bf16[8,256,256]{2,1,0:T(8,128)(2,1)S(1)} %get-tuple-element.96.dv_ref), custom_call_target="tpu_custom_call" | custom-call | flops 1 | bytes 4194304 | tf_op jit(solution)/shard_map/swap_grads/pallas_call | solution.py:869
  128.2 3.6 %last_stage.1 = (bf16[6,256,256]{2,1,0:T(8,128)(2,1)S(1)}, bf16[3,4,8,32,256]{4,3,2,1,0:T(8,128)(2,1)S(1)}, f32[24,128]{1,0:T(8,128)S(1)}) custom-call(bf16[6,256,256]{2,1,0:T(8,128)(2,1)S(1)} %get-tuple-element.94.dq_ref, bf16[6,256,256]{2,1,0:T(8,128)(2,1)S(1)} %get-tuple-element.97.dk_ref, bf16[6,256,256]{2,1,0:T(8,128)(2,1)S(1)} %get-tuple-element.98.dv_ref, ...), custom_call_target="tpu_custom_call" | custom-call | flops 3000000000 | bytes 1048576 | tf_op jit(solution)/shard_map/last_stage/pallas_call | solution.py:480
  131.8 0.0 copy-start.1
  131.8 1.1 copy-done.1
  132.9 44.7 %leave.1 = (bf16[3,4,8,32,256]{4,3,2,1,0:T(8,128)(2,1)S(1)}, f32[24,128]{1,0:T(8,128)S(1)}, bf16[6,256,256]{2,1,0:T(8,128)(2,1)S(1)}, bf16[6,256,256]{2,1,0:T(8,128)(2,1)S(1)}) custom-call(bf16[3,4,8,32,256]{4,3,2,1,0:T(8,128)(2,1)} %copy-done.1, f32[24,128]{1,0:T(8,128)S(1)} %get-tuple-element.112.pp_ref, ...), custom_call_target="tpu_custom_call" | custom-call | flops 1 | bytes 20971520 | tf_op jit(solution)/shard_map/leave/pallas_call | solution.py:1015
  177.7 0.0 copy-start.2
  177.7 1.2 copy-done.2
  178.8 0.0 copy-start.3
  178.8 0.1 slice.10
  178.9 0.6 fusion.1
  179.5 1.3 convert_element_type.6
  180.8 1.3 convert_element_type.7
  182.1 0.0 copy-done.3
  182.1 9.1 %adam.1 = (f32[4096,128]{1,0:T(8,128)}, f32[4096,128]{1,0:T(8,128)}, f32[4096,128]{1,0:T(8,128)}) custom-call(s32[7]{0:T(128)} %owner_ref.3, bf16[12,256,256]{2,1,0:T(8,128)(2,1)} %bitcast.10, f32[24,128]{1,0:T(8,128)} %copy-done.3, f32[4096,128]{1,0:T(8,128)} %bitcast.12, f32[4096,128]{1,0:T(8,128)} %bitcast.13, f32[4096,128]{1,0:T(8,128)} %bitcast.8), custom_call_target="tpu_custom_call" | custom-call | flops 10485760 | bytes 14680064 | tf_op jit(solution)/shard_map/adam/pallas_call | solution.py:1113
  (1 shorter events, 0.0 us)
Async XLA Ops:
  0.6 1.6 copy-start
  2.2 0.7 copy-start.4
  2.9 1.1 copy-start.5
  2.9 1.4 copy-start.6
  54.8 43.4 %copy-start.7 = (bf16[2,8,256,128]{3,2,1,0:T(8,128)(2,1)}, bf16[2,8,256,128]{3,2,1,0:T(8,128)(2,1)S(1)}, u32[]{:S(2)}) copy-start(bf16[2,8,256,128]{3,2,1,0:T(8,128)(2,1)S(1)} %get-tuple-element.88.k_ref) | copy-start | bytes 3145732
  54.8 43.4 %copy-start.9 = (bf16[2,8,256,128]{3,2,1,0:T(8,128)(2,1)}, bf16[2,8,256,128]{3,2,1,0:T(8,128)(2,1)S(1)}, u32[]{:S(2)}) copy-start(bf16[2,8,256,128]{3,2,1,0:T(8,128)(2,1)S(1)} %get-tuple-element.89.v_ref) | copy-start | bytes 3145732
  98.2 2.2 %copy-start.8 = (bf16[2,8,256,128]{3,2,1,0:T(8,128)(2,1)S(1)}, bf16[2,8,256,128]{3,2,1,0:T(8,128)(2,1)}, u32[]{:S(2)}) copy-start(bf16[2,8,256,128]{3,2,1,0:T(8,128)(2,1)} %copy-done.7) | copy-start | bytes 3145732
  98.2 2.1 %copy-start.10 = (bf16[2,8,256,128]{3,2,1,0:T(8,128)(2,1)S(1)}, bf16[2,8,256,128]{3,2,1,0:T(8,128)(2,1)}, u32[]{:S(2)}) copy-start(bf16[2,8,256,128]{3,2,1,0:T(8,128)(2,1)} %copy-done.9) | copy-start | bytes 3145732
  131.8 1.1 copy-start.1
  177.7 1.2 copy-start.2
  178.8 3.2 %copy-start.3 = (f32[24,128]{1,0:T(8,128)}, f32[24,128]{1,0:T(8,128)S(1)}, u32[]{:S(2)}) copy-start(f32[24,128]{1,0:T(8,128)S(1)} %get-tuple-element.117.p_ref) | copy-start | bytes 36868

commit v4 on v3

v4 whole, which is shorter than its diff:
```python
import math
from functools import partial

import jax
import jax.numpy as jnp
from jax import lax
from jax.experimental import pallas as pl
from jax.experimental.pallas import tpu as pltpu
from jax.sharding import PartitionSpec as P

D = 256
HEADS = 4
HD = 64
FF = 1024
STEP = 3
SMALL = 9
BLK = 256
OWN = 4
UNITS = 6
ALL = 8
F32 = jnp.float32
BF16 = jnp.bfloat16
MESH = pl.DeviceIdType.MESH

norm_eps = 1e-05
stat_eps = 1e-06
adam_eps = 1e-08
masked_score = -1e30


def dot(left, right):
    return lax.dot_general(left, right, (((1,), (0,)), ((), ())), preferred_element_type=F32)


def dot_nt(left, right):
    return lax.dot_general(left, right, (((1,), (1,)), ((), ())), preferred_element_type=F32)


def wide(column):
    return jnp.concatenate([column, column], axis=1)


def fold(values):
    return values[:, :128] + values[:, 128:]


def standardize(values):
    average = jnp.mean(values, axis=0, keepdims=True)
    centered = values - average
    spread = jnp.mean(centered * centered, axis=0, keepdims=True)
    inverse = lax.rsqrt(spread + norm_eps)
    return centered * inverse, inverse


def standardize_back(grad, unit_values, inverse):
    average = jnp.mean(grad, axis=0, keepdims=True)
    inner = jnp.mean(grad * unit_values, axis=0, keepdims=True)
    return (grad - average - unit_values * inner) * inverse


def param(small_ref, row):
    return wide(small_ref[row * D : (row + 1) * D, :])


def gelu_parts(e):
    cdf = 0.5 * lax.erf(e * math.sqrt(0.5)) + 0.5
    hid = e * cdf
    slope = cdf + e * (jnp.exp(-0.5 * e * e) * (1.0 / math.sqrt(2.0 * math.pi)))
    return hid, slope


def full(shape):
    return pl.BlockSpec(shape, lambda *args: (0,) * len(shape), pipeline_mode=pl.Buffered(1))


def params_of(ndims=1, mib=56):
    return pltpu.CompilerParams(
        dimension_semantics=("arbitrary",) * ndims, vmem_limit_bytes=mib << 20
    )


def cost(flops, nbytes, trans=0):
    return pl.CostEstimate(flops=int(flops), bytes_accessed=int(nbytes), transcendentals=int(trans))


LOG2E = math.log2(math.e)
VROWS = HD + 16


def unit_place(unit, core):
    later = unit // OWN
    place = (1 - later) * unit + later * (core + (unit - OWN) * (3 - 2 * core))
    return place, later * OWN


def lanes(start, size):
    return pl.ds(pl.multiple_of(start, BLK), size)


def pair_rows(pair):
    return pl.ds(pl.multiple_of(pair * 128, 128), 128)


def matrix(w_ref, kind, part):
    n, rows = w_ref.shape[2:4]
    if rows % 16 == 0:
        return w_ref[kind, part].reshape(D, D)
    return jnp.concatenate([w_ref[kind, part, i] for i in range(n)], axis=0)


def peers_of(seq):
    return {1: seq + 1 - 2 * (seq % 2), 2: (seq + 2) % 4, 3: 3 - seq}


def greet(n, dp, peers, wide_group):
    barrier = pltpu.get_barrier_semaphore()
    count = 0
    for peer in peers:
        pl.semaphore_signal(barrier, inc=1, device_id={"seq": peer}, device_id_type=MESH)
        count += 1
    if wide_group:
        for k in range(1, n):
            pl.semaphore_signal(barrier, inc=1, device_id={"dp": (dp + k) % n}, device_id_type=MESH)
            count += 1
    pl.semaphore_wait(barrier, count)


def send(source, target, sems, index, device):
    return pltpu.make_async_remote_copy(
        src_ref=source,
        dst_ref=target,
        send_sem=sems[0].at[index],
        recv_sem=sems[1].at[index],
        device_id=device,
        device_id_type=MESH,
    )


def pair_of_sems(shape):
    return [pltpu.SemaphoreType.DMA(shape), pltpu.SemaphoreType.DMA(shape)]


def project(j, a, wt_ref, q_ref, kt_ref, vt_ref, k_ref, v_ref):
    where = lanes(j * BLK, BLK)
    q_ref[j] = (dot(wt_ref[0:D], a) * HD ** (-0.5)).astype(BF16)
    kt = dot(wt_ref[D : 2 * D], a).astype(BF16)
    vt = dot(wt_ref[2 * D : 3 * D], a).astype(BF16)
    for h in range(HEADS):
        kt_ref[h, :, where] = kt[h * HD : (h + 1) * HD]
        vt_ref[h, 0:HD, where] = vt[h * HD : (h + 1) * HD]
    k = kt.T
    v = vt.T
    for h in range(2):
        k_ref[h, j] = k[:, h * 128 : (h + 1) * 128]
        v_ref[h, j] = v[:, h * 128 : (h + 1) * 128]


def head_rows(values, half):
    rows = lax.broadcasted_iota(jnp.int32, values.shape, 0)
    keep = (rows < HD) if half == 0 else (rows >= HD)
    return jnp.where(keep, values, jnp.zeros_like(values))


def set_mask(mask_ref):
    keys = lax.broadcasted_iota(jnp.int32, (BLK, BLK), 0)
    queries = lax.broadcasted_iota(jnp.int32, (BLK, BLK), 1)
    mask_ref[...] = jnp.where(keys <= queries, 0.0, masked_score)


def groups(values, op):
    out = values[0:8]
    for i in range(1, values.shape[0] // 8):
        out = op(out, values[i * 8 : (i + 1) * 8])
    return out


SUB = 128


def ordered(i):
    return (i + OWN) % UNITS


def attend(core, q_ref, k_ref, vt_ref, o_ref, log_ref, mask_ref, score_ref, prob_ref, progress=None):
    def step(i, carry):
        if progress is not None:
            progress(i)
        pair, unit = i % 2, ordered(i // 2)
        place, base = unit_place(unit, core)

        def branch(last):
            block = q_ref[base + place, pair_rows(pair), :]
            for half in range(2):
                q = head_rows(block, half)
                top = None
                for kb in range(last + 1):
                    for sub in range(BLK // SUB):
                        rows = slice(sub * SUB, (sub + 1) * SUB)
                        score = dot(k_ref[pair, base + kb, rows, :], q)
                        if kb == last:
                            score = score + mask_ref[rows, :]
                        score_ref[half, kb, rows, :] = score
                        peak = groups(score, jnp.maximum)
                        top = peak if top is None else jnp.maximum(top, peak)
                top = jnp.max(top, axis=0, keepdims=True)
                for kb in range(last + 1):
                    for sub in range(BLK // SUB):
                        rows = slice(sub * SUB, (sub + 1) * SUB)
                        weight = jnp.exp(score_ref[half, kb, rows, :] - top)
                        prob_ref[half, kb * BLK + sub * SUB : kb * BLK + (sub + 1) * SUB, :] = weight.astype(BF16)
                keys = (last + 1) * BLK
                out = dot(vt_ref[2 * pair + half, :, lanes(base * BLK, keys)], prob_ref[half, 0:keys, :])
                total = out[HD : HD + 1]
                o_ref[unit, pl.ds(pl.multiple_of(pair * 128 + half * HD, HD), HD), :] = (out[0:HD] / total).astype(BF16)
                log_ref[unit, pair, half : half + 1, :] = top + jnp.log(total)

        for last in range(OWN):
            pl.when(place == last)(partial(branch, last))
        return carry

    lax.fori_loop(0, 2 * UNITS, step, 0)


def attend_back(
    core, q_ref, k_ref, kt_ref, v_ref, go_ref, o_ref, log_ref, dq_ref, dk_ref, dv_ref, mask_ref, prob_ref, slope_ref, dk_acc, dv_acc,
    part_ref, got_ref, ds0, ds1, peer, progress=None,
):
    dk_acc[...] = jnp.zeros_like(dk_acc)
    dv_acc[...] = jnp.zeros_like(dv_acc)

    pairs = ((0, dk_acc, dk_ref), (1, dv_acc, dv_ref))

    def piece(acc, j):
        return acc[:, :, j * BLK : (j + 1) * BLK].reshape(D, BLK)

    def swap(which, side):
        position = 1 - core if side == 0 else 2 + core
        return send(part_ref.at[which, position], got_ref.at[which, side], (ds0, ds1), (which, side), {"seq": peer})

    def step(i, carry):
        @pl.when(i == 4)
        def _():
            for which, acc, _ in pairs:
                for position in range(OWN):
                    part_ref[which, position] = piece(acc, OWN + position).astype(BF16)
            for which in range(2):
                for side in range(2):
                    swap(which, side).start()

        if progress is not None:
            progress(i)
        pair, unit = i % 2, ordered(i // 2)
        place, base = unit_place(unit, core)

        def branch(last):
            block = q_ref[base + place, pair_rows(pair), :]
            go_block = go_ref[unit, pair_rows(pair), :]
            o_block = o_ref[unit, pair_rows(pair), :]
            keys = (last + 1) * BLK
            for half in range(2):
                lo, hi = half * HD, (half + 1) * HD
                q = head_rows(block, half)
                go = head_rows(go_block, half)
                q_head = block[lo:hi]
                go_head = go_block[lo:hi]
                log_total = log_ref[unit, pair, half : half + 1, :]
                inner = jnp.sum(go_head.astype(F32) * o_block[lo:hi].astype(F32), axis=0, keepdims=True)
                for kb in range(last + 1):
                    for sub in range(BLK // SUB):
                        rows = slice(sub * SUB, (sub + 1) * SUB)
                        to = slice(kb * BLK + sub * SUB, kb * BLK + (sub + 1) * SUB)
                        score = dot(k_ref[pair, base + kb, rows, :], q)
                        if kb == last:
                            score = score + mask_ref[rows, :]
                        weight = jnp.exp(score - log_total)
                        slope = dot(v_ref[pair, base + kb, rows, :], go)
                        prob_ref[half, to, :] = weight.astype(BF16)
                        slope_ref[half, to, :] = (weight * (slope - inner)).astype(BF16)
                head = 2 * pair + half
                where = lanes(base * BLK, keys)
                dv_acc[head, :, where] += dot_nt(go_head, prob_ref[half, 0:keys, :])
                dk_acc[head, :, where] += dot_nt(q_head, slope_ref[half, 0:keys, :])
                dq = dot(kt_ref[head, :, where], slope_ref[half, 0:keys, :])
                dq_ref[unit, pl.ds(pl.multiple_of(pair * 128 + lo, HD), HD), :] = (dq * HD ** (-0.5)).astype(BF16)

        for last in range(OWN):
            pl.when(place == last)(partial(branch, last))
        return carry

    lax.fori_loop(0, 2 * UNITS, step, 0)
    for which, acc, ref in pairs:
        for j in range(OWN):
            ref[j] = piece(acc, j).astype(BF16)
    for which, acc, ref in pairs:
        for side, position in enumerate((core, 3 - core)):
            swap(which, side).wait()
            ref[OWN + side] = (part_ref[which, position].astype(F32) + got_ref[which, side].astype(F32)).astype(BF16)


def forward_parts(z, o, wot_ref, small_ref):
    r = z + dot(wot_ref[...], o)
    unit_values, inverse = standardize(r)
    m = (unit_values * param(small_ref, 2) + param(small_ref, 3)).astype(BF16)
    return r, unit_values, inverse, m


def squares_of(out):
    return groups(out * out, jnp.add)


def first_stage_body(
    n, pk_ref, pp_ref, x_ref, c_ref,
    xt_ref, a_ref, q_ref, kt_ref, k_ref, v_ref, o_ref, log_ref, r_ref, hid_ref, slope_ref, z_ref, a2_ref, sq_ref,
    wt_ref, wot_ref, wut_ref, wdt_ref, small_ref, w_ref, co_ref,
    vt_ref, mask_ref, score_ref, prob_ref, xo_ref, slot_ref, pslot_ref, chunk_ref,
    ss0, ss1, rs0, rs1, ps0, ps1, gs0, gs1, xs0, xs1, cs0, cs1, ns0, ns1, hid_buf, slope_buf, hs,
):
    dp = lax.axis_index("dp")
    seq = lax.axis_index("seq")
    chip, core = seq // 2, seq % 2
    peers = peers_of(seq)

    def scatter(kind, k):
        to = (dp + k) % n
        return send(pk_ref.at[kind, to], slot_ref.at[kind, k], (ss0, ss1), (kind, k), {"dp": to})

    def small(k):
        return send(pp_ref, pslot_ref.at[k], (ps0, ps1), k, {"dp": (dp + k) % n})

    def gather(kind, k):
        return send(chunk_ref.at[kind], w_ref.at[kind, seq, dp], (rs0, rs1), (kind, k), {"dp": (dp + k) % n})

    def side(kind, which):
        part = peers[2] if which == 2 else seq
        to = peers[2] if which == 0 else peers[1]
        return send(w_ref.at[kind, part], w_ref.at[kind, part], (gs0, gs1), (kind, which), {"seq": to})

    def own(o):
        to = peers[o]
        return send(x_ref.at[3 * (to // 2) + to % 2], xo_ref.at[seq], (xs0, xs1), (o, 0), {"seq": to})

    def shared(o):
        if o == 3:
            there = xo_ref.at[OWN + peers[2]]
            return send(there, there, (xs0, xs1), (3, 1), {"seq": peers[1]})
        to = peers[o]
        return send(x_ref.at[3 * (to // 2) + 2], xo_ref.at[OWN + seq], (xs0, xs1), (o, 1), {"seq": to})

    def target(o):
        to = peers[o]
        return send(c_ref.at[3 * (to // 2) + to % 2], co_ref.at[seq], (cs0, cs1), o, {"seq": to})

    def target_shared(o):
        slot = 4 if o == 2 else 5
        return send(c_ref.at[2 if o == 3 else 5], co_ref.at[slot], (cs0, cs1), 4 + o, {"seq": peers[o]})

    def sum_up(kind):
        total = pk_ref[kind, dp].astype(F32)
        for k in range(1, n):
            scatter(kind, k).wait_recv()
            total = total + slot_ref[kind, k].astype(F32)
        chunk_ref[kind] = total.astype(BF16)
        w_ref[kind, seq, dp] = total.astype(BF16)

    offsets = range(1, n)
    greet(n, dp, [peers[1], peers[2], peers[3]], True)
    for k in offsets:
        scatter(0, k).start()
    for o in (2, 1):
        shared(o).start()
    for o in (2, 3, 1):
        own(o).start()
    for k in offsets:
        small(k).start()
    xo_ref[seq] = x_ref[3 * chip + core]
    xo_ref[OWN + seq] = x_ref[3 * chip + 2]
    co_ref[seq] = c_ref[3 * chip + core]
    pl.when(chip == 0)(lambda: co_ref.__setitem__(4, c_ref[2]))
    set_mask(mask_ref)
    vt_ref[:, HD:, :] = jnp.ones((HEADS, VROWS - HD, ALL * BLK), BF16)
    sum_up(0)
    for k in offsets:
        gather(0, k).start()
    for kind in (1, 2):
        for k in offsets:
            scatter(kind, k).start()
    total = pp_ref[...]
    for k in offsets:
        small(k).wait_recv()
        total = total + pslot_ref[k]
    for row in range(SMALL):
        for part in range(2):
            line = jnp.broadcast_to(total[2 * row + part : 2 * row + part + 1, :], (128, 128))
            small_ref[row * D + part * 128 : row * D + (part + 1) * 128, :] = line.T
    shared(2).wait_recv()
    shared(3).start()
    for o in (2, 3, 1):
        own(o).wait_recv()
    shared(1).wait_recv()
    for k in offsets:
        gather(0, k).wait_recv()
    side(0, 0).start()
    side(0, 1).start()
    for o in (2, 3, 1):
        target(o).start()
    pl.when(chip == 0)(lambda: target_shared(2).start())
    pl.when(chip == 1)(lambda: target_shared(3).start())
    pl.when(chip == 1)(lambda: target_shared(1).start())
    shared(3).wait_recv()

    def begin(j, carry):
        xt = xo_ref[j].T
        xt_ref[j] = xt
        unit_values, _ = standardize(xt.astype(F32))
        a_ref[j] = (unit_values * param(small_ref, 0) + param(small_ref, 1)).astype(BF16)
        return carry

    lax.fori_loop(0, ALL, begin, 0)
    side(0, 0).wait_recv()
    side(0, 2).start()
    side(0, 1).wait_recv()
    side(0, 2).wait_recv()
    for t in range(3):
        wt_ref[t * D : (t + 1) * D, :] = matrix(w_ref, 0, t).T
    for kind in (1, 2):
        sum_up(kind)
        for k in offsets:
            gather(kind, k).start()

    def middle(j, carry):
        project(j, a_ref[j], wt_ref, q_ref, kt_ref, vt_ref, k_ref, v_ref)
        return carry

    lax.fori_loop(0, ALL, middle, 0)

    def progress(i):
        @pl.when(i == 3)
        def _():
            for kind in (1, 2):
                for k in offsets:
                    gather(kind, k).wait_recv()
                side(kind, 0).start()
                side(kind, 1).start()

        @pl.when(i == 10)
        def _():
            for kind in (1, 2):
                side(kind, 0).wait_recv()
                side(kind, 2).start()

    attend(core, q_ref, k_ref, vt_ref, o_ref, log_ref, mask_ref, score_ref, prob_ref, progress)
    wot_ref[...] = matrix(w_ref, 0, 3).T
    for kind in (1, 2):
        side(kind, 1).wait_recv()
        side(kind, 2).wait_recv()
    for c in range(4):
        part = slice(c * D, (c + 1) * D)
        wut_ref[part, :] = matrix(w_ref, 1, c).T
        wdt_ref[:, part] = matrix(w_ref, 2, c).T

    def normal(side):
        there = a2_ref.at[OWN + core if side == 0 else OWN + 3 - core]
        return send(there, there, (ns0, ns1), side, {"seq": peers[1]})

    def store(i):
        slot, u = i % 2, ordered(i)
        return (
            pltpu.make_async_copy(hid_buf.at[slot], hid_ref.at[u], hs.at[0, slot]),
            pltpu.make_async_copy(slope_buf.at[slot], slope_ref.at[u], hs.at[1, slot]),
        )

    def feed(i, carry):
        @pl.when(i == 2)
        def _():
            normal(0).start()
            normal(1).start()

        slot = i % 2

        @pl.when(i >= 2)
        def _():
            for copy in store(i - 2):
                copy.wait()

        u = ordered(i)
        place, base = unit_place(u, core)
        x = xt_ref[base + place].astype(F32)
        r, _, _, m = forward_parts(x, o_ref[u], wot_ref, small_ref)
        r_ref[u] = r
        out = r + param(small_ref, 4)
        for c in range(FF // BLK):
            rows = slice(c * BLK, (c + 1) * BLK)
            e = dot(wut_ref[rows, :], m) + param(small_ref, 5 + c)
            hid, slope = gelu_parts(e)
            hid = hid.astype(BF16)
            hid_buf[slot, rows, :] = hid
            slope_buf[slot, rows, :] = slope.astype(BF16)
            out = out + dot(wdt_ref[:, rows], hid)
        sq_ref[u] = squares_of(out)
        z = out + x
        z_ref[u] = z
        unit_values, _ = standardize(z)
        a2_ref[base + place] = (unit_values * param(small_ref, 0) + param(small_ref, 1)).astype(BF16)
        for copy in store(i):
            copy.start()
        return carry

    lax.fori_loop(0, UNITS, feed, 0)
    for i in (UNITS - 2, UNITS - 1):
        for copy in store(i):
            copy.wait()
    normal(0).wait()
    normal(1).wait()
    for o in (2, 3, 1):
        target(o).wait()
        own(o).wait_send()
        shared(o).wait_send()

    @pl.when(chip == 0)
    def _():
        target_shared(2).wait_send()
        target_shared(3).wait_recv()

    @pl.when(chip == 1)
    def _():
        target_shared(3).wait_send()
        target_shared(1).wait_send()
        target_shared(2).wait_recv()
        target_shared(1).wait_recv()

    for kind in range(3):
        for k in offsets:
            scatter(kind, k).wait_send()
            gather(kind, k).wait_send()
        for which in range(3):
            side(kind, which).wait_send()
    for k in offsets:
        small(k).wait_send()


VM = pl.BlockSpec(memory_space=pltpu.VMEM)
HB = pl.BlockSpec(memory_space=pltpu.HBM)


def shape_of(shape, dtype=BF16):
    return jax.ShapeDtypeStruct(shape, dtype)


KEYS = [
    shape_of((HEADS, HD, ALL * BLK)),
    shape_of((2, ALL, BLK, 128)),
    shape_of((2, ALL, BLK, 128)),
]
ATTEND_SCRATCH = [
    pltpu.VMEM((BLK, BLK), F32),
    pltpu.VMEM((2, OWN, BLK, BLK), F32),
    pltpu.VMEM((2, OWN * BLK, BLK), BF16),
]
BACK_SCRATCH = [
    pltpu.VMEM((BLK, BLK), F32),
    pltpu.VMEM((2, OWN * BLK, BLK), BF16),
    pltpu.VMEM((2, OWN * BLK, BLK), BF16),
    pltpu.VMEM((HEADS, HD, ALL * BLK), F32),
    pltpu.VMEM((HEADS, HD, ALL * BLK), F32),
    pltpu.VMEM((2, OWN, BLK, BLK), BF16),
    pltpu.VMEM((2, 2, BLK, BLK), BF16),
    *pair_of_sems((2, 2)),
]


def stage_call(body, name, args, outs, scratch, mib, flops, hbm_in=(), hbm_out=(), **comm):
    return pl.pallas_call(
        body,
        in_specs=[HB if i in hbm_in else VM for i in range(len(args))],
        out_specs=[HB if i in hbm_out else VM for i in range(len(outs))],
        out_shape=outs,
        scratch_shapes=scratch,
        compiler_params=pltpu.CompilerParams(vmem_limit_bytes=mib << 20, has_side_effects=bool(comm), **comm),
        cost_estimate=cost(flops, 1 << 20),
        name=name,
    )(*args)


def first_stage(n, pk, pp, x, c):
    rows = D // n
    tile, eight = (UNITS, BLK, BLK), (ALL, BLK, BLK)
    outs = [shape_of(eight), shape_of(eight), shape_of(eight)] + KEYS
    outs += [shape_of(tile), shape_of((UNITS, 2, 8, BLK), F32), shape_of(tile, F32)]
    outs += [shape_of((UNITS, FF, BLK)), shape_of((UNITS, FF, BLK)), shape_of(tile, F32), shape_of(eight)]
    outs += [shape_of((UNITS, 8, BLK), F32), shape_of((3 * D, D)), shape_of((D, D)), shape_of((FF, D))]
    outs += [shape_of((D, FF)), shape_of((SMALL * D, 128), F32), shape_of((3, 4, n, rows, D)), shape_of(tile)]
    scratch = [pltpu.VMEM((HEADS, VROWS, ALL * BLK), BF16)] + ATTEND_SCRATCH
    scratch += [
        pltpu.VMEM(eight, BF16),
        pltpu.VMEM((3, n, rows, D), BF16),
        pltpu.VMEM((n, 24, 128), F32),
        pltpu.VMEM((3, rows, D), BF16),
        *pair_of_sems((3, n)),
        *pair_of_sems((3, n)),
        *pair_of_sems((n,)),
        *pair_of_sems((3, 3)),
        *pair_of_sems((4, 2)),
        *pair_of_sems((8,)),
        *pair_of_sems((2,)),
        pltpu.VMEM((2, FF, BLK), BF16),
        pltpu.VMEM((2, FF, BLK), BF16),
        pltpu.SemaphoreType.DMA((2, 2)),
    ]
    return stage_call(
        partial(first_stage_body, n), "first_stage", [pk, pp, x, c], outs, scratch, FIRST_MIB, 8e9, hbm_out=(9, 10),
        collective_id=0,
    )


def feed_back_tail(
    u, g, gy, r_unit, r_inv, m, o, small_ref, parts, w_ref, gr_ref, go_ref, gd_acc, gu_acc, go_acc, tail_acc
):
    tail_acc[2 * D : 3 * D, :] += fold(gy.astype(F32))
    gm = jnp.zeros((D, BLK), F32)
    for c in range(FF // BLK):
        rows = slice(c * BLK, (c + 1) * BLK)
        hid, slope = parts(c)
        gd_acc[rows, :] += dot_nt(hid, gy)
        ge = (dot(matrix(w_ref, 2, c), gy) * slope).astype(BF16)
        gu_acc[:, rows] += dot_nt(m, ge)
        tail_acc[3 * D + c * BLK : 3 * D + (c + 1) * BLK, :] += fold(ge.astype(F32))
        gm = gm + dot(matrix(w_ref, 1, c), ge)
    tail_acc[0:D, :] += fold(gm * r_unit)
    tail_acc[D : 2 * D, :] += fold(gm)
    gr = g + standardize_back(gm * param(small_ref, 2), r_unit, r_inv)
    gr_ref[u] = gr
    ga = gr.astype(BF16)
    go_acc[...] += dot_nt(o, ga)
    go_ref[u] = dot(matrix(w_ref, 0, 3), ga).astype(BF16)


TAIL = 3 * D + FF


def second_stage_body(
    a_ref, z_ref, cot_ref, w_ref, wt_ref, wot_ref, wut_ref, wdt_ref, small_ref,
    final_ref, sq_ref, gr_ref, gd_acc, gu_acc, go_acc, tail_acc, dq_ref, dk_ref, dv_ref,
    q_ref, kt_ref, k_ref, v_ref, vt_ref, o_ref, log_ref, go_ref, score_ref, hid_buf, slope_buf,
    mask_ref, prob_ref, ds_ref, dk_acc, dv_acc, part_ref, got_ref, ds0, ds1,
):
    seq = lax.axis_index("seq")
    core = seq % 2
    peer = peers_of(seq)[1]
    greet(1, 0, [peer], False)
    set_mask(mask_ref)
    vt_ref[:, HD:, :] = jnp.ones((HEADS, VROWS - HD, ALL * BLK), BF16)
    for acc in (gd_acc, gu_acc, go_acc, tail_acc):
        acc[...] = jnp.zeros_like(acc)

    def begin(j, carry):
        project(j, a_ref[j], wt_ref, q_ref, kt_ref, vt_ref, k_ref, v_ref)
        return carry

    lax.fori_loop(0, ALL, begin, 0)
    attend(core, q_ref, k_ref, vt_ref, o_ref, log_ref, mask_ref, score_ref, prob_ref)

    def feed(u, carry):
        r, r_unit, r_inv, m = forward_parts(z_ref[u], o_ref[u], wot_ref, small_ref)
        out = r + param(small_ref, 4)
        for c in range(FF // BLK):
            rows = slice(c * BLK, (c + 1) * BLK)
            e = dot(wut_ref[rows, :], m) + param(small_ref, 5 + c)
            hid, slope = gelu_parts(e)
            hid = hid.astype(BF16)
            hid_buf[rows, :] = hid
            slope_buf[rows, :] = slope
            out = out + dot(wdt_ref[:, rows], hid)
        sq_ref[u] = squares_of(out)
        final_ref[u] = out.T.astype(BF16)
        gy = cot_ref[u].T
        feed_back_tail(
            u, gy.astype(F32), gy, r_unit, r_inv, m, o_ref[u], small_ref,
            lambda c: (hid_buf[c * BLK : (c + 1) * BLK, :], slope_buf[c * BLK : (c + 1) * BLK, :]),
            w_ref, gr_ref, go_ref, gd_acc, gu_acc, go_acc, tail_acc,
        )
        return carry

    lax.fori_loop(0, UNITS, feed, 0)
    attend_back(
        core, q_ref, k_ref, kt_ref, v_ref, go_ref, o_ref, log_ref, dq_ref, dk_ref, dv_ref, mask_ref, prob_ref, ds_ref, dk_acc, dv_acc,
        part_ref, got_ref, ds0, ds1, peer,
    )


def second_stage(a, z, cot, w, wt, wot, wut, wdt, small):
    tile, eight = (UNITS, BLK, BLK), (ALL, BLK, BLK)
    outs = [shape_of(tile), shape_of((UNITS, 8, BLK), F32), shape_of(tile, F32), shape_of((FF, D), F32)]
    outs += [shape_of((D, FF), F32), shape_of((D, D), F32), shape_of((TAIL, 128), F32), shape_of(tile)]
    outs += [shape_of(tile), shape_of(tile)]
    scratch = [pltpu.VMEM(eight, BF16)] + [pltpu.VMEM(s.shape, s.dtype) for s in KEYS]
    scratch += [pltpu.VMEM((HEADS, VROWS, ALL * BLK), BF16), pltpu.VMEM(tile, BF16)]
    scratch += [pltpu.VMEM((UNITS, 2, 8, BLK), F32), pltpu.VMEM(tile, BF16), ATTEND_SCRATCH[1]]
    scratch += [pltpu.VMEM((FF, BLK), BF16), pltpu.VMEM((FF, BLK), F32)] + BACK_SCRATCH
    return stage_call(
        second_stage_body, "second_stage", [a, z, cot, w, wt, wot, wut, wdt, small], outs, scratch, SECOND_MIB, 20e9,
        collective_id=1,
    )


def project_weights(a, dq, dk, dv, gqkv_acc):
    gqkv_acc[0] += dot_nt(a, dq)
    gqkv_acc[1] += dot_nt(a, dk)
    gqkv_acc[2] += dot_nt(a, dv)


def project_back(z, dq, dk, dv, gr, small_ref, w_ref, head_acc):
    grad = dot(matrix(w_ref, 0, 0), dq) + dot(matrix(w_ref, 0, 1), dk) + dot(matrix(w_ref, 0, 2), dv)
    unit_values, inverse = standardize(z)
    head_acc[0:D, :] += fold(grad * unit_values)
    head_acc[D : 2 * D, :] += fold(grad)
    return gr + standardize_back(grad * param(small_ref, 0), unit_values, inverse)


def third_stage_body(
    n, dq_in, dk_in, dv_in, a2_ref, z_ref, gr_in, hid_ref, slope_ref, r_ref, o_ref, log_ref, q_ref, kt_ref, k_ref, v_ref,
    small_ref, w_ref, gd_in, gu_in, go_in, tail_in, a_ref, xt_ref, sq1_ref, sq2_ref, f_ref,
    sum_ref, p_ref, fo_ref, io_ref,
    gz_ref, gr_ref, gd_acc, gu_acc, go_acc, tail_acc, gqkv_acc, head_acc, dq_ref, dk_ref, dv_ref, i_ref,
    g_ref, pp_ref, half_ref, quarter_ref, out_ref, mine_ref, slot_ref, chunk_ref, pslot_ref, psum_ref,
    as0, as1, bs0, bs1, ss0, ss1, rs0, rs1, gs0, gs1, ps0, ps1, xs0, xs1,
    go_ref, hid_buf, slope_buf, hs, mask_ref, prob_ref, ds_ref, dk_acc, dv_acc, part_ref, got_ref, ds0, ds1,
):
    dp = lax.axis_index("dp")
    seq = lax.axis_index("seq")
    chip, core = seq // 2, seq % 2
    peers = peers_of(seq)
    offsets = range(1, n)

    def half(kind, j):
        part = peers[1] if j == 0 else peers[3]
        return send(g_ref.at[kind, part], half_ref.at[kind, j], (as0, as1), (kind, j), {"seq": peers[1]})

    def cross(kind):
        return send(out_ref.at[kind], quarter_ref.at[kind], (bs0, bs1), kind, {"seq": peers[2]})

    def scatter(kind, k):
        to = (dp + k) % n
        return send(mine_ref.at[kind, to], slot_ref.at[kind, k], (ss0, ss1), (kind, k), {"dp": to})

    def gather(kind, k):
        return send(chunk_ref.at[kind], sum_ref.at[kind, seq, dp], (rs0, rs1), (kind, k), {"dp": (dp + k) % n})

    def side(kind, which):
        part = peers[2] if which == 2 else seq
        to = peers[2] if which == 0 else peers[1]
        return send(sum_ref.at[kind, part], sum_ref.at[kind, part], (gs0, gs1), (kind, which), {"seq": to})

    def small(k):
        if k == 0:
            return send(pp_ref, pslot_ref.at[0], (ps0, ps1), 0, {"seq": peers[1]})
        if k == 1:
            return send(psum_ref.at[0], pslot_ref.at[1], (ps0, ps1), 1, {"seq": peers[2]})
        return send(psum_ref.at[1], pslot_ref.at[k], (ps0, ps1), k, {"dp": (dp + k - 1) % n})

    def halves(kind):
        half(kind, 0).start()
        half(kind, 1).start()

    def crossing(kind):
        half(kind, 0).wait_recv()
        half(kind, 1).wait_recv()
        out_ref[kind] = (g_ref[kind, peers[2]].astype(F32) + half_ref[kind, 1].astype(F32)).astype(BF16)
        cross(kind).start()

    def scattering(kind):
        cross(kind).wait_recv()
        mine_ref[kind] = (
            g_ref[kind, seq].astype(F32) + half_ref[kind, 0].astype(F32) + quarter_ref[kind].astype(F32)
        ).astype(BF16)
        for k in offsets:
            scatter(kind, k).start()

    def gathering(kind):
        total = mine_ref[kind, dp].astype(F32)
        for k in offsets:
            scatter(kind, k).wait_recv()
            total = total + slot_ref[kind, k].astype(F32)
        chunk_ref[kind] = total.astype(BF16)
        sum_ref[kind, seq, dp] = total.astype(BF16)
        for k in offsets:
            gather(kind, k).start()

    def sharing(kind):
        for k in offsets:
            gather(kind, k).wait_recv()
        side(kind, 0).start()
        side(kind, 1).start()

    def passing(kind):
        side(kind, 0).wait_recv()
        side(kind, 2).start()

    def settled(kind):
        side(kind, 1).wait_recv()
        side(kind, 2).wait_recv()

    own = 3 * chip + core

    def move(which, o, source_ref, target_ref):
        return send(source_ref.at[peers[o]], target_ref.at[own], (xs0, xs1), (which, o), {"seq": peers[o]})

    def move_shared(which, o, source_ref, target_ref):
        source = source_ref.at[4 if o == 2 else 5]
        return send(source, target_ref.at[2 if o == 3 else 5], (xs0, xs1), (which, 4 + o), {"seq": peers[o]})

    def start_moves(which, source_ref, target_ref):
        pl.when(chip == 0)(lambda: move_shared(which, 3, source_ref, target_ref).start())
        pl.when(chip == 1)(lambda: move_shared(which, 2, source_ref, target_ref).start())
        pl.when(chip == 1)(lambda: move_shared(which, 1, source_ref, target_ref).start())
        for o in (2, 3, 1):
            move(which, o, source_ref, target_ref).start()
        target_ref[own] = source_ref[seq]
        pl.when(chip == 0)(lambda: target_ref.__setitem__(2, source_ref[4]))

    def finish_moves(which, source_ref, target_ref):
        @pl.when(chip == 0)
        def _():
            move_shared(which, 3, source_ref, target_ref).wait_send()
            move_shared(which, 2, source_ref, target_ref).wait_recv()

        @pl.when(chip == 1)
        def _():
            move_shared(which, 2, source_ref, target_ref).wait_send()
            move_shared(which, 1, source_ref, target_ref).wait()
            move_shared(which, 3, source_ref, target_ref).wait_recv()

        for o in (2, 3, 1):
            move(which, o, source_ref, target_ref).wait()

    def fetch(u):
        slot = u % 2
        return (
            pltpu.make_async_copy(hid_ref.at[u], hid_buf.at[slot], hs.at[0, slot]),
            pltpu.make_async_copy(slope_ref.at[u], slope_buf.at[slot], hs.at[1, slot]),
        )

    split = lambda values: values.astype(BF16).reshape(g_ref.shape[2:])
    for copy in fetch(0):
        copy.start()
    greet(n, dp, [peers[1], peers[2], peers[3]], True)
    start_moves(0, f_ref, fo_ref)
    set_mask(mask_ref)
    gqkv_acc[...] = jnp.zeros_like(gqkv_acc)
    head_acc[...] = jnp.zeros_like(head_acc)
    for acc, given in ((gd_acc, gd_in), (gu_acc, gu_in), (go_acc, go_in), (tail_acc, tail_in)):
        acc[...] = given[...]

    def feed(u, carry):
        @pl.when(u < UNITS - 1)
        def _():
            for copy in fetch(u + 1):
                copy.start()

        for copy in fetch(u):
            copy.wait()
        slot = u % 2
        place, base = unit_place(u, core)
        project_weights(a2_ref[base + place], dq_in[u], dk_in[u], dv_in[u], gqkv_acc)
        g = project_back(z_ref[u], dq_in[u], dk_in[u], dv_in[u], gr_in[u], small_ref, w_ref, head_acc)
        gz_ref[u] = g
        r_unit, r_inv = standardize(r_ref[u])
        m = (r_unit * param(small_ref, 2) + param(small_ref, 3)).astype(BF16)
        feed_back_tail(
            u, g, g.astype(BF16), r_unit, r_inv, m, o_ref[u], small_ref,
            lambda c: (
                hid_buf[slot, c * BLK : (c + 1) * BLK, :],
                slope_buf[slot, c * BLK : (c + 1) * BLK, :].astype(F32),
            ),
            w_ref, gr_ref, go_ref, gd_acc, gu_acc, go_acc, tail_acc,
        )
        return carry

    lax.fori_loop(0, UNITS, feed, 0)
    for c in range(4):
        g_ref[1, c] = split(gu_acc[:, c * D : (c + 1) * D])
        g_ref[2, c] = split(gd_acc[c * D : (c + 1) * D, :])
    halves(1)
    halves(2)

    def progress(i):
        @pl.when(i == 1)
        def _():
            crossing(1)
            crossing(2)

        @pl.when(i == 6)
        def _():
            scattering(1)
            scattering(2)

    attend_back(
        core, q_ref, k_ref, kt_ref, v_ref, go_ref, o_ref, log_ref, dq_ref, dk_ref, dv_ref, mask_ref, prob_ref, ds_ref, dk_acc, dv_acc,
        part_ref, got_ref, ds0, ds1, peers[1], progress,
    )
    gathering(1)
    gathering(2)

    def early(u, carry):
        place, base = unit_place(u, core)
        project_weights(a_ref[base + place], dq_ref[u], dk_ref[u], dv_ref[u], gqkv_acc)
        return carry

    lax.fori_loop(0, UNITS, early, 0)
    for t in range(3):
        g_ref[0, t] = split(gqkv_acc[t])
    g_ref[0, 3] = split(go_acc[...])
    halves(0)

    def end(u, carry):
        pl.when(u == 1)(lambda: crossing(0))
        place, base = unit_place(u, core)
        g = project_back(
            xt_ref[base + place].astype(F32), dq_ref[u], dk_ref[u], dv_ref[u], gr_ref[u], small_ref, w_ref, head_acc
        )
        i_ref[u] = (g + gz_ref[u]).T.astype(BF16)
        return carry

    lax.fori_loop(0, UNITS, end, 0)
    start_moves(1, i_ref, io_ref)
    for row in range(SMALL):
        for part in range(2):
            ref, first = (head_acc, row) if row < 2 else (tail_acc, row - 2)
            first = first * D + part * 128
            pp_ref[2 * row + part : 2 * row + part + 1, :] = jnp.sum(ref[first : first + 128, :].T, axis=0, keepdims=True)
    sequences = 6 * n
    place = lax.broadcasted_iota(jnp.int32, (6, 128), 0) * 128 + lax.broadcasted_iota(jnp.int32, (6, 128), 1)
    stats = jnp.zeros((6, 128), F32)
    for i, ref in enumerate((sq1_ref, sq2_ref)):
        lines = [jnp.sum(ref[u], axis=0, keepdims=True) for u in range(UNITS)]
        mine = jnp.sum(lines[0] + lines[1] + lines[2] + lines[3], axis=1, keepdims=True)
        shared = jnp.sum(lines[4] + lines[5], axis=1, keepdims=True)
        start = i * sequences + 6 * dp + 3 * chip
        stats = jnp.where(place == start + core, jnp.broadcast_to(mine, (6, 128)), stats)
        stats = jnp.where(place == start + 2, jnp.broadcast_to(shared, (6, 128)), stats)
    pp_ref[18:24, :] = stats
    small(0).start()
    scattering(0)
    small(0).wait_recv()
    psum_ref[0] = pp_ref[...] + pslot_ref[0]
    small(1).start()
    small(1).wait_recv()
    psum_ref[1] = psum_ref[0] + pslot_ref[1]
    for k in offsets:
        small(1 + k).start()
    sharing(1)
    sharing(2)
    gathering(0)
    passing(1)
    passing(2)
    total = psum_ref[1]
    for k in offsets:
        small(1 + k).wait_recv()
        total = total + pslot_ref[1 + k]
    p_ref[...] = total
    sharing(0)
    settled(1)
    settled(2)
    passing(0)
    settled(0)
    finish_moves(0, f_ref, fo_ref)
    finish_moves(1, i_ref, io_ref)
    for kind in range(3):
        half(kind, 0).wait_send()
        half(kind, 1).wait_send()
        cross(kind).wait_send()
        for k in offsets:
            scatter(kind, k).wait_send()
            gather(kind, k).wait_send()
        for which in range(3):
            side(kind, which).wait_send()
    for k in range(n + 1):
        small(k).wait_send()


def third_stage(n, *args):
    rows = D // n
    tile = (UNITS, BLK, BLK)
    quarter = (3, n, rows, D)
    outs = [shape_of((3, 4, n, rows, D)), shape_of((24, 128), F32), shape_of(tile), shape_of(tile)]
    scratch = [
        pltpu.VMEM(tile, F32),
        pltpu.VMEM(tile, F32),
        pltpu.VMEM((FF, D), F32),
        pltpu.VMEM((D, FF), F32),
        pltpu.VMEM((D, D), F32),
        pltpu.VMEM((TAIL, 128), F32),
        pltpu.VMEM((3, D, D), F32),
        pltpu.VMEM((2 * D, 128), F32),
        pltpu.VMEM(tile, BF16),
        pltpu.VMEM(tile, BF16),
        pltpu.VMEM(tile, BF16),
        pltpu.VMEM(tile, BF16),
        pltpu.VMEM((3, 4, n, rows, D), BF16),
        pltpu.VMEM((24, 128), F32),
        pltpu.VMEM((3, 2, n, rows, D), BF16),
        pltpu.VMEM(quarter, BF16),
        pltpu.VMEM(quarter, BF16),
        pltpu.VMEM(quarter, BF16),
        pltpu.VMEM(quarter, BF16),
        pltpu.VMEM((3, rows, D), BF16),
        pltpu.VMEM((1 + n, 24, 128), F32),
        pltpu.VMEM((2, 24, 128), F32),
        *pair_of_sems((3, 2)),
        *pair_of_sems((3,)),
        *pair_of_sems((3, n)),
        *pair_of_sems((3, n)),
        *pair_of_sems((3, 3)),
        *pair_of_sems((1 + n,)),
        *pair_of_sems((2, 8)),
        pltpu.VMEM(tile, BF16),
        pltpu.VMEM((2, FF, BLK), BF16),
        pltpu.VMEM((2, FF, BLK), BF16),
        pltpu.SemaphoreType.DMA((2, 2)),
        *BACK_SCRATCH,
    ]
    return stage_call(
        partial(third_stage_body, n), "third_stage", args, outs, scratch, THIRD_MIB, 20e9, hbm_in=(6, 7), collective_id=2
    )


FIRST_MIB, SECOND_MIB, THIRD_MIB, ADAM_MIB = 38, 22, 31, 58


def owner_scalars(owner_ref):
    sizes = [D * D] * 4 + [D * FF, FF * D, SMALL * D]
    starts = []
    for t in range(7):
        offset = jnp.int32(0)
        for u in range(t):
            offset = offset + jnp.where(owner_ref[u] == owner_ref[t], sizes[u], 0).astype(jnp.int32)
        starts.append(offset)
    return starts


def pack_body(owner_ref, row_ref, w_ref, p_ref):
    dp = lax.axis_index("dp")
    seq = lax.axis_index("seq")
    starts = owner_scalars(owner_ref)
    square = jnp.where(seq == 0, starts[0], jnp.where(seq == 1, starts[1], jnp.where(seq == 2, starts[2], starts[3])))
    plans = (
        (owner_ref[seq], square // 128, 2),
        (owner_ref[4], starts[4] // 128 + 2 * seq, FF // 128),
        (owner_ref[5], starts[5] // 128 + 2 * D * seq, 2),
    )
    for kind, (owner, base, stride) in enumerate(plans):
        keep = jnp.where(owner == dp, 1.0, 0.0).astype(F32)
        for side in range(2):
            values = row_ref[pl.ds(base + side, D, stride=stride), :]
            w_ref[kind, :, side * 128 : (side + 1) * 128] = (values * keep).astype(BF16)
    keep = jnp.where(owner_ref[6] == dp, 1.0, 0.0).astype(F32)
    values = row_ref[pl.ds(pl.multiple_of(starts[6] // 128, 8), 24), :] * keep
    rows = lax.broadcasted_iota(jnp.int32, (24, 128), 0)
    p_ref[...] = jnp.where(rows < 2 * SMALL, values, 0.0)


def pack(owner_list, row):
    return pl.pallas_call(
        pack_body,
        in_specs=[pl.BlockSpec(memory_space=pltpu.SMEM), pl.BlockSpec(memory_space=pltpu.VMEM)],
        out_specs=[pl.BlockSpec(memory_space=pltpu.VMEM)] * 2,
        out_shape=[jax.ShapeDtypeStruct((3, D, D), BF16), jax.ShapeDtypeStruct((24, 128), F32)],
        compiler_params=pltpu.CompilerParams(vmem_limit_bytes=20 << 20),
        cost_estimate=cost(1, 3 << 20),
        name="pack",
    )(owner_list, row)


ROWS = D * D // 128


def adam_body(owner_ref, g_ref, p_ref, f_ref, i_ref, m_ref, v_ref, w_ref, m_out, v_out, w_out, f_out, i_out, grad_ref):
    dp = lax.axis_index("dp")
    block = pl.program_id(0)
    starts = owner_scalars(owner_ref)
    counts = [1, 1, 1, 1, 4, 4, 1]
    rate = jnp.float32(D ** (-0.5))
    decay = jnp.float32(0.1)
    limit = jnp.int32(0)
    f_out[...] = f_ref[...].astype(F32)
    i_out[...] = i_ref[...].astype(F32)
    for t in range(7):
        first = starts[t] // (D * D)
        here = (owner_ref[t] == dp) & (block >= first) & (block < first + counts[t])
        part = block - first
        limit = jnp.where(here, 2 * SMALL if t == 6 else ROWS, limit)
        if t == 5:
            rate = jnp.where(here, FF ** (-0.5), rate)
        if t == 6:
            rate = jnp.where(here, 0.5, rate)
            decay = jnp.where(here, 0.0, decay)

        @pl.when(here)
        def _(t=t, part=part):
            if t == 6:
                grad_ref[0:24, :] = p_ref[...]
            elif t == 4:
                for c in range(4):
                    piece = g_ref[4 + c, pl.ds(pl.multiple_of(part * 64, 64), 64), :].astype(F32)
                    for side in range(2):
                        grad_ref[pl.ds(2 * c + side, 64, stride=8), :] = piece[:, side * 128 : (side + 1) * 128]
            else:
                for r in range(4):
                    piece = g_ref[8 + part if t == 5 else t, r * 64 : (r + 1) * 64, :].astype(F32)
                    for side in range(2):
                        grad_ref[pl.ds(r * 128 + side, 64, stride=2), :] = piece[:, side * 128 : (side + 1) * 128]

    @pl.when(limit == 0)
    def _():
        for out in (m_out, v_out, w_out):
            out[...] = jnp.zeros_like(out)

    @pl.when(limit > 0)
    def _():
        scale = 1.0 / (1.0 - 0.5**STEP)
        for r in range(0, ROWS, PIECE):
            rows = slice(r, r + PIECE)
            grad = grad_ref[rows, :]
            valid = lax.broadcasted_iota(jnp.int32, (PIECE, 128), 0) + r < limit
            first_new = 0.5 * m_ref[rows, :] + 0.5 * grad
            second_new = 0.5 * v_ref[rows, :] + 0.5 * grad * grad
            old = w_ref[rows, :]
            update = first_new * scale / (jnp.sqrt(second_new * scale) + adam_eps) + decay * old
            m_out[rows, :] = jnp.where(valid, first_new, 0.0)
            v_out[rows, :] = jnp.where(valid, second_new, 0.0)
            w_out[rows, :] = jnp.where(valid, old - rate * update, 0.0)


PIECE = 64


def adam(owner_list, g, p, f, i, m, v, w):
    blocks = m.shape[0] // ROWS
    tile = pl.BlockSpec((ROWS, 128), lambda b, t: (b, 0))
    states = pl.BlockSpec((f.shape[0] // blocks, D), lambda b, t: (b, 0))
    out = jax.ShapeDtypeStruct(m.shape, F32)
    state = jax.ShapeDtypeStruct(f.shape, F32)
    whole = pl.BlockSpec(memory_space=pltpu.VMEM)
    spec = pltpu.PrefetchScalarGridSpec(
        num_scalar_prefetch=1,
        grid=(blocks,),
        in_specs=[whole, whole, states, states, tile, tile, tile],
        out_specs=[tile, tile, tile, states, states],
        scratch_shapes=[pltpu.VMEM((ROWS, 128), F32)],
    )
    return pl.pallas_call(
        adam_body,
        grid_spec=spec,
        out_shape=[out, out, out, state, state],
        compiler_params=params_of(mib=ADAM_MIB),
        cost_estimate=cost(20 * 524288, 14 << 20),
        name="adam",
    )(owner_list, g, p, f, i, m, v, w)


def per_device(inputs, cotangent, owner_list, master_rows, moment1_rows, moment2_rows):
    n = lax.axis_size("dp")
    rows = D // n
    flat = [r.reshape(-1, 128) for r in (master_rows, moment1_rows, moment2_rows)]
    pk, pp = pack(owner_list, flat[0])
    (xt, a1, q1, kt1, k1, v1, o1, log1, r1, hid, slope, z2, a2, sq1, wt, wot, wut, wdt, small, w, cot) = first_stage(
        n, pk.reshape(3, n, rows, D), pp, inputs, cotangent
    )
    final, sq2, gr, gd, gu, gout, tail, dq, dk, dv = second_stage(a2, z2, cot, w, wt, wot, wut, wdt, small)
    g, p, final, grad = third_stage(
        n, dq, dk, dv, a2, z2, gr, hid, slope, r1, o1, log1, q1, kt1, k1, v1, small, w, gd, gu, gout, tail,
        a1, xt, sq1, sq2, final,
    )
    states = [r.reshape(-1, D) for r in (final, grad)]
    m_new, v_new, w_new, final, grad = adam(owner_list, g.reshape(12, D, D), p, *states, flat[1], flat[2], flat[0])
    sequences = inputs.shape[0] * n
    entries = inputs.shape[1] * lax.axis_size("seq") * D
    squares = p[18:].reshape(-1)[: 2 * sequences].reshape(2, sequences)
    stats = jnp.sqrt(squares / entries + stat_eps)
    back = lambda r: r.reshape(master_rows.shape)
    return (final.reshape(inputs.shape), grad.reshape(inputs.shape), stats, back(m_new), back(v_new), back(w_new))


def solution(mesh):
    placed = (P("dp", "seq", None), P("dp", "seq", None), P(), P("dp", None), P("dp", None), P("dp", None))
    return jax.shard_map(
        per_device,
        mesh=mesh,
        in_specs=placed,
        out_specs=(P("dp", "seq", None), P("dp", "seq", None), P(), P("dp", None), P("dp", None), P("dp", None)),
        check_vma=False,
    )
```

time: 192 us -> 183 us (0.953)
  Pallas kernels: 182 us -> 172 us
  local copies, waits for them, and re-layouts: 5.34 us -> 8.75 us
  other arithmetic: 3.15 us -> 0.58 us
    pallas_call x9 -> x4, Pallas kernels: 181 us -> 172 us  [the longest x3 161 us: stage_call(): pl.pallas_call(body, in_specs=[HB if i in hbm_in else VM for i in range(l...]
    unnamed x22, local copies, waits for them, and re-layouts: 5.26 us -> 8.67 us
    convert_element_type x2 -> x0, other arithmetic: 2.57 us -> none  [the longest x1 1.28 us: per_device(): grad.astype(F32)]
where the time goes in v4:
time: 183 us
  Pallas kernels  172 us (94%)
  local copies, waits for them, and re-layouts  8.75 us (5%)
    pallas_call x3, Pallas kernels, stage_call(): pl.pallas_call(body, in_specs=[HB if i in hbm_in else VM for i in range(l...  161 us
    pallas_call x1, Pallas kernels, adam(): pl.pallas_call(adam_body, grid_spec=spec, out_shape=[out, out, out, state...  10.9 us
    unnamed x22, local copies, waits for them, and re-layouts  8.67 us

profile of v4, /device:TPU:0, one launch (start us, length us, event | category | flops | bytes accessed | tf_op | source)
XLA Modules:
  0.0 182.6 jit_solution(6019703802791824775)
XLA Ops:
  0.6 0.0 copy-start
  0.6 1.6 copy-done
  2.2 0.0 copy-start.5
  2.2 0.7 copy-done.5
  2.9 0.0 copy-start.6
  2.9 0.0 copy-start.7
  2.9 0.7 pack.1
  3.6 0.4 copy-done.6
  4.0 0.2 copy-done.7
  4.3 51.7 %first_stage.1 = (bf16[8,256,256]{2,1,0:T(8,128)(2,1)S(1)}, bf16[8,256,256]{2,1,0:T(8,128)(2,1)S(1)}, bf16[8,256,256]{2,1,0:T(8,128)(2,1)S(1)}, bf16[4,64,2048]{...) custom-call(bf16[3,8,32,256]{3,2,1,0:T(8,128)(2,1)S(1)} %bitcast.17,, ...), custom_call_target="tpu_custom_call" | custom-call | flops 8000000000 | bytes 1048576 | tf_op jit(solution)/shard_map/first_stage/pallas_call | solution.py:572
  56.0 0.0 copy-start.8
  56.0 1.4 copy-done.8
  57.4 0.0 copy-start.10
  57.4 1.4 copy-done.10
  58.8 0.0 copy-start.9
  58.8 43.1 %second_stage.1 = (bf16[6,256,256]{2,1,0:T(8,128)(2,1)S(1)}, f32[6,8,256]{2,1,0:T(8,128)S(1)}, f32[6,256,256]{2,1,0:T(8,128)S(1)}, f32[1024,256]{1,0:T(8,128)S(1...) custom-call(bf16[8,256,256]{2,1,0:T(8,128)(2,1)S(1)} %get-tuple-elem, ...), custom_call_target="tpu_custom_call" | custom-call | flops 20000000000 | bytes 1048576 | tf_op jit(solution)/shard_map/second_stage/pallas_call | solution.py:572
  101.9 0.0 copy-done.9
  101.9 66.1 %third_stage.1 = (bf16[3,4,8,32,256]{4,3,2,1,0:T(8,128)(2,1)S(1)}, f32[24,128]{1,0:T(8,128)S(1)}, bf16[6,256,256]{2,1,0:T(8,128)(2,1)S(1)}, bf16[6,256,256]{2,1,0:T(8,128)(2,1)S(1)}) custom-call(bf16[6,256,256]{2,1,0:T(8,128)(2,1)S(1)} %get-tuple-element.59.dq_in, bf16[6,256,256]{2,1,0:T(8,128)(2,1)S(1)} %get-tuple-element.60.dk_in, ...), custom_call_target="tpu_custom_call" | custom-call | flops 20000000000 | bytes 1048576 | tf_op jit(solution)/shard_map/third_stage/pallas_call | solution.py:572
  168.0 0.0 copy-start.1
  168.0 1.2 copy-done.1
  169.2 0.0 copy-start.2
  169.2 0.9 copy-done.2
  170.0 0.0 copy-start.3
  170.0 0.9 copy-done.3
  170.9 0.0 copy-start.4
  170.9 0.1 slice.10
  171.0 0.6 fusion.1
  171.6 0.0 copy-done.4
  171.6 10.9 %adam.1 = (f32[4096,128]{1,0:T(8,128)}, f32[4096,128]{1,0:T(8,128)}, f32[4096,128]{1,0:T(8,128)}, f32[1536,256]{1,0:T(8,128)}, f32[1536,256]{1,0:T(8,128)}) custom-call(s32[7]{0:T(128)} %owner_ref.3, bf16[12,256,256]{2,1,0:T(8,128)(2,1)} %bitcast.14, f32[24,128]{1,0:T(8,128)} %copy-done.4, bf16[1536,256]{1,0:T(8,128)(2,1)} %bitcast.15, ...), custom_call_target="tpu_custom_call" | custom-call | flops 10485760 | bytes 14680064 | tf_op jit(solution)/shard_map/adam/pallas_call | solution.py:1150
  (1 shorter events, 0.0 us)
Async XLA Ops:
  0.6 1.6 copy-start
  2.2 0.7 copy-start.5
  2.9 1.1 copy-start.6
  2.9 1.4 copy-start.7
  56.0 1.4 copy-start.8
  57.4 1.4 copy-start.10
  58.8 43.1 %copy-start.9 = (f32[6,256,256]{2,1,0:T(8,128)S(1)}, f32[6,256,256]{2,1,0:T(8,128)}, u32[]{:S(2)}) copy-start(f32[6,256,256]{2,1,0:T(8,128)} %get-tuple-element.51.z_ref) | copy-start | bytes 4718596
  168.0 1.2 copy-start.1
  169.2 0.9 copy-start.2
  170.0 0.9 copy-start.3
  170.9 0.7 copy-start.4

commit v5 on v4

--- a/solution.py
+++ b/solution.py
@@ -175,6 +175,7 @@
 
 
 SUB = 128
+BSUB = 256
 
 
 def ordered(i):
@@ -185,40 +186,55 @@
     def step(i, carry):
         if progress is not None:
             progress(i)
-        pair, unit = i % 2, ordered(i // 2)
+        unit = ordered(i)
         place, base = unit_place(unit, core)
 
         def branch(last):
-            block = q_ref[base + place, pair_rows(pair), :]
-            for half in range(2):
-                q = head_rows(block, half)
-                top = None
-                for kb in range(last + 1):
-                    for sub in range(BLK // SUB):
-                        rows = slice(sub * SUB, (sub + 1) * SUB)
-                        score = dot(k_ref[pair, base + kb, rows, :], q)
-                        if kb == last:
-                            score = score + mask_ref[rows, :]
-                        score_ref[half, kb, rows, :] = score
-                        peak = groups(score, jnp.maximum)
-                        top = peak if top is None else jnp.maximum(top, peak)
-                top = jnp.max(top, axis=0, keepdims=True)
-                for kb in range(last + 1):
-                    for sub in range(BLK // SUB):
-                        rows = slice(sub * SUB, (sub + 1) * SUB)
-                        weight = jnp.exp(score_ref[half, kb, rows, :] - top)
-                        prob_ref[half, kb * BLK + sub * SUB : kb * BLK + (sub + 1) * SUB, :] = weight.astype(BF16)
-                keys = (last + 1) * BLK
-                out = dot(vt_ref[2 * pair + half, :, lanes(base * BLK, keys)], prob_ref[half, 0:keys, :])
-                total = out[HD : HD + 1]
-                o_ref[unit, pl.ds(pl.multiple_of(pair * 128 + half * HD, HD), HD), :] = (out[0:HD] / total).astype(BF16)
-                log_ref[unit, pair, half : half + 1, :] = top + jnp.log(total)
+            keys = (last + 1) * BLK
+            chunks = [(kb, sub) for kb in range(last + 1) for sub in range(BLK // SUB)]
+            queries = [head_rows(q_ref[base + place, (h // 2) * 128 : (h // 2 + 1) * 128, :], h % 2) for h in range(HEADS)]
+            tops = [None] * HEADS
+            outs = [None] * HEADS
+
+            def scores(h, kb, sub):
+                rows = slice(sub * SUB, (sub + 1) * SUB)
+                score = dot(k_ref[h // 2, base + kb, rows, :], queries[h])
+                if kb == last:
+                    score = score + mask_ref[rows, :]
+                score_ref[h % 2, kb, rows, :] = score
+                peak = groups(score, jnp.maximum)
+                tops[h] = peak if tops[h] is None else jnp.maximum(tops[h], peak)
+
+            def weights(h, kb, sub):
+                rows = slice(sub * SUB, (sub + 1) * SUB)
+                weight = jnp.exp(score_ref[h % 2, kb, rows, :] - tops[h])
+                prob_ref[h % 2, kb * BLK + sub * SUB : kb * BLK + (sub + 1) * SUB, :] = weight.astype(BF16)
+
+            def mixed(h, kb):
+                part = dot(vt_ref[h, :, lanes((base + kb) * BLK, BLK)], prob_ref[h % 2, kb * BLK : (kb + 1) * BLK, :])
+                outs[h] = part if outs[h] is None else outs[h] + part
+
+            for t in range(HEADS + 2):
+                if 0 <= t - 1 < HEADS:
+                    tops[t - 1] = jnp.max(tops[t - 1], axis=0, keepdims=True)
+                for kb, sub in chunks:
+                    if t < HEADS:
+                        scores(t, kb, sub)
+                    if 0 <= t - 1 < HEADS:
+                        weights(t - 1, kb, sub)
+                    if 0 <= t - 2 < HEADS and sub == 0:
+                        mixed(t - 2, kb)
+                if 0 <= t - 2 < HEADS:
+                    h = t - 2
+                    total = outs[h][HD : HD + 1]
+                    o_ref[unit, h * HD : (h + 1) * HD, :] = (outs[h][0:HD] / total).astype(BF16)
+                    log_ref[unit, h // 2, h % 2 : h % 2 + 1, :] = tops[h] + jnp.log(total)
 
         for last in range(OWN):
             pl.when(place == last)(partial(branch, last))
         return carry
 
-    lax.fori_loop(0, 2 * UNITS, step, 0)
+    lax.fori_loop(0, UNITS, step, 0)
 
 
 def attend_back(
@@ -227,7 +243,6 @@
 ):
     dk_acc[...] = jnp.zeros_like(dk_acc)
     dv_acc[...] = jnp.zeros_like(dv_acc)
-
     pairs = ((0, dk_acc, dk_ref), (1, dv_acc, dv_ref))
 
     def piece(acc, j):
@@ -238,7 +253,7 @@
         return send(part_ref.at[which, position], got_ref.at[which, side], (ds0, ds1), (which, side), {"seq": peer})
 
     def step(i, carry):
-        @pl.when(i == 4)
+        @pl.when(i == 2)
         def _():
             for which, acc, _ in pairs:
                 for position in range(OWN):
@@ -249,45 +264,79 @@
 
         if progress is not None:
             progress(i)
-        pair, unit = i % 2, ordered(i // 2)
+        unit = ordered(i)
         place, base = unit_place(unit, core)
 
         def branch(last):
-            block = q_ref[base + place, pair_rows(pair), :]
-            go_block = go_ref[unit, pair_rows(pair), :]
-            o_block = o_ref[unit, pair_rows(pair), :]
-            keys = (last + 1) * BLK
-            for half in range(2):
-                lo, hi = half * HD, (half + 1) * HD
-                q = head_rows(block, half)
-                go = head_rows(go_block, half)
-                q_head = block[lo:hi]
-                go_head = go_block[lo:hi]
-                log_total = log_ref[unit, pair, half : half + 1, :]
-                inner = jnp.sum(go_head.astype(F32) * o_block[lo:hi].astype(F32), axis=0, keepdims=True)
-                for kb in range(last + 1):
-                    for sub in range(BLK // SUB):
-                        rows = slice(sub * SUB, (sub + 1) * SUB)
-                        to = slice(kb * BLK + sub * SUB, kb * BLK + (sub + 1) * SUB)
-                        score = dot(k_ref[pair, base + kb, rows, :], q)
-                        if kb == last:
-                            score = score + mask_ref[rows, :]
-                        weight = jnp.exp(score - log_total)
-                        slope = dot(v_ref[pair, base + kb, rows, :], go)
-                        prob_ref[half, to, :] = weight.astype(BF16)
-                        slope_ref[half, to, :] = (weight * (slope - inner)).astype(BF16)
-                head = 2 * pair + half
-                where = lanes(base * BLK, keys)
-                dv_acc[head, :, where] += dot_nt(go_head, prob_ref[half, 0:keys, :])
-                dk_acc[head, :, where] += dot_nt(q_head, slope_ref[half, 0:keys, :])
-                dq = dot(kt_ref[head, :, where], slope_ref[half, 0:keys, :])
-                dq_ref[unit, pl.ds(pl.multiple_of(pair * 128 + lo, HD), HD), :] = (dq * HD ** (-0.5)).astype(BF16)
+            chunks = [(kb, sub) for kb in range(last + 1) for sub in range(BLK // BSUB)]
+            heads = []
+            for h in range(HEADS):
+                pair = slice((h // 2) * 128, (h // 2 + 1) * 128)
+                block = q_ref[base + place, pair, :]
+                go_block = go_ref[unit, pair, :]
+                mine = slice((h % 2) * HD, (h % 2 + 1) * HD)
+                inner = jnp.sum(
+                    go_block[mine].astype(F32) * o_ref[unit, h * HD : (h + 1) * HD, :].astype(F32), axis=0, keepdims=True
+                )
+                heads.append(
+                    (head_rows(block, h % 2), head_rows(go_block, h % 2), log_ref[unit, h // 2, h % 2 : h % 2 + 1, :], inner)
+                )
+            dqs = [None] * HEADS
+            ready = {}
+
+            def products(h, kb, sub):
+                rows = slice(sub * BSUB, (sub + 1) * BSUB)
+                q, go, _, _ = heads[h]
+                ready[h, kb, sub] = (
+                    dot(k_ref[h // 2, base + kb, rows, :], q),
+                    dot(v_ref[h // 2, base + kb, rows, :], go),
+                )
+
+            def elements(h, kb, sub):
+                rows = slice(sub * BSUB, (sub + 1) * BSUB)
+                to = slice(kb * BLK + sub * BSUB, kb * BLK + (sub + 1) * BSUB)
+                _, _, log_total, inner = heads[h]
+                score, slope = ready.pop((h, kb, sub))
+                if kb == last:
+                    score = score + mask_ref[rows, :]
+                weight = jnp.exp(score - log_total)
+                prob_ref[h % 2, to, :] = weight.astype(BF16)
+                slope_ref[h % 2, to, :] = (weight * (slope - inner)).astype(BF16)
+
+            def gradients(h, kb, which):
+                rows = slice(kb * BLK, (kb + 1) * BLK)
+                where = lanes((base + kb) * BLK, BLK)
+                head = slice(h * HD, (h + 1) * HD)
+                if which == 0:
+                    dv_acc[h, :, where] += dot_nt(go_ref[unit, head, :], prob_ref[h % 2, rows, :])
+                elif which == 1:
+                    dk_acc[h, :, where] += dot_nt(q_ref[base + place, head, :], slope_ref[h % 2, rows, :])
+                else:
+                    part = dot(kt_ref[h, :, where], slope_ref[h % 2, rows, :])
+                    dqs[h] = part if dqs[h] is None else dqs[h] + part
+
+            work = [(h, kb, sub) for h in range(HEADS) for kb, sub in chunks]
+            per = BLK // BSUB
+            products(*work[0])
+            for at, (h, kb, sub) in enumerate(work):
+                if at + 1 < len(work):
+                    products(*work[at + 1])
+                elements(h, kb, sub)
+                if h > 0 and sub == 0:
+                    for which in range(3):
+                        gradients(h - 1, kb, which)
+                if h > 0 and kb == last and sub == per - 1:
+                    dq_ref[unit, (h - 1) * HD : h * HD, :] = (dqs[h - 1] * HD ** (-0.5)).astype(BF16)
+            for kb in range(last + 1):
+                for which in range(3):
+                    gradients(HEADS - 1, kb, which)
+            dq_ref[unit, (HEADS - 1) * HD :, :] = (dqs[HEADS - 1] * HD ** (-0.5)).astype(BF16)
 
         for last in range(OWN):
             pl.when(place == last)(partial(branch, last))
         return carry
 
-    lax.fori_loop(0, 2 * UNITS, step, 0)
+    lax.fori_loop(0, UNITS, step, 0)
     for which, acc, ref in pairs:
         for j in range(OWN):
             ref[j] = piece(acc, j).astype(BF16)
@@ -434,7 +483,7 @@
     lax.fori_loop(0, ALL, middle, 0)
 
     def progress(i):
-        @pl.when(i == 3)
+        @pl.when(i == 2)
         def _():
             for kind in (1, 2):
                 for k in offsets:
@@ -442,7 +491,7 @@
                 side(kind, 0).start()
                 side(kind, 1).start()
 
-        @pl.when(i == 10)
+        @pl.when(i == 5)
         def _():
             for kind in (1, 2):
                 side(kind, 0).wait_recv()
@@ -888,10 +937,8 @@
             crossing(1)
             crossing(2)
 
-        @pl.when(i == 6)
-        def _():
-            scattering(1)
-            scattering(2)
+        pl.when(i == 4)(lambda: scattering(1))
+        pl.when(i == 5)(lambda: scattering(2))
 
     attend_back(
         core, q_ref, k_ref, kt_ref, v_ref, go_ref, o_ref, log_ref, dq_ref, dk_ref, dv_ref, mask_ref, prob_ref, ds_ref, dk_acc, dv_acc,
@@ -913,6 +960,7 @@
 
     def end(u, carry):
         pl.when(u == 1)(lambda: crossing(0))
+        pl.when(u == 4)(lambda: sharing(1))
         place, base = unit_place(u, core)
         g = project_back(
             xt_ref[base + place].astype(F32), dq_ref[u], dk_ref[u], dv_ref[u], gr_ref[u], small_ref, w_ref, head_acc
@@ -947,7 +995,6 @@
     psum_ref[1] = psum_ref[0] + pslot_ref[1]
     for k in offsets:
         small(1 + k).start()
-    sharing(1)
     sharing(2)
     gathering(0)
     passing(1)

time: 183 us -> 173 us (0.945)
  Pallas kernels: 172 us -> 162 us
    pallas_call x3, Pallas kernels: 161 us -> 151 us  [stage_call(): pl.pallas_call(body, in_specs=[HB if i in hbm_in else VM for i in range(l...]
where the time goes in v5:
time: 173 us; the launch traced here: 172 us
  Pallas kernels  162 us (94%)
  local copies, waits for them, and re-layouts  8.75 us (5%)
    pallas_call x3, Pallas kernels, stage_call(): pl.pallas_call(body, in_specs=[HB if i in hbm_in else VM for i in range(l...  151 us
    pallas_call x1, Pallas kernels, adam(): pl.pallas_call(adam_body, grid_spec=spec, out_shape=[out, out, out, state...  10.7 us
    unnamed x22, local copies, waits for them, and re-layouts  8.67 us

profile of v5, /device:TPU:0, one launch (start us, length us, event | category | flops | bytes accessed | tf_op | source)
XLA Modules:
  0.0 172.2 jit_solution(10999283459880653567)
XLA Ops:
  0.6 0.0 copy-start
  0.6 1.6 copy-done
  2.2 0.0 copy-start.5
  2.2 0.7 copy-done.5
  2.9 0.0 copy-start.6
  2.9 0.0 copy-start.7
  2.9 0.7 pack.1
  3.6 0.4 copy-done.6
  4.0 0.2 copy-done.7
  4.3 50.1 %first_stage.1 = (bf16[8,256,256]{2,1,0:T(8,128)(2,1)S(1)}, bf16[8,256,256]{2,1,0:T(8,128)(2,1)S(1)}, bf16[8,256,256]{2,1,0:T(8,128)(2,1)S(1)}, bf16[4,64,2048]{...) custom-call(bf16[3,8,32,256]{3,2,1,0:T(8,128)(2,1)S(1)} %bitcast.17,, ...), custom_call_target="tpu_custom_call" | custom-call | flops 8000000000 | bytes 1048576 | tf_op jit(solution)/shard_map/first_stage/pallas_call | solution.py:621
  54.4 0.0 copy-start.8
  54.4 1.4 copy-done.8
  55.8 0.0 copy-start.10
  55.8 1.4 copy-done.10
  57.2 0.0 copy-start.9
  57.2 34.5 %second_stage.1 = (bf16[6,256,256]{2,1,0:T(8,128)(2,1)S(1)}, f32[6,8,256]{2,1,0:T(8,128)S(1)}, f32[6,256,256]{2,1,0:T(8,128)S(1)}, f32[1024,256]{1,0:T(8,128)S(1...) custom-call(bf16[8,256,256]{2,1,0:T(8,128)(2,1)S(1)} %get-tuple-elem, ...), custom_call_target="tpu_custom_call" | custom-call | flops 20000000000 | bytes 1048576 | tf_op jit(solution)/shard_map/second_stage/pallas_call | solution.py:621
  91.7 0.0 copy-done.9
  91.7 66.0 %third_stage.1 = (bf16[3,4,8,32,256]{4,3,2,1,0:T(8,128)(2,1)S(1)}, f32[24,128]{1,0:T(8,128)S(1)}, bf16[6,256,256]{2,1,0:T(8,128)(2,1)S(1)}, bf16[6,256,256]{2,1,0:T(8,128)(2,1)S(1)}) custom-call(bf16[6,256,256]{2,1,0:T(8,128)(2,1)S(1)} %get-tuple-element.59.dq_in, bf16[6,256,256]{2,1,0:T(8,128)(2,1)S(1)} %get-tuple-element.60.dk_in, ...), custom_call_target="tpu_custom_call" | custom-call | flops 20000000000 | bytes 1048576 | tf_op jit(solution)/shard_map/third_stage/pallas_call | solution.py:621
  157.8 0.0 copy-start.1
  157.8 1.2 copy-done.1
  158.9 0.0 copy-start.2
  158.9 0.9 copy-done.2
  159.8 0.0 copy-start.3
  159.8 0.9 copy-done.3
  160.7 0.0 copy-start.4
  160.7 0.1 slice.10
  160.8 0.6 fusion.1
  161.4 0.0 copy-done.4
  161.4 10.7 %adam.1 = (f32[4096,128]{1,0:T(8,128)}, f32[4096,128]{1,0:T(8,128)}, f32[4096,128]{1,0:T(8,128)}, f32[1536,256]{1,0:T(8,128)}, f32[1536,256]{1,0:T(8,128)}) custom-call(s32[7]{0:T(128)} %owner_ref.3, bf16[12,256,256]{2,1,0:T(8,128)(2,1)} %bitcast.14, f32[24,128]{1,0:T(8,128)} %copy-done.4, bf16[1536,256]{1,0:T(8,128)(2,1)} %bitcast.15, ...), custom_call_target="tpu_custom_call" | custom-call | flops 10485760 | bytes 14680064 | tf_op jit(solution)/shard_map/adam/pallas_call | solution.py:1197
  (1 shorter events, 0.0 us)
Async XLA Ops:
  0.6 1.6 copy-start
  2.2 0.7 copy-start.5
  2.9 1.1 copy-start.6
  2.9 1.4 copy-start.7
  54.4 1.4 copy-start.8
  55.8 1.4 copy-start.10
  57.2 34.5 %copy-start.9 = (f32[6,256,256]{2,1,0:T(8,128)S(1)}, f32[6,256,256]{2,1,0:T(8,128)}, u32[]{:S(2)}) copy-start(f32[6,256,256]{2,1,0:T(8,128)} %get-tuple-element.51.z_ref) | copy-start | bytes 4718596
  157.8 1.2 copy-start.1
  158.9 0.9 copy-start.2
  159.8 0.9 copy-start.3
  160.7 0.7 copy-start.4

commit v6 on v5

--- a/solution.py
+++ b/solution.py
@@ -362,7 +362,7 @@
     xt_ref, a_ref, q_ref, kt_ref, k_ref, v_ref, o_ref, log_ref, r_ref, hid_ref, slope_ref, z_ref, a2_ref, sq_ref,
     wt_ref, wot_ref, wut_ref, wdt_ref, small_ref, w_ref, co_ref,
     vt_ref, mask_ref, score_ref, prob_ref, xo_ref, slot_ref, pslot_ref, chunk_ref,
-    ss0, ss1, rs0, rs1, ps0, ps1, gs0, gs1, xs0, xs1, cs0, cs1, ns0, ns1, hid_buf, slope_buf, hs,
+    ss0, ss1, rs0, rs1, ps0, ps1, gs0, gs1, xs0, xs1, cs0, cs1, ns0, ns1, hid_buf, slope_buf, hs, ls,
 ):
     dp = lax.axis_index("dp")
     seq = lax.axis_index("seq")
@@ -411,7 +411,38 @@
         chunk_ref[kind] = total.astype(BF16)
         w_ref[kind, seq, dp] = total.astype(BF16)
 
+    def kept():
+        return pltpu.make_async_copy(c_ref.at[2], co_ref.at[4], ls.at[3])
+
+    locals_ = (
+        pltpu.make_async_copy(x_ref.at[3 * chip + core], xo_ref.at[seq], ls.at[0]),
+        pltpu.make_async_copy(x_ref.at[3 * chip + 2], xo_ref.at[OWN + seq], ls.at[1]),
+        pltpu.make_async_copy(c_ref.at[3 * chip + core], co_ref.at[seq], ls.at[2]),
+    )
     offsets = range(1, n)
+
+    def summed(kind):
+        sum_up(kind)
+        for k in offsets:
+            gather(kind, k).start()
+
+    def sharing(kind):
+        for k in offsets:
+            gather(kind, k).wait_recv()
+        side(kind, 0).start()
+        side(kind, 1).start()
+
+    def passing(kind):
+        side(kind, 0).wait_recv()
+        side(kind, 2).start()
+
+    def targets():
+        for o in (2, 3, 1):
+            target(o).start()
+        pl.when(chip == 0)(lambda: target_shared(2).start())
+        pl.when(chip == 1)(lambda: target_shared(3).start())
+        pl.when(chip == 1)(lambda: target_shared(1).start())
+
     greet(n, dp, [peers[1], peers[2], peers[3]], True)
     for k in offsets:
         scatter(0, k).start()
@@ -421,10 +452,9 @@
         own(o).start()
     for k in offsets:
         small(k).start()
-    xo_ref[seq] = x_ref[3 * chip + core]
-    xo_ref[OWN + seq] = x_ref[3 * chip + 2]
-    co_ref[seq] = c_ref[3 * chip + core]
-    pl.when(chip == 0)(lambda: co_ref.__setitem__(4, c_ref[2]))
+    for copy in locals_:
+        copy.start()
+    pl.when(chip == 0)(lambda: kept().start())
     set_mask(mask_ref)
     vt_ref[:, HD:, :] = jnp.ones((HEADS, VROWS - HD, ALL * BLK), BF16)
     sum_up(0)
@@ -450,12 +480,10 @@
         gather(0, k).wait_recv()
     side(0, 0).start()
     side(0, 1).start()
-    for o in (2, 3, 1):
-        target(o).start()
-    pl.when(chip == 0)(lambda: target_shared(2).start())
-    pl.when(chip == 1)(lambda: target_shared(3).start())
-    pl.when(chip == 1)(lambda: target_shared(1).start())
     shared(3).wait_recv()
+    for copy in locals_:
+        copy.wait()
+    pl.when(chip == 0)(lambda: kept().wait())
 
     def begin(j, carry):
         xt = xo_ref[j].T
@@ -465,37 +493,27 @@
         return carry
 
     lax.fori_loop(0, ALL, begin, 0)
+    summed(1)
     side(0, 0).wait_recv()
     side(0, 2).start()
     side(0, 1).wait_recv()
     side(0, 2).wait_recv()
     for t in range(3):
         wt_ref[t * D : (t + 1) * D, :] = matrix(w_ref, 0, t).T
-    for kind in (1, 2):
-        sum_up(kind)
-        for k in offsets:
-            gather(kind, k).start()
+    summed(2)
 
     def middle(j, carry):
+        pl.when(j == 5)(lambda: sharing(1))
         project(j, a_ref[j], wt_ref, q_ref, kt_ref, vt_ref, k_ref, v_ref)
         return carry
 
     lax.fori_loop(0, ALL, middle, 0)
 
     def progress(i):
-        @pl.when(i == 2)
-        def _():
-            for kind in (1, 2):
-                for k in offsets:
-                    gather(kind, k).wait_recv()
-                side(kind, 0).start()
-                side(kind, 1).start()
-
-        @pl.when(i == 5)
-        def _():
-            for kind in (1, 2):
-                side(kind, 0).wait_recv()
-                side(kind, 2).start()
+        pl.when(i == 2)(lambda: sharing(2))
+        pl.when(i == 3)(targets)
+        pl.when(i == 4)(lambda: passing(1))
+        pl.when(i == 5)(lambda: passing(2))
 
     attend(core, q_ref, k_ref, vt_ref, o_ref, log_ref, mask_ref, score_ref, prob_ref, progress)
     wot_ref[...] = matrix(w_ref, 0, 3).T
@@ -654,9 +672,10 @@
         pltpu.VMEM((2, FF, BLK), BF16),
         pltpu.VMEM((2, FF, BLK), BF16),
         pltpu.SemaphoreType.DMA((2, 2)),
+        pltpu.SemaphoreType.DMA((4,)),
     ]
     return stage_call(
-        partial(first_stage_body, n), "first_stage", [pk, pp, x, c], outs, scratch, FIRST_MIB, 8e9, hbm_out=(9, 10),
+        partial(first_stage_body, n), "first_stage", [pk, pp, x, c], outs, scratch, FIRST_MIB, 8e9, hbm_in=(2, 3), hbm_out=(9, 10),
         collective_id=0,
     )
 
@@ -771,7 +790,7 @@
     sum_ref, p_ref, fo_ref, io_ref,
     gz_ref, gr_ref, gd_acc, gu_acc, go_acc, tail_acc, gqkv_acc, head_acc, dq_ref, dk_ref, dv_ref, i_ref,
     g_ref, pp_ref, half_ref, quarter_ref, out_ref, mine_ref, slot_ref, chunk_ref, pslot_ref, psum_ref,
-    as0, as1, bs0, bs1, ss0, ss1, rs0, rs1, gs0, gs1, ps0, ps1, xs0, xs1,
+    as0, as1, bs0, bs1, ss0, ss1, rs0, rs1, gs0, gs1, ps0, ps1, xs0, xs1, us0, us1, vs0, vs1,
     go_ref, hid_buf, slope_buf, hs, mask_ref, prob_ref, ds_ref, dk_acc, dv_acc, part_ref, got_ref, ds0, ds1,
 ):
     dp = lax.axis_index("dp")
@@ -799,6 +818,13 @@
         to = peers[2] if which == 0 else peers[1]
         return send(sum_ref.at[kind, part], sum_ref.at[kind, part], (gs0, gs1), (kind, which), {"seq": to})
 
+    def chunk(kind):
+        return send(chunk_ref.at[kind], sum_ref.at[kind, seq, dp], (us0, us1), kind, {"seq": peers[2]})
+
+    def again(kind, k):
+        there = sum_ref.at[kind, peers[2], dp]
+        return send(there, there, (vs0, vs1), (kind, k), {"dp": (dp + k) % n})
+
     def small(k):
         if k == 0:
             return send(pp_ref, pslot_ref.at[0], (ps0, ps1), 0, {"seq": peers[1]})
@@ -831,17 +857,30 @@
             total = total + slot_ref[kind, k].astype(F32)
         chunk_ref[kind] = total.astype(BF16)
         sum_ref[kind, seq, dp] = total.astype(BF16)
+        if kind in DOUBLE:
+            chunk(kind).start()
         for k in offsets:
             gather(kind, k).start()
+
+    def doubling(kind):
+        if kind in DOUBLE:
+            chunk(kind).wait_recv()
+            for k in offsets:
+                again(kind, k).start()
 
     def sharing(kind):
         for k in offsets:
             gather(kind, k).wait_recv()
-        side(kind, 0).start()
+        if kind not in DOUBLE:
+            side(kind, 0).start()
         side(kind, 1).start()
 
     def passing(kind):
-        side(kind, 0).wait_recv()
+        if kind in DOUBLE:
+            for k in offsets:
+                again(kind, k).wait_recv()
+        else:
+            side(kind, 0).wait_recv()
         side(kind, 2).start()
 
     def settled(kind):
@@ -861,10 +900,13 @@
         pl.when(chip == 0)(lambda: move_shared(which, 3, source_ref, target_ref).start())
         pl.when(chip == 1)(lambda: move_shared(which, 2, source_ref, target_ref).start())
         pl.when(chip == 1)(lambda: move_shared(which, 1, source_ref, target_ref).start())
-        for o in (2, 3, 1):
-            move(which, o, source_ref, target_ref).start()
+        move(which, 1, source_ref, target_ref).start()
         target_ref[own] = source_ref[seq]
         pl.when(chip == 0)(lambda: target_ref.__setitem__(2, source_ref[4]))
+
+    def more_moves(which, source_ref, target_ref):
+        for o in (2, 3):
+            move(which, o, source_ref, target_ref).start()
 
     def finish_moves(which, source_ref, target_ref):
         @pl.when(chip == 0)
@@ -893,6 +935,7 @@
         copy.start()
     greet(n, dp, [peers[1], peers[2], peers[3]], True)
     start_moves(0, f_ref, fo_ref)
+    more_moves(0, f_ref, fo_ref)
     set_mask(mask_ref)
     gqkv_acc[...] = jnp.zeros_like(gqkv_acc)
     head_acc[...] = jnp.zeros_like(head_acc)
@@ -960,6 +1003,7 @@
 
     def end(u, carry):
         pl.when(u == 1)(lambda: crossing(0))
+        pl.when(u == 3)(lambda: doubling(2))
         pl.when(u == 4)(lambda: sharing(1))
         place, base = unit_place(u, core)
         g = project_back(
@@ -997,6 +1041,8 @@
         small(1 + k).start()
     sharing(2)
     gathering(0)
+    more_moves(1, i_ref, io_ref)
+    doubling(0)
     passing(1)
     passing(2)
     total = psum_ref[1]
@@ -1018,10 +1064,17 @@
         for k in offsets:
             scatter(kind, k).wait_send()
             gather(kind, k).wait_send()
-        for which in range(3):
+        if kind in DOUBLE:
+            chunk(kind).wait_send()
+            for k in offsets:
+                again(kind, k).wait_send()
+        for which in (1, 2) if kind in DOUBLE else range(3):
             side(kind, which).wait_send()
     for k in range(n + 1):
         small(k).wait_send()
+
+
+DOUBLE = (0, 2)
 
 
 def third_stage(n, *args):
@@ -1059,6 +1112,8 @@
         *pair_of_sems((3, 3)),
         *pair_of_sems((1 + n,)),
         *pair_of_sems((2, 8)),
+        *pair_of_sems((3,)),
+        *pair_of_sems((3, n)),
         pltpu.VMEM(tile, BF16),
         pltpu.VMEM((2, FF, BLK), BF16),
         pltpu.VMEM((2, FF, BLK), BF16),

time: 173 us -> 164 us (0.948)
  Pallas kernels: 162 us -> 153 us
    pallas_call x3, Pallas kernels: 151 us -> 141 us  [stage_call(): pl.pallas_call(body, in_specs=[HB if i in hbm_in else VM for i in range(l...]
where the time goes in v6:
time: 164 us; the launch traced here: 163 us
  Pallas kernels  153 us (93%)
  local copies, waits for them, and re-layouts  8.75 us (5%)
    pallas_call x3, Pallas kernels, stage_call(): pl.pallas_call(body, in_specs=[HB if i in hbm_in else VM for i in range(l...  141 us
    pallas_call x1, Pallas kernels, adam(): pl.pallas_call(adam_body, grid_spec=spec, out_shape=[out, out, out, state...  10.9 us
    unnamed x22, local copies, waits for them, and re-layouts  8.67 us

profile of v6, /device:TPU:0, one launch (start us, length us, event | category | flops | bytes accessed | tf_op | source)
XLA Modules:
  0.0 162.7 jit_solution(4012898594685161028)
XLA Ops:
  0.6 0.0 copy-start
  0.6 1.6 copy-done
  2.2 0.0 copy-start.5
  2.2 0.7 copy-done.5
  2.9 0.0 copy-start.6
  2.9 0.0 copy-start.7
  2.9 0.7 pack.1
  3.6 0.4 copy-done.6
  4.0 0.2 copy-done.7
  4.3 47.9 %first_stage.1 = (bf16[8,256,256]{2,1,0:T(8,128)(2,1)S(1)}, bf16[8,256,256]{2,1,0:T(8,128)(2,1)S(1)}, bf16[8,256,256]{2,1,0:T(8,128)(2,1)S(1)}, bf16[4,64,2048]{...) custom-call(bf16[3,8,32,256]{3,2,1,0:T(8,128)(2,1)S(1)} %bitcast.17,, ...), custom_call_target="tpu_custom_call" | custom-call | flops 8000000000 | bytes 1048576 | tf_op jit(solution)/shard_map/first_stage/pallas_call | solution.py:639
  52.1 0.0 copy-start.8
  52.1 1.4 copy-done.8
  53.5 0.0 copy-start.10
  53.5 1.4 copy-done.10
  54.9 0.0 copy-start.9
  54.9 34.5 %second_stage.1 = (bf16[6,256,256]{2,1,0:T(8,128)(2,1)S(1)}, f32[6,8,256]{2,1,0:T(8,128)S(1)}, f32[6,256,256]{2,1,0:T(8,128)S(1)}, f32[1024,256]{1,0:T(8,128)S(1...) custom-call(bf16[8,256,256]{2,1,0:T(8,128)(2,1)S(1)} %get-tuple-elem, ...), custom_call_target="tpu_custom_call" | custom-call | flops 20000000000 | bytes 1048576 | tf_op jit(solution)/shard_map/second_stage/pallas_call | solution.py:639
  89.4 0.0 copy-done.9
  89.4 58.6 %third_stage.1 = (bf16[3,4,8,32,256]{4,3,2,1,0:T(8,128)(2,1)S(1)}, f32[24,128]{1,0:T(8,128)S(1)}, bf16[6,256,256]{2,1,0:T(8,128)(2,1)S(1)}, bf16[6,256,256]{2,1,0:T(8,128)(2,1)S(1)}) custom-call(bf16[6,256,256]{2,1,0:T(8,128)(2,1)S(1)} %get-tuple-element.59.dq_in, bf16[6,256,256]{2,1,0:T(8,128)(2,1)S(1)} %get-tuple-element.60.dk_in, ...), custom_call_target="tpu_custom_call" | custom-call | flops 20000000000 | bytes 1048576 | tf_op jit(solution)/shard_map/third_stage/pallas_call | solution.py:639
  148.1 0.0 copy-start.1
  148.1 1.2 copy-done.1
  149.2 0.0 copy-start.2
  149.2 0.9 copy-done.2
  150.1 0.0 copy-start.3
  150.1 0.9 copy-done.3
  151.0 0.0 copy-start.4
  151.0 0.1 slice.10
  151.1 0.6 fusion.1
  151.7 0.0 copy-done.4
  151.7 10.9 %adam.1 = (f32[4096,128]{1,0:T(8,128)}, f32[4096,128]{1,0:T(8,128)}, f32[4096,128]{1,0:T(8,128)}, f32[1536,256]{1,0:T(8,128)}, f32[1536,256]{1,0:T(8,128)}) custom-call(s32[7]{0:T(128)} %owner_ref.3, bf16[12,256,256]{2,1,0:T(8,128)(2,1)} %bitcast.14, f32[24,128]{1,0:T(8,128)} %copy-done.4, bf16[1536,256]{1,0:T(8,128)(2,1)} %bitcast.15, ...), custom_call_target="tpu_custom_call" | custom-call | flops 10485760 | bytes 14680064 | tf_op jit(solution)/shard_map/adam/pallas_call | solution.py:1252
  (1 shorter events, 0.0 us)
Async XLA Ops:
  0.6 1.6 copy-start
  2.2 0.7 copy-start.5
  2.9 1.1 copy-start.6
  2.9 1.4 copy-start.7
  52.1 1.4 copy-start.8
  53.5 1.4 copy-start.10
  54.9 34.5 %copy-start.9 = (f32[6,256,256]{2,1,0:T(8,128)S(1)}, f32[6,256,256]{2,1,0:T(8,128)}, u32[]{:S(2)}) copy-start(f32[6,256,256]{2,1,0:T(8,128)} %get-tuple-element.51.z_ref) | copy-start | bytes 4718596
  148.1 1.2 copy-start.1
  149.2 0.9 copy-start.2
  150.1 0.9 copy-start.3
  151.0 0.7 copy-start.4

commit v7 on v6

--- a/solution.py
+++ b/solution.py
@@ -362,7 +362,7 @@
     xt_ref, a_ref, q_ref, kt_ref, k_ref, v_ref, o_ref, log_ref, r_ref, hid_ref, slope_ref, z_ref, a2_ref, sq_ref,
     wt_ref, wot_ref, wut_ref, wdt_ref, small_ref, w_ref, co_ref,
     vt_ref, mask_ref, score_ref, prob_ref, xo_ref, slot_ref, pslot_ref, chunk_ref,
-    ss0, ss1, rs0, rs1, ps0, ps1, gs0, gs1, xs0, xs1, cs0, cs1, ns0, ns1, hid_buf, slope_buf, hs, ls,
+    ss0, ss1, rs0, rs1, ps0, ps1, gs0, gs1, xs0, xs1, cs0, cs1, ns0, ns1, hid_buf, slope_buf, r_buf, hs, ls,
 ):
     dp = lax.axis_index("dp")
     seq = lax.axis_index("seq")
@@ -534,6 +534,7 @@
         return (
             pltpu.make_async_copy(hid_buf.at[slot], hid_ref.at[u], hs.at[0, slot]),
             pltpu.make_async_copy(slope_buf.at[slot], slope_ref.at[u], hs.at[1, slot]),
+            pltpu.make_async_copy(r_buf.at[slot], r_ref.at[u], hs.at[2, slot]),
         )
 
     def feed(i, carry):
@@ -553,7 +554,7 @@
         place, base = unit_place(u, core)
         x = xt_ref[base + place].astype(F32)
         r, _, _, m = forward_parts(x, o_ref[u], wot_ref, small_ref)
-        r_ref[u] = r
+        r_buf[slot] = r
         out = r + param(small_ref, 4)
         for c in range(FF // BLK):
             rows = slice(c * BLK, (c + 1) * BLK)
@@ -671,11 +672,12 @@
         *pair_of_sems((2,)),
         pltpu.VMEM((2, FF, BLK), BF16),
         pltpu.VMEM((2, FF, BLK), BF16),
-        pltpu.SemaphoreType.DMA((2, 2)),
+        pltpu.VMEM((2, BLK, BLK), F32),
+        pltpu.SemaphoreType.DMA((3, 2)),
         pltpu.SemaphoreType.DMA((4,)),
     ]
     return stage_call(
-        partial(first_stage_body, n), "first_stage", [pk, pp, x, c], outs, scratch, FIRST_MIB, 8e9, hbm_in=(2, 3), hbm_out=(9, 10),
+        partial(first_stage_body, n), "first_stage", [pk, pp, x, c], outs, scratch, FIRST_MIB, 8e9, hbm_in=(2, 3), hbm_out=(8, 9, 10),
         collective_id=0,
     )
 
@@ -791,7 +793,7 @@
     gz_ref, gr_ref, gd_acc, gu_acc, go_acc, tail_acc, gqkv_acc, head_acc, dq_ref, dk_ref, dv_ref, i_ref,
     g_ref, pp_ref, half_ref, quarter_ref, out_ref, mine_ref, slot_ref, chunk_ref, pslot_ref, psum_ref,
     as0, as1, bs0, bs1, ss0, ss1, rs0, rs1, gs0, gs1, ps0, ps1, xs0, xs1, us0, us1, vs0, vs1,
-    go_ref, hid_buf, slope_buf, hs, mask_ref, prob_ref, ds_ref, dk_acc, dv_acc, part_ref, got_ref, ds0, ds1,
+    go_ref, hid_buf, slope_buf, r_buf, hs, mask_ref, prob_ref, ds_ref, dk_acc, dv_acc, part_ref, got_ref, ds0, ds1,
 ):
     dp = lax.axis_index("dp")
     seq = lax.axis_index("seq")
@@ -928,6 +930,7 @@
         return (
             pltpu.make_async_copy(hid_ref.at[u], hid_buf.at[slot], hs.at[0, slot]),
             pltpu.make_async_copy(slope_ref.at[u], slope_buf.at[slot], hs.at[1, slot]),
+            pltpu.make_async_copy(r_ref.at[u], r_buf.at[slot], hs.at[2, slot]),
         )
 
     split = lambda values: values.astype(BF16).reshape(g_ref.shape[2:])
@@ -955,7 +958,7 @@
         project_weights(a2_ref[base + place], dq_in[u], dk_in[u], dv_in[u], gqkv_acc)
         g = project_back(z_ref[u], dq_in[u], dk_in[u], dv_in[u], gr_in[u], small_ref, w_ref, head_acc)
         gz_ref[u] = g
-        r_unit, r_inv = standardize(r_ref[u])
+        r_unit, r_inv = standardize(r_buf[slot])
         m = (r_unit * param(small_ref, 2) + param(small_ref, 3)).astype(BF16)
         feed_back_tail(
             u, g, g.astype(BF16), r_unit, r_inv, m, o_ref[u], small_ref,
@@ -1117,15 +1120,16 @@
         pltpu.VMEM(tile, BF16),
         pltpu.VMEM((2, FF, BLK), BF16),
         pltpu.VMEM((2, FF, BLK), BF16),
-        pltpu.SemaphoreType.DMA((2, 2)),
+        pltpu.VMEM((2, BLK, BLK), F32),
+        pltpu.SemaphoreType.DMA((3, 2)),
         *BACK_SCRATCH,
     ]
     return stage_call(
-        partial(third_stage_body, n), "third_stage", args, outs, scratch, THIRD_MIB, 20e9, hbm_in=(6, 7), collective_id=2
+        partial(third_stage_body, n), "third_stage", args, outs, scratch, THIRD_MIB, 20e9, hbm_in=(6, 7, 8), collective_id=2
     )
 
 
-FIRST_MIB, SECOND_MIB, THIRD_MIB, ADAM_MIB = 38, 22, 31, 58
+FIRST_MIB, SECOND_MIB, THIRD_MIB, ADAM_MIB = 36, 21, 31, 58
 
 
 def owner_scalars(owner_ref):
@@ -1175,61 +1179,103 @@
 ROWS = D * D // 128
 
 
-def adam_body(owner_ref, g_ref, p_ref, f_ref, i_ref, m_ref, v_ref, w_ref, m_out, v_out, w_out, f_out, i_out, grad_ref):
+def adam_body(
+    owner_ref, g_ref, p_ref, f_ref, i_ref, m_ref, v_ref, w_ref, m_out, v_out, w_out, f_out, i_out,
+    row_buf, state_buf, grad_ref, ins, outs, states,
+):
     dp = lax.axis_index("dp")
-    block = pl.program_id(0)
     starts = owner_scalars(owner_ref)
     counts = [1, 1, 1, 1, 4, 4, 1]
-    rate = jnp.float32(D ** (-0.5))
-    decay = jnp.float32(0.1)
-    limit = jnp.int32(0)
-    f_out[...] = f_ref[...].astype(F32)
-    i_out[...] = i_ref[...].astype(F32)
-    for t in range(7):
-        first = starts[t] // (D * D)
-        here = (owner_ref[t] == dp) & (block >= first) & (block < first + counts[t])
-        part = block - first
-        limit = jnp.where(here, 2 * SMALL if t == 6 else ROWS, limit)
-        if t == 5:
-            rate = jnp.where(here, FF ** (-0.5), rate)
-        if t == 6:
-            rate = jnp.where(here, 0.5, rate)
-            decay = jnp.where(here, 0.0, decay)
-
-        @pl.when(here)
-        def _(t=t, part=part):
+    blocks = m_ref.shape[0] // ROWS
+
+    def rows_of(block):
+        return pl.ds(pl.multiple_of(block * ROWS, ROWS), ROWS)
+
+    def reads(block):
+        return [
+            pltpu.make_async_copy(ref.at[rows_of(block)], row_buf.at[j, block], ins.at[j, block])
+            for j, ref in enumerate((m_ref, v_ref, w_ref))
+        ]
+
+    def writes(block):
+        return [
+            pltpu.make_async_copy(row_buf.at[j, block], ref.at[rows_of(block)], outs.at[j, block])
+            for j, ref in enumerate((m_out, v_out, w_out))
+        ]
+
+    widened = [
+        pltpu.make_async_copy(state_buf.at[j], ref, states.at[j]) for j, ref in enumerate((f_out, i_out))
+    ]
+    for block in range(blocks):
+        for copy in reads(block):
+            copy.start()
+    for j, ref in enumerate((f_ref, i_ref)):
+        for u in range(UNITS):
+            state_buf[j, u] = ref[u].astype(F32)
+        widened[j].start()
+
+    def step(block, carry):
+        rate = jnp.float32(D ** (-0.5))
+        decay = jnp.float32(0.1)
+        limit = jnp.int32(0)
+        for t in range(7):
+            first = starts[t] // (D * D)
+            here = (owner_ref[t] == dp) & (block >= first) & (block < first + counts[t])
+            part = block - first
+            limit = jnp.where(here, 2 * SMALL if t == 6 else ROWS, limit)
+            if t == 5:
+                rate = jnp.where(here, FF ** (-0.5), rate)
             if t == 6:
-                grad_ref[0:24, :] = p_ref[...]
-            elif t == 4:
-                for c in range(4):
-                    piece = g_ref[4 + c, pl.ds(pl.multiple_of(part * 64, 64), 64), :].astype(F32)
-                    for side in range(2):
-                        grad_ref[pl.ds(2 * c + side, 64, stride=8), :] = piece[:, side * 128 : (side + 1) * 128]
-            else:
-                for r in range(4):
-                    piece = g_ref[8 + part if t == 5 else t, r * 64 : (r + 1) * 64, :].astype(F32)
-                    for side in range(2):
-                        grad_ref[pl.ds(r * 128 + side, 64, stride=2), :] = piece[:, side * 128 : (side + 1) * 128]
-
-    @pl.when(limit == 0)
-    def _():
-        for out in (m_out, v_out, w_out):
-            out[...] = jnp.zeros_like(out)
-
-    @pl.when(limit > 0)
-    def _():
-        scale = 1.0 / (1.0 - 0.5**STEP)
-        for r in range(0, ROWS, PIECE):
-            rows = slice(r, r + PIECE)
-            grad = grad_ref[rows, :]
-            valid = lax.broadcasted_iota(jnp.int32, (PIECE, 128), 0) + r < limit
-            first_new = 0.5 * m_ref[rows, :] + 0.5 * grad
-            second_new = 0.5 * v_ref[rows, :] + 0.5 * grad * grad
-            old = w_ref[rows, :]
-            update = first_new * scale / (jnp.sqrt(second_new * scale) + adam_eps) + decay * old
-            m_out[rows, :] = jnp.where(valid, first_new, 0.0)
-            v_out[rows, :] = jnp.where(valid, second_new, 0.0)
-            w_out[rows, :] = jnp.where(valid, old - rate * update, 0.0)
+                rate = jnp.where(here, 0.5, rate)
+                decay = jnp.where(here, 0.0, decay)
+
+            @pl.when(here)
+            def _(t=t, part=part):
+                if t == 6:
+                    grad_ref[0:24, :] = p_ref[...]
+                elif t == 4:
+                    for c in range(4):
+                        piece = g_ref[4 + c, pl.ds(pl.multiple_of(part * 64, 64), 64), :].astype(F32)
+                        for side in range(2):
+                            grad_ref[pl.ds(2 * c + side, 64, stride=8), :] = piece[:, side * 128 : (side + 1) * 128]
+                else:
+                    for r in range(4):
+                        piece = g_ref[8 + part if t == 5 else t, r * 64 : (r + 1) * 64, :].astype(F32)
+                        for side in range(2):
+                            grad_ref[pl.ds(r * 128 + side, 64, stride=2), :] = piece[:, side * 128 : (side + 1) * 128]
+
+        for copy in reads(block):
+            copy.wait()
+
+        @pl.when(limit == 0)
+        def _():
+            row_buf[:, block] = jnp.zeros((3, ROWS, 128), F32)
+
+        @pl.when(limit > 0)
+        def _():
+            scale = 1.0 / (1.0 - 0.5**STEP)
+            for r in range(0, ROWS, PIECE):
+                rows = slice(r, r + PIECE)
+                grad = grad_ref[rows, :]
+                valid = lax.broadcasted_iota(jnp.int32, (PIECE, 128), 0) + r < limit
+                first_new = 0.5 * row_buf[0, block, rows, :] + 0.5 * grad
+                second_new = 0.5 * row_buf[1, block, rows, :] + 0.5 * grad * grad
+                old = row_buf[2, block, rows, :]
+                update = first_new * scale / (jnp.sqrt(second_new * scale) + adam_eps) + decay * old
+                row_buf[0, block, rows, :] = jnp.where(valid, first_new, 0.0)
+                row_buf[1, block, rows, :] = jnp.where(valid, second_new, 0.0)
+                row_buf[2, block, rows, :] = jnp.where(valid, old - rate * update, 0.0)
+
+        for copy in writes(block):
+            copy.start()
+        return carry
+
+    lax.fori_loop(0, blocks, step, 0)
+    for block in range(blocks):
+        for copy in writes(block):
+            copy.wait()
+    for copy in widened:
+        copy.wait()
 
 
 PIECE = 64
@@ -1237,23 +1283,21 @@
 
 def adam(owner_list, g, p, f, i, m, v, w):
     blocks = m.shape[0] // ROWS
-    tile = pl.BlockSpec((ROWS, 128), lambda b, t: (b, 0))
-    states = pl.BlockSpec((f.shape[0] // blocks, D), lambda b, t: (b, 0))
-    out = jax.ShapeDtypeStruct(m.shape, F32)
-    state = jax.ShapeDtypeStruct(f.shape, F32)
-    whole = pl.BlockSpec(memory_space=pltpu.VMEM)
-    spec = pltpu.PrefetchScalarGridSpec(
-        num_scalar_prefetch=1,
-        grid=(blocks,),
-        in_specs=[whole, whole, states, states, tile, tile, tile],
-        out_specs=[tile, tile, tile, states, states],
-        scratch_shapes=[pltpu.VMEM((ROWS, 128), F32)],
-    )
+    outs = [jax.ShapeDtypeStruct(m.shape, F32)] * 3 + [jax.ShapeDtypeStruct(f.shape, F32)] * 2
     return pl.pallas_call(
         adam_body,
-        grid_spec=spec,
-        out_shape=[out, out, out, state, state],
-        compiler_params=params_of(mib=ADAM_MIB),
+        in_specs=[pl.BlockSpec(memory_space=pltpu.SMEM)] + [VM] * 4 + [HB] * 3,
+        out_specs=[HB] * 5,
+        out_shape=outs,
+        scratch_shapes=[
+            pltpu.VMEM((3, blocks, ROWS, 128), F32),
+            pltpu.VMEM((2, *f.shape), F32),
+            pltpu.VMEM((ROWS, 128), F32),
+            pltpu.SemaphoreType.DMA((3, blocks)),
+            pltpu.SemaphoreType.DMA((3, blocks)),
+            pltpu.SemaphoreType.DMA((2,)),
+        ],
+        compiler_params=pltpu.CompilerParams(vmem_limit_bytes=ADAM_MIB << 20),
         cost_estimate=cost(20 * 524288, 14 << 20),
         name="adam",
     )(owner_list, g, p, f, i, m, v, w)
@@ -1272,8 +1316,7 @@
         n, dq, dk, dv, a2, z2, gr, hid, slope, r1, o1, log1, q1, kt1, k1, v1, small, w, gd, gu, gout, tail,
         a1, xt, sq1, sq2, final,
     )
-    states = [r.reshape(-1, D) for r in (final, grad)]
-    m_new, v_new, w_new, final, grad = adam(owner_list, g.reshape(12, D, D), p, *states, flat[1], flat[2], flat[0])
+    m_new, v_new, w_new, final, grad = adam(owner_list, g.reshape(12, D, D), p, final, grad, flat[1], flat[2], flat[0])
     sequences = inputs.shape[0] * n
     entries = inputs.shape[1] * lax.axis_size("seq") * D
     squares = p[18:].reshape(-1)[: 2 * sequences].reshape(2, sequences)

time: 164 us -> 157 us (0.957)
  Pallas kernels: 153 us -> 149 us
  local copies, waits for them, and re-layouts: 8.75 us -> 5.92 us
    unnamed x22 -> x18, local copies, waits for them, and re-layouts: 8.67 us -> 5.84 us
    pallas_call x1, Pallas kernels: 10.9 us -> 8.74 us  [adam(): pl.pallas_call(adam_body, in_specs=[pl.BlockSpec(memory_space=pltpu.SMEM)...]
where the time goes in v7:
time: 157 us
  Pallas kernels  149 us (95%)
  local copies, waits for them, and re-layouts  5.92 us (4%)
    pallas_call x3, Pallas kernels, stage_call(): pl.pallas_call(body, in_specs=[HB if i in hbm_in else VM for i in range(l...  140 us
    pallas_call x1, Pallas kernels, adam(): pl.pallas_call(adam_body, in_specs=[pl.BlockSpec(memory_space=pltpu.SMEM)...  8.74 us
    unnamed x18, local copies, waits for them, and re-layouts  5.84 us

profile of v7, /device:TPU:0, one launch (start us, length us, event | category | flops | bytes accessed | tf_op | source)
XLA Modules:
  0.0 156.5 jit_solution(2490723201408913321)
XLA Ops:
  0.6 0.0 copy-start
  0.6 1.6 %copy-done = f32[1,524288]{1,0:T(1,128)S(1)} copy-done((f32[1,524288]{1,0:T(1,128)S(1)}, f32[1,524288]{1,0:T(1,128)}, u32[]{:S(2)}) %copy-start) | copy-done | bytes 2097176
  2.2 0.0 copy-start.5
  2.2 0.7 copy-done.5
  2.9 0.0 copy-start.6
  2.9 0.0 copy-start.7
  2.9 0.7 pack.1
  3.6 0.4 copy-done.6
  4.0 0.2 copy-done.7
  4.3 46.3 %first_stage.1 = (bf16[8,256,256]{2,1,0:T(8,128)(2,1)S(1)}, bf16[8,256,256]{2,1,0:T(8,128)(2,1)S(1)}, bf16[8,256,256]{2,1,0:T(8,128)(2,1)S(1)}, bf16[4,64,2048]{...) custom-call(bf16[3,8,32,256]{3,2,1,0:T(8,128)(2,1)S(1)} %bitcast.11,, ...), custom_call_target="tpu_custom_call" | custom-call | flops 8000000000 | bytes 1048576 | tf_op jit(solution)/shard_map/first_stage/pallas_call | solution.py:640
  50.6 0.0 copy-start.8
  50.6 34.6 %second_stage.1 = (bf16[6,256,256]{2,1,0:T(8,128)(2,1)S(1)}, f32[6,8,256]{2,1,0:T(8,128)S(1)}, f32[6,256,256]{2,1,0:T(8,128)S(1)}, f32[1024,256]{1,0:T(8,128)S(1...) custom-call(bf16[8,256,256]{2,1,0:T(8,128)(2,1)S(1)} %get-tuple-elem, ...), custom_call_target="tpu_custom_call" | custom-call | flops 20000000000 | bytes 1048576 | tf_op jit(solution)/shard_map/second_stage/pallas_call | solution.py:640
  85.2 0.0 copy-done.8
  85.2 58.8 %third_stage.1 = (bf16[3,4,8,32,256]{4,3,2,1,0:T(8,128)(2,1)S(1)}, f32[24,128]{1,0:T(8,128)S(1)}, bf16[6,256,256]{2,1,0:T(8,128)(2,1)S(1)}, bf16[6,256,256]{2,1,0:T(8,128)(2,1)S(1)}) custom-call(bf16[6,256,256]{2,1,0:T(8,128)(2,1)S(1)} %get-tuple-element.59.dq_in, bf16[6,256,256]{2,1,0:T(8,128)(2,1)S(1)} %get-tuple-element.60.dk_in, ...), custom_call_target="tpu_custom_call" | custom-call | flops 20000000000 | bytes 1048576 | tf_op jit(solution)/shard_map/third_stage/pallas_call | solution.py:640
  144.0 0.0 copy-start.1
  144.0 1.2 copy-done.1
  145.2 0.0 copy-start.2
  145.2 0.9 copy-done.2
  146.1 0.0 copy-start.3
  146.1 0.9 copy-done.3
  146.9 0.0 copy-start.4
  146.9 0.1 slice.10
  147.0 0.6 fusion.1
  147.6 0.0 copy-done.4
  147.6 8.7 %adam.1 = (f32[4096,128]{1,0:T(8,128)}, f32[4096,128]{1,0:T(8,128)}, f32[4096,128]{1,0:T(8,128)}, f32[6,256,256]{2,1,0:T(8,128)}, f32[6,256,256]{2,1,0:T(8,128)}) custom-call(s32[7]{0:T(128)} %owner_ref.3, bf16[12,256,256]{2,1,0:T(8,128)(2,1)} %bitcast.10, f32[24,128]{1,0:T(8,128)} %copy-done.4, bf16[6,256,256]{2,1,0:T(8,128)(2,1)} %copy-done.2, ...), custom_call_target="tpu_custom_call" | custom-call | flops 10485760 | bytes 14680064 | tf_op jit(solution)/shard_map/adam/pallas_call | solution.py:1287
  (1 shorter events, 0.0 us)
Async XLA Ops:
  0.6 1.6 %copy-start = (f32[1,524288]{1,0:T(1,128)S(1)}, f32[1,524288]{1,0:T(1,128)}, u32[]{:S(2)}) copy-start(f32[1,524288]{1,0:T(1,128)} %param.9) | copy-start | bytes 6291460
  2.2 0.7 copy-start.5
  2.9 1.1 copy-start.6
  2.9 1.4 copy-start.7
  50.6 34.6 %copy-start.8 = (bf16[3,4,8,32,256]{4,3,2,1,0:T(8,128)(2,1)}, bf16[3,4,8,32,256]{4,3,2,1,0:T(8,128)(2,1)S(1)}, u32[]{:S(2)}) copy-start(bf16[3,4,8,32,256]{4,3,2,1,0:T(8,128)(2,1)S(1)} %get-tuple-element.53.w_ref) | copy-start | bytes 4718596
  144.0 1.2 copy-start.1
  145.2 0.9 copy-start.2
  146.1 0.9 copy-start.3
  146.9 0.7 copy-start.4
